TPU v7x, 32 devices: a whole 2x2x4 slice. The times are simulated.
32 devices in a mesh: mem: 4 (over x, core), ty: 2 (over y), tx: 4 (over z).
Axes of the slice: x: 2, y: 2, z: 4, core: 2. Of those that a mesh axis runs over, the one named last changes fastest.
Arguments:
- pressure: float32 [8, 50, 64, 512], P('mem', None, 'ty', 'tx'), may hold values from -6 to 6
- east_wind: float32 [8, 50, 64, 512], P('mem', None, 'ty', 'tx'), may hold values from -6 to 6
- north_wind: float32 [8, 50, 64, 512], P('mem', None, 'ty', 'tx'), may hold values from -6 to 6
- vertical_wind: float32 [8, 49, 64, 512], P('mem', None, 'ty', 'tx'), may hold values from -6 to 6
- sound_squared: float32 [50, 64, 512], P(None, 'ty', 'tx'), may hold values from 0.5 to 2
- thickness: float32 [50], replicated, may hold values from 0.05 to 0.5
- owner_map: int32 [8], replicated, may hold values from 0 to 7, each once
Outputs:
- analysis: float32 [2, 4, 6, 32, 128], P('ty', 'tx', None, 'mem')
Inputs may be any that keep to these rules, and one draw needn't show every extreme that they name: `owner_map`: every tile index appears exactly once.
All inputs are finite; a program needn't handle non-finite values.
Results may differ from a plain program's by a relative error of at most 0.0001.
Values sent between devices are 32-bit elements; how exact they have to be, the bound alone decides.
No kernel may reach another device: no remote copies, remote signals or barrier semaphores. Data moves between devices by JAX's collectives and lax.ppermute only.
A program may use at most 128 MiB of HBM per device.

v0:
```python
import jax
import jax.numpy as jnp
from jax import lax
from jax.sharding import PartitionSpec as P

SUBSTEPS = 2


horiz_ratio = 0.35
vert_ratio = 1.5


def shifted(block, axis, distance):
    devices = range(lax.axis_size(axis))
    route = [((i - distance) % len(devices), i) for i in devices]
    return lax.ppermute(block, axis, route)


def column_solve(coeff, rhs_list):
    count = len(rhs_list)
    factors = []
    values = []
    pivot = 1.0 + coeff[1] + coeff[0]
    values.append(rhs_list[0] / pivot)
    factors.append(-coeff[1] / pivot)
    for position in range(1, count):
        pivot = (
            1.0 + coeff[position + 1] + coeff[position] + coeff[position] * factors[position - 1]
        )
        values.append((rhs_list[position] + coeff[position] * values[position - 1]) / pivot)
        factors.append(-coeff[position + 1] / pivot)
    solved = [values[count - 1]]
    for position in range(count - 2, -1, -1):
        solved.insert(0, values[position] - factors[position] * solved[0])
    return solved


def substep_run(pressure, east_wind, north_wind, vertical_wind, sound_squared, coeff):
    levels = pressure.shape[1]
    western = shifted(pressure[..., -1:], "tx", 1)
    pressure_west = jnp.concatenate([western, pressure[..., :-1]], axis=3)
    southern = shifted(pressure[..., -1:, :], "ty", 1)
    pressure_south = jnp.concatenate([southern, pressure[..., :-1, :]], axis=2)
    east_wind = east_wind - horiz_ratio * (pressure - pressure_west)
    north_wind = north_wind - horiz_ratio * (pressure - pressure_south)
    eastern = shifted(east_wind[..., :1], "tx", -1)
    east_next = jnp.concatenate([east_wind[..., 1:], eastern], axis=3)
    northern = shifted(north_wind[..., :1, :], "ty", -1)
    north_next = jnp.concatenate([north_wind[..., 1:, :], northern], axis=2)
    divergence = east_next - east_wind + (north_next - north_wind)
    partial_value = pressure - horiz_ratio * sound_squared * divergence
    rhs_list = [
        vertical_wind[:, level]
        - vert_ratio * (partial_value[:, level + 1] - partial_value[:, level])
        for level in range(levels - 1)
    ]
    vertical_wind = jnp.stack(column_solve(coeff, rhs_list), axis=1)
    zero_layer = jnp.zeros_like(partial_value[:, :1])
    padded = jnp.concatenate([zero_layer, vertical_wind, zero_layer], axis=1)
    pressure = partial_value - vert_ratio * sound_squared * (padded[:, 1:] - padded[:, :-1])
    return (pressure, east_wind, north_wind, vertical_wind)


def finish_stats(first_sum, second_sum, members):
    mean = first_sum / members
    variance = second_sum / (members - 1)
    return jnp.concatenate([mean, variance], axis=0)


def local(pressure, east_wind, north_wind, vertical_wind, sound_squared, thickness, owner_map):
    levels = pressure.shape[1]
    rows_tile = pressure.shape[2]
    cols_tile = pressure.shape[3]
    members = pressure.shape[0] * lax.axis_size("mem")
    quarter = rows_tile // lax.axis_size("mem")
    coeff_field = vert_ratio * vert_ratio * sound_squared
    coeff = [coeff_field[level] for level in range(levels)]
    for substep in range(SUBSTEPS):
        pressure, east_wind, north_wind, vertical_wind = substep_run(
            pressure, east_wind, north_wind, vertical_wind, sound_squared, coeff
        )
    mass = jnp.einsum("k,mkyx->myx", thickness, pressure, precision=lax.Precision.HIGHEST)
    east_total = jnp.einsum("k,mkyx->myx", thickness, east_wind, precision=lax.Precision.HIGHEST)
    north_total = jnp.einsum("k,mkyx->myx", thickness, north_wind, precision=lax.Precision.HIGHEST)
    integrals = jnp.stack([mass, east_total, north_total], axis=1)
    first_local = jnp.sum(integrals, axis=0)
    ensemble_total = lax.psum(first_local, "mem")
    ensemble_mean = ensemble_total / members
    second_local = jnp.sum((integrals - ensemble_mean) ** 2, axis=0)
    my_tile = lax.axis_index(("ty", "tx"))
    row_start = lax.axis_index("mem") * quarter
    first_sum, second_sum = lax.psum((first_local, second_local), "mem")
    stats = finish_stats(first_sum, second_sum, members)
    weights = (owner_map == my_tile).astype(jnp.float32)
    rows_mine = lax.dynamic_slice_in_dim(
        lax.all_gather(stats[None], ("ty", "tx"), axis=0, tiled=True), row_start, quarter, 2
    )
    result = jnp.einsum("t,tsyx->syx", weights, rows_mine, precision=lax.Precision.HIGHEST)
    return result.reshape(1, 1, 6, quarter, cols_tile)


def solution(mesh):
    placed = (
        P("mem", None, "ty", "tx"),
        P("mem", None, "ty", "tx"),
        P("mem", None, "ty", "tx"),
        P("mem", None, "ty", "tx"),
        P(None, "ty", "tx"),
        P(),
        P(),
    )
    return jax.shard_map(
        local,
        mesh=mesh,
        in_specs=placed,
        out_specs=P("ty", "tx", None, "mem", None),
        check_vma=False,
    )
```

profile of v0, /device:TPU:0, one launch (start us, length us, event | category | flops | bytes accessed | tf_op | source)
XLA Modules:
  0.0 218.5 jit_solution(2176977665702427386)
XLA Ops:
  0.0 1.9 slice.749
  1.9 1.7 copy.808
  3.7 3.1 %collective-permute-start = (f32[2,50,32,1]{1,2,3,0:T(8,128)}, f32[2,50,32,1]{1,2,3,0:T(8,128)S(1)}, u32[]{:S(2)}, u32[]{:S(2)}) collective-permute-start(f32[2,50,32,1]{1,2,3,0:T(8,128)} %copy.808), channel_id=1, source_target_pairs={{3,0},{0,1},{1,2},{2,3},{7,4},{4,5},{5,6},{6,7},{11,8},{8,9},{9,10... | collective-permute-start | bytes 38408 | tf_op jit(solution)/shard_map/ppermute | solution.py:16
  6.9 1.6 collective-permute-start.2
  8.4 2.5 %broadcast_multiply_fusion.1 = (f32[50,32,128]{2,1,0:T(8,128)}, f32[50,32,128]{2,1,0:T(8,128)}, f32[50,32,128]{2,1,0:T(8,128)S(1)}) fusion(f32[50,32,128]{2,1,0:T(8,128)} %param.11), kind=kLoop, calls=%fused_computation.231 | loop fusion | flops 614400 | bytes 3276800 | tf_op jit(solution)/shard_map/mul | solution.py:60
  11.6 1.0 multiply_add_fusion.3
  41.0 2.5 %copy.733 = f32[2,50,32,1]{3,2,0,1:T(8,128)} copy(f32[2,50,32,1]{1,2,3,0:T(8,128)S(1)} %collective-permute-done) | data formatting | bytes 25600 | tf_op jit(solution)/shard_map/ppermute | solution.py:16
  43.7 4.8 %fusion.7 = (f32[2,50,32,128]{3,2,0,1:T(8,128)S(1)}, f32[2,50,32,128]{3,2,0,1:T(8,128)}) fusion(f32[2,50,32,1]{3,2,0,1:T(8,128)} %copy.733, f32[2,50,32,128]{3,2,1,0:T(8,128)} %param.8, f32[2,50,32,128]{3,2,1,0:T(8,128)S(1)} %copy-done.1, f32[2,50,1,128]{3,2,0,1:T(1,128)} %collective-permute-done.2, f32[2,50,32,128]{3,2,1,0:T(8,128)} %param.9), kind=kLoop, calls=%fused_computation.8 | loop fusion | flops 3276800 | bytes 11532800 | tf_op jit(solution)/shard_map/sub | solution.py:44
  48.4 1.8 copy.736
  50.2 2.2 %collective-permute-start.1 = (f32[2,50,32,1]{1,2,3,0:T(8,128)}, f32[2,50,32,1]{1,2,3,0:T(8,128)}, u32[]{:S(2)}, u32[]{:S(2)}) collective-permute-start(f32[2,50,32,1]{1,2,3,0:T(8,128)} %copy.736), channel_id=1, source_target_pairs={{1,0},{2,1},{3,2},{0,3},{5,4},{6,5},{7,6},{4,7},{9,8},{10,9},{11,1... | collective-permute-start | bytes 38408 | tf_op jit(solution)/shard_map/ppermute | solution.py:16
  52.4 1.6 slice.970
  55.0 1.6 slice.965
  56.6 1.6 slice.969
  58.2 3.3 %copy.737 = f32[2,50,32,1]{3,2,0,1:T(8,128)} copy(f32[2,50,32,1]{1,2,3,0:T(8,128)} %collective-permute-done.1) | data formatting | bytes 25600 | tf_op jit(solution)/shard_map/ppermute | solution.py:16
  61.8 4.7 %fusion.10 = f32[2,50,32,128]{3,2,0,1:T(8,128)S(1)} fusion(f32[2,50,32,128]{3,2,0,1:T(8,128)S(1)} %get-tuple-element.319, f32[2,50,32,1]{3,2,0,1:T(8,128)} %copy.737, f32[2,50,32,127]{3,2,0,1:T(8,128)} %slice.965, f32[2,50,32,128]{3,2,0,1:T(8,128)} %get-tuple-element.320, f32[2,50,1,128]{3,2,0,1:T(1,128)} %collective-permute-done.3, ...), kind=kLoop, calls=%fused_computation.12 | loop fusion | flops 2867200 | bytes 10649600 | tf_op jit(solution)/shard_map/sub | solution.py:51
  66.8 2.5 %add_divide_fusion.50 = (f32[2,1,32,128]{3,2,0,1:T(8,128)S(1)}, f32[2,1,32,128]{3,2,0,1:T(8,128)S(1)}, f32[2,1,32,128]{3,2,0,1:T(8,128)S(1)}, f32[2,1,32,128]{3,...) fusion(f32[32,128]{1,0:T(8,128)} %bitcast.1801, ...), kind=kLoop, calls=%fused_computation.760 | loop fusion | flops 1851392 | bytes 5619712 | tf_op jit(solution)/shard_map/div | solution.py:30
  69.7 3.2 %constant_dynamic-update-slice_fusion.98 = (f32[2,50,32,128]{3,2,0,1:T(8,128)S(1)}, f32[2,1,32,128]{3,2,0,1:T(8,128)}, f32[2,1,32,128]{3,2,0,1:T(8,128)}, f32[2,...) fusion(f32[2,50,32,128]{3,2,0,1:T(8,128)S(1)} %copy-done.8, ...), kind=kLoop, calls=%fused_computation.128 | loop fusion | flops 1777664 | bytes 5554176
  72.9 0.8 constant_dynamic-update-slice_fusion.49
  73.7 0.8 constant_dynamic-update-slice_fusion.97
  74.5 0.8 constant_dynamic-update-slice_fusion.96
  75.3 0.8 constant_dynamic-update-slice_fusion.95
  79.1 0.8 constant_dynamic-update-slice_fusion.90
  81.7 0.8 constant_dynamic-update-slice_fusion.87
  106.1 1.7 fusion.149
  107.9 1.0 constant_dynamic-update-slice_fusion.56
  111.4 1.8 copy.792
  113.1 1.7 collective-permute-start.6
  115.5 3.6 %collective-permute-done.4 = f32[2,50,32,1]{1,2,3,0:T(8,128)S(1)} collective-permute-done((f32[2,50,32,1]{1,2,3,0:T(8,128)}, f32[2,50,32,1]{1,2,3,0:T(8,128)S(1)}, u32[]{:S(2)}, u32[]{:S(2)}) %collective-permute-start.4) | collective-permute-done | bytes 12832 | tf_op jit(solution)/shard_map/ppermute | solution.py:16
  119.0 2.6 %copy.793 = f32[2,50,32,1]{3,2,0,1:T(8,128)} copy(f32[2,50,32,1]{1,2,3,0:T(8,128)S(1)} %collective-permute-done.4) | data formatting | bytes 25600 | tf_op jit(solution)/shard_map/ppermute | solution.py:16
  122.2 4.8 %fusion.14 = (f32[2,50,32,128]{3,2,0,1:T(8,128)S(1)}, f32[2,50,32,128]{3,2,0,1:T(8,128)}) fusion(f32[2,50,32,128]{3,2,0,1:T(8,128)} %copy-done.2, f32[2,50,32,128]{3,2,0,1:T(8,128)S(1)} %multiply_subtract_fusion.1, f32[2,50,32,127]{3,2,0,1:T(8,128)S(1)} %bitcast.1630, f32[2,50,32,1]{3,2,0,1:T(8,128)} %copy.793, f32[2,50,32,128]{3,2,0,1:T(8,128)} %get-tuple-element.320, ...), kind=kLoop, calls=%fused_computation.19 | loop fusion | flops 3276800 | bytes 11468800 | tf_op jit(solution)/shard_map/sub | solution.py:44
  127.0 1.8 copy.794
  129.0 1.8 slice.1078
  130.8 1.5 collective-permute-start.7
  132.3 2.7 %fusion.2 = f32[1,2,32,128]{3,0,2,1:T(1,128)} fusion(f32[2,50,32,128]{3,2,0,1:T(8,128)S(1)} %get-tuple-element.317, f32[50]{0:T(128)S(1)} %copy-done), kind=kOutput, calls=%fused_computation.2 | convolution fusion | flops 4915200 | bytes 1671368 | tf_op jit(solution)/shard_map/k,mkyx->myx/dot_general | solution.py:83
  135.0 2.7 %fusion = f32[1,2,32,128]{3,0,2,1:T(1,128)} fusion(f32[2,50,32,128]{3,2,0,1:T(8,128)S(1)} %copy-done.3, f32[50]{0:T(128)S(1)} %copy-done), kind=kOutput, calls=%fused_computation | convolution fusion | flops 4915200 | bytes 1671368 | tf_op jit(solution)/shard_map/k,mkyx->myx/dot_general | solution.py:84
  137.7 1.7 slice.1073
  139.4 1.5 slice.1077
  140.9 3.3 %copy.795 = f32[2,50,32,1]{3,2,0,1:T(8,128)} copy(f32[2,50,32,1]{1,2,3,0:T(8,128)} %collective-permute-done.5) | data formatting | bytes 25600 | tf_op jit(solution)/shard_map/ppermute | solution.py:16
  144.6 4.6 %fusion.17 = f32[2,50,32,128]{3,2,0,1:T(8,128)S(1)} fusion(f32[2,50,32,128]{3,2,0,1:T(8,128)S(1)} %multiply_subtract_fusion.1, f32[2,50,32,128]{3,2,0,1:T(8,128)S(1)} %get-tuple-element.317, f32[2,50,32,1]{3,2,0,1:T(8,128)} %copy.795, f32[2,50,32,127]{3,2,0,1:T(8,128)} %slice.1073, f32[2,50,32,128]{3,2,0,1:T(8,128)} %get-tuple-element.318, ...), kind=kLoop, calls=%fused_computation.23 | loop fusion | flops 2867200 | bytes 10649600 | tf_op jit(solution)/shard_map/sub | solution.py:51
  149.6 3.4 %fusion.32 = (f32[2,32,128]{2,1,0:T(8,128)S(1)}, f32[2,32,128]{2,1,0:T(8,128)S(1)}, f32[2,32,128]{2,1,0:T(8,128)S(1)}, f32[2,32,128]{2,1,0:T(8,128)S(1)}, f32[2,...) fusion(f32[2,32,128]{2,1,0:T(8,128)} %copy-done.207, f32[32,128]{1,0:T(8,128)} %get-tuple-element.258, ...), kind=kLoop, calls=%fused_computation.301 | loop fusion | flops 4046848 | bytes 5652480 | tf_op jit(solution)/shard_map/div | solution.py:30
  153.0 2.4 %add_divide_fusion = (f32[2,1,32,128]{3,2,0,1:T(8,128)S(1)}, f32[2,1,32,128]{3,2,0,1:T(8,128)S(1)}, f32[2,1,32,128]{3,2,0,1:T(8,128)S(1)}, f32[2,1,32,128]{3,2,0...) fusion(f32[2,1,32,128]{3,2,0,1:T(8,128)} %get-tuple-element.149, ...), kind=kLoop, calls=%fused_computation.616 | loop fusion | flops 1949696 | bytes 5259264 | tf_op jit(solution)/shard_map/div | solution.py:30
  155.4 2.2 %constant_dynamic-update-slice_fusion.198 = (f32[2,50,32,128]{3,2,0,1:T(8,128)S(1)}, f32[2,1,32,128]{3,2,0,1:T(8,128)S(1)}, f32[2,1,32,128]{3,2,0,1:T(8,128)S(1)...) fusion(f32[2,50,32,128]{3,2,0,1:T(8,128)S(1)} %copy-done.7, ...), kind=kLoop, calls=%fused_computation.228 | loop fusion | flops 1548288 | bytes 4456448
  159.3 0.8 multiply_subtract_fusion
  160.1 2.3 %fusion.4 = f32[1,2,32,128]{3,0,2,1:T(1,128)S(1)} fusion(f32[2,50,32,128]{3,2,0,1:T(8,128)S(1)} %multiply_subtract_fusion, f32[50]{0:T(128)S(1)} %copy-done), kind=kOutput, calls=%fused_computation.4 | convolution fusion | flops 4915200 | bytes 1671368 | tf_op jit(solution)/shard_map/k,mkyx->myx/dot_general | solution.py:82
  162.5 10.5 %psum.14 = f32[3,32,128]{2,1,0:T(8,128)S(1)} all-reduce(f32[3,32,128]{2,1,0:T(8,128)S(1)} %fusion.22), channel_id=1, replica_groups=mesh['mem'=4,'ty'=2,'tx'=4] {'mem'}, use_global_device_ids=true, to_apply=%region_1.0 | all-reduce | flops 12288 | bytes 98304 | tf_op jit(solution)/shard_map/psum | solution.py:92
  173.0 11.2 %psum.18 = f32[3,32,128]{2,1,0:T(8,128)S(1)} all-reduce(f32[3,32,128]{2,1,0:T(8,128)S(1)} %multiply_reduce_fusion), channel_id=1, replica_groups=mesh['mem'=4,'ty'=2,'tx'=4] {'mem'}, use_global_device_ids=true, to_apply=%region_3.0 | all-reduce | flops 12288 | bytes 98304 | tf_op jit(solution)/shard_map/psum | solution.py:92
  184.3 33.3 %all-gather = f32[48,32,128]{2,1,0:T(8,128)S(1)} all-gather(f32[6,32,128]{2,1,0:T(8,128)S(1)} %pad_maximum_fusion.1), channel_id=2, replica_groups=mesh['mem'=4,'ty'=2,'tx'=4] {'ty','tx'}, dimensions={0}, use_global_device_ids=true | all-gather | bytes 884736 | tf_op jit(solution)/shard_map/all_gather | solution.py:96
  217.6 0.9 fusion.20
  (594 shorter events, 63.2 us)
Async XLA Ops:
  0.0 132.3 %copy-start = (f32[50]{0:T(128)S(1)}, f32[50]{0:T(128)}, u32[]{:S(2)}) copy-start(f32[50]{0:T(128)} %param.12) | copy-start | bytes 604
  3.7 37.3 %collective-permute-start = (f32[2,50,32,1]{1,2,3,0:T(8,128)}, f32[2,50,32,1]{1,2,3,0:T(8,128)S(1)}, u32[]{:S(2)}, u32[]{:S(2)}) collective-permute-start(f32[2,50,32,1]{1,2,3,0:T(8,128)} %copy.808), channel_id=1, source_target_pairs={{3,0},{0,1},{1,2},{2,3},{7,4},{4,5},{5,6},{6,7},{11,8},{8,9},{9,10... | collective-permute-start | bytes 38408 | tf_op jit(solution)/shard_map/ppermute | solution.py:16
  6.9 36.8 %collective-permute-start.2 = (f32[2,50,1,128]{3,2,0,1:T(1,128)S(1)}, f32[2,50,1,128]{3,2,0,1:T(1,128)}, u32[]{:S(2)}, u32[]{:S(2)}) collective-permute-start(f32[2,50,1,128]{3,2,0,1:T(1,128)S(1)} %copy.872), channel_id=1, source_target_pairs={{4,0},{0,4},{5,1},{1,5},{6,2},{2,6},{7,3},{3,7},{12,8},{8,12},{13,... | collective-permute-start | bytes 153608 | tf_op jit(solution)/shard_map/ppermute | solution.py:16
  50.2 8.0 %collective-permute-start.1 = (f32[2,50,32,1]{1,2,3,0:T(8,128)}, f32[2,50,32,1]{1,2,3,0:T(8,128)}, u32[]{:S(2)}, u32[]{:S(2)}) collective-permute-start(f32[2,50,32,1]{1,2,3,0:T(8,128)} %copy.736), channel_id=1, source_target_pairs={{1,0},{2,1},{3,2},{0,3},{5,4},{6,5},{7,6},{4,7},{9,8},{10,9},{11,1... | collective-permute-start | bytes 38408 | tf_op jit(solution)/shard_map/ppermute | solution.py:16
  54.1 7.4 %collective-permute-start.3 = (f32[2,50,1,128]{3,2,0,1:T(1,128)}, f32[2,50,1,128]{3,2,0,1:T(1,128)}, u32[]{:S(2)}, u32[]{:S(2)}) collective-permute-start(f32[2,50,1,128]{3,2,0,1:T(1,128)} %slice.970), channel_id=1, source_target_pairs={{4,0},{0,4},{5,1},{1,5},{6,2},{2,6},{7,3},{3,7},{12,8},{8,12},{13,... | collective-permute-start | bytes 153608 | tf_op jit(solution)/shard_map/ppermute | solution.py:16
  69.3 36.1 %copy-start.138 = (f32[2,1,32,128]{3,2,0,1:T(8,128)}, f32[2,1,32,128]{3,2,0,1:T(8,128)S(1)}, u32[]{:S(2)}) copy-start(f32[2,1,32,128]{3,2,0,1:T(8,128)S(1)} %get-tuple-element.261) | copy-start | bytes 98308
  69.3 36.1 %copy-start.139 = (f32[2,1,32,128]{3,2,0,1:T(8,128)}, f32[2,1,32,128]{3,2,0,1:T(8,128)S(1)}, u32[]{:S(2)}) copy-start(f32[2,1,32,128]{3,2,0,1:T(8,128)S(1)} %get-tuple-element.264) | copy-start | bytes 98308
  69.3 36.1 %copy-start.140 = (f32[2,1,32,128]{3,2,0,1:T(8,128)}, f32[2,1,32,128]{3,2,0,1:T(8,128)S(1)}, u32[]{:S(2)}) copy-start(f32[2,1,32,128]{3,2,0,1:T(8,128)S(1)} %get-tuple-element.267) | copy-start | bytes 98308
  69.3 36.1 %copy-start.141 = (f32[2,1,32,128]{3,2,0,1:T(8,128)}, f32[2,1,32,128]{3,2,0,1:T(8,128)S(1)}, u32[]{:S(2)}) copy-start(f32[2,1,32,128]{3,2,0,1:T(8,128)S(1)} %get-tuple-element.270) | copy-start | bytes 98308
  69.3 36.1 %copy-start.142 = (f32[2,1,32,128]{3,2,0,1:T(8,128)}, f32[2,1,32,128]{3,2,0,1:T(8,128)S(1)}, u32[]{:S(2)}) copy-start(f32[2,1,32,128]{3,2,0,1:T(8,128)S(1)} %get-tuple-element.273) | copy-start | bytes 98308
  69.4 36.1 %copy-start.143 = (f32[2,1,32,128]{3,2,0,1:T(8,128)}, f32[2,1,32,128]{3,2,0,1:T(8,128)S(1)}, u32[]{:S(2)}) copy-start(f32[2,1,32,128]{3,2,0,1:T(8,128)S(1)} %get-tuple-element.276) | copy-start | bytes 98308
  69.4 36.1 %copy-start.144 = (f32[2,1,32,128]{3,2,0,1:T(8,128)}, f32[2,1,32,128]{3,2,0,1:T(8,128)S(1)}, u32[]{:S(2)}) copy-start(f32[2,1,32,128]{3,2,0,1:T(8,128)S(1)} %get-tuple-element.279) | copy-start | bytes 98308
  69.4 36.1 %copy-start.145 = (f32[2,1,32,128]{3,2,0,1:T(8,128)}, f32[2,1,32,128]{3,2,0,1:T(8,128)S(1)}, u32[]{:S(2)}) copy-start(f32[2,1,32,128]{3,2,0,1:T(8,128)S(1)} %get-tuple-element.282) | copy-start | bytes 98308
  69.4 36.1 %copy-start.146 = (f32[2,1,32,128]{3,2,0,1:T(8,128)}, f32[2,1,32,128]{3,2,0,1:T(8,128)S(1)}, u32[]{:S(2)}) copy-start(f32[2,1,32,128]{3,2,0,1:T(8,128)S(1)} %get-tuple-element.285) | copy-start | bytes 98308
  69.4 36.1 %copy-start.147 = (f32[2,1,32,128]{3,2,0,1:T(8,128)}, f32[2,1,32,128]{3,2,0,1:T(8,128)S(1)}, u32[]{:S(2)}) copy-start(f32[2,1,32,128]{3,2,0,1:T(8,128)S(1)} %get-tuple-element.288) | copy-start | bytes 98308
  69.4 36.1 %copy-start.148 = (f32[2,1,32,128]{3,2,0,1:T(8,128)}, f32[2,1,32,128]{3,2,0,1:T(8,128)S(1)}, u32[]{:S(2)}) copy-start(f32[2,1,32,128]{3,2,0,1:T(8,128)S(1)} %get-tuple-element.291) | copy-start | bytes 98308
  69.4 36.1 %copy-start.149 = (f32[2,1,32,128]{3,2,0,1:T(8,128)}, f32[2,1,32,128]{3,2,0,1:T(8,128)S(1)}, u32[]{:S(2)}) copy-start(f32[2,1,32,128]{3,2,0,1:T(8,128)S(1)} %get-tuple-element.294) | copy-start | bytes 98308
  69.4 36.1 %copy-start.150 = (f32[2,1,32,128]{3,2,0,1:T(8,128)}, f32[2,1,32,128]{3,2,0,1:T(8,128)S(1)}, u32[]{:S(2)}) copy-start(f32[2,1,32,128]{3,2,0,1:T(8,128)S(1)} %get-tuple-element.297) | copy-start | bytes 98308
  69.4 36.1 %copy-start.151 = (f32[2,1,32,128]{3,2,0,1:T(8,128)}, f32[2,1,32,128]{3,2,0,1:T(8,128)S(1)}, u32[]{:S(2)}) copy-start(f32[2,1,32,128]{3,2,0,1:T(8,128)S(1)} %get-tuple-element.300) | copy-start | bytes 98308
  69.4 36.1 %copy-start.152 = (f32[2,1,32,128]{3,2,0,1:T(8,128)}, f32[2,1,32,128]{3,2,0,1:T(8,128)S(1)}, u32[]{:S(2)}) copy-start(f32[2,1,32,128]{3,2,0,1:T(8,128)S(1)} %get-tuple-element.303) | copy-start | bytes 98308
  69.5 36.1 %copy-start.153 = (f32[2,1,32,128]{3,2,0,1:T(8,128)}, f32[2,1,32,128]{3,2,0,1:T(8,128)S(1)}, u32[]{:S(2)}) copy-start(f32[2,1,32,128]{3,2,0,1:T(8,128)S(1)} %get-tuple-element.306) | copy-start | bytes 98308
  69.5 36.1 %copy-start.154 = (f32[2,1,32,128]{3,2,0,1:T(8,128)}, f32[2,1,32,128]{3,2,0,1:T(8,128)S(1)}, u32[]{:S(2)}) copy-start(f32[2,1,32,128]{3,2,0,1:T(8,128)S(1)} %get-tuple-element.309) | copy-start | bytes 98308
  69.5 36.1 %copy-start.155 = (f32[2,1,32,128]{3,2,0,1:T(8,128)}, f32[2,1,32,128]{3,2,0,1:T(8,128)S(1)}, u32[]{:S(2)}) copy-start(f32[2,1,32,128]{3,2,0,1:T(8,128)S(1)} %get-tuple-element.312) | copy-start | bytes 98308
  69.5 36.1 %copy-start.156 = (f32[2,1,32,128]{3,2,0,1:T(8,128)}, f32[2,1,32,128]{3,2,0,1:T(8,128)S(1)}, u32[]{:S(2)}) copy-start(f32[2,1,32,128]{3,2,0,1:T(8,128)S(1)} %get-tuple-element.315) | copy-start | bytes 98308
  69.5 36.1 %copy-start.190 = (f32[2,1,32,128]{3,2,0,1:T(8,128)}, f32[2,1,32,128]{3,2,0,1:T(8,128)S(1)}, u32[]{:S(2)}) copy-start(f32[2,1,32,128]{3,2,0,1:T(8,128)S(1)} %get-tuple-element.262) | copy-start | bytes 98308
  69.5 36.1 %copy-start.191 = (f32[2,1,32,128]{3,2,0,1:T(8,128)}, f32[2,1,32,128]{3,2,0,1:T(8,128)S(1)}, u32[]{:S(2)}) copy-start(f32[2,1,32,128]{3,2,0,1:T(8,128)S(1)} %get-tuple-element.265) | copy-start | bytes 98308
  69.5 36.1 %copy-start.192 = (f32[2,1,32,128]{3,2,0,1:T(8,128)}, f32[2,1,32,128]{3,2,0,1:T(8,128)S(1)}, u32[]{:S(2)}) copy-start(f32[2,1,32,128]{3,2,0,1:T(8,128)S(1)} %get-tuple-element.268) | copy-start | bytes 98308
  69.5 36.1 %copy-start.193 = (f32[2,1,32,128]{3,2,0,1:T(8,128)}, f32[2,1,32,128]{3,2,0,1:T(8,128)S(1)}, u32[]{:S(2)}) copy-start(f32[2,1,32,128]{3,2,0,1:T(8,128)S(1)} %get-tuple-element.271) | copy-start | bytes 98308
  69.5 36.1 %copy-start.194 = (f32[2,1,32,128]{3,2,0,1:T(8,128)}, f32[2,1,32,128]{3,2,0,1:T(8,128)S(1)}, u32[]{:S(2)}) copy-start(f32[2,1,32,128]{3,2,0,1:T(8,128)S(1)} %get-tuple-element.274) | copy-start | bytes 98308
  69.5 36.1 %copy-start.195 = (f32[2,1,32,128]{3,2,0,1:T(8,128)}, f32[2,1,32,128]{3,2,0,1:T(8,128)S(1)}, u32[]{:S(2)}) copy-start(f32[2,1,32,128]{3,2,0,1:T(8,128)S(1)} %get-tuple-element.277) | copy-start | bytes 98308
  69.6 36.1 %copy-start.196 = (f32[2,1,32,128]{3,2,0,1:T(8,128)}, f32[2,1,32,128]{3,2,0,1:T(8,128)S(1)}, u32[]{:S(2)}) copy-start(f32[2,1,32,128]{3,2,0,1:T(8,128)S(1)} %get-tuple-element.280) | copy-start | bytes 98308
  69.6 36.1 %copy-start.197 = (f32[2,1,32,128]{3,2,0,1:T(8,128)}, f32[2,1,32,128]{3,2,0,1:T(8,128)S(1)}, u32[]{:S(2)}) copy-start(f32[2,1,32,128]{3,2,0,1:T(8,128)S(1)} %get-tuple-element.283) | copy-start | bytes 98308
  69.6 36.1 %copy-start.198 = (f32[2,1,32,128]{3,2,0,1:T(8,128)}, f32[2,1,32,128]{3,2,0,1:T(8,128)S(1)}, u32[]{:S(2)}) copy-start(f32[2,1,32,128]{3,2,0,1:T(8,128)S(1)} %get-tuple-element.286) | copy-start | bytes 98308
  69.6 36.1 %copy-start.199 = (f32[2,1,32,128]{3,2,0,1:T(8,128)}, f32[2,1,32,128]{3,2,0,1:T(8,128)S(1)}, u32[]{:S(2)}) copy-start(f32[2,1,32,128]{3,2,0,1:T(8,128)S(1)} %get-tuple-element.289) | copy-start | bytes 98308
  69.6 36.1 %copy-start.200 = (f32[2,1,32,128]{3,2,0,1:T(8,128)}, f32[2,1,32,128]{3,2,0,1:T(8,128)S(1)}, u32[]{:S(2)}) copy-start(f32[2,1,32,128]{3,2,0,1:T(8,128)S(1)} %get-tuple-element.292) | copy-start | bytes 98308
  69.6 36.1 %copy-start.201 = (f32[2,1,32,128]{3,2,0,1:T(8,128)}, f32[2,1,32,128]{3,2,0,1:T(8,128)S(1)}, u32[]{:S(2)}) copy-start(f32[2,1,32,128]{3,2,0,1:T(8,128)S(1)} %get-tuple-element.295) | copy-start | bytes 98308
  69.6 36.1 %copy-start.202 = (f32[2,1,32,128]{3,2,0,1:T(8,128)}, f32[2,1,32,128]{3,2,0,1:T(8,128)S(1)}, u32[]{:S(2)}) copy-start(f32[2,1,32,128]{3,2,0,1:T(8,128)S(1)} %get-tuple-element.298) | copy-start | bytes 98308
  72.9 32.9 %copy-start.136 = (f32[2,1,32,128]{3,2,0,1:T(8,128)}, f32[2,1,32,128]{3,2,0,1:T(8,128)S(1)}, u32[]{:S(2)}) copy-start(f32[2,1,32,128]{3,2,0,1:T(8,128)S(1)} %get-tuple-element.152) | copy-start | bytes 98308
  72.9 32.9 %copy-start.137 = (f32[2,1,32,128]{3,2,0,1:T(8,128)}, f32[2,1,32,128]{3,2,0,1:T(8,128)S(1)}, u32[]{:S(2)}) copy-start(f32[2,1,32,128]{3,2,0,1:T(8,128)S(1)} %get-tuple-element.153) | copy-start | bytes 98308
  72.9 32.9 %copy-start.187 = (f32[2,1,32,128]{3,2,0,1:T(8,128)}, f32[2,1,32,128]{3,2,0,1:T(8,128)S(1)}, u32[]{:S(2)}) copy-start(f32[2,1,32,128]{3,2,0,1:T(8,128)S(1)} %get-tuple-element.154) | copy-start | bytes 98308
  72.9 32.9 %copy-start.188 = (f32[2,1,32,128]{3,2,0,1:T(8,128)}, f32[2,1,32,128]{3,2,0,1:T(8,128)S(1)}, u32[]{:S(2)}) copy-start(f32[2,1,32,128]{3,2,0,1:T(8,128)S(1)} %get-tuple-element.156) | copy-start | bytes 98308
  72.9 34.9 %copy-start.157 = (f32[2,1,32,128]{3,2,0,1:T(8,128)}, f32[2,1,32,128]{3,2,0,1:T(8,128)S(1)}, u32[]{:S(2)}) copy-start(f32[2,1,32,128]{3,2,0,1:T(8,128)S(1)} %get-tuple-element.155) | copy-start | bytes 98308
  72.9 34.9 %copy-start.158 = (f32[2,1,32,128]{3,2,0,1:T(8,128)}, f32[2,1,32,128]{3,2,0,1:T(8,128)S(1)}, u32[]{:S(2)}) copy-start(f32[2,1,32,128]{3,2,0,1:T(8,128)S(1)} %get-tuple-element.157) | copy-start | bytes 98308
  113.1 5.9 %collective-permute-start.4 = (f32[2,50,32,1]{1,2,3,0:T(8,128)}, f32[2,50,32,1]{1,2,3,0:T(8,128)S(1)}, u32[]{:S(2)}, u32[]{:S(2)}) collective-permute-start(f32[2,50,32,1]{1,2,3,0:T(8,128)} %copy.792), channel_id=1, source_target_pairs={{3,0},{0,1},{1,2},{2,3},{7,4},{4,5},{5,6},{6,7},{11,8},{8,9},{9,10... | collective-permute-start | bytes 38408 | tf_op jit(solution)/shard_map/ppermute | solution.py:16
  113.1 8.5 %collective-permute-start.6 = (f32[2,50,1,128]{3,2,0,1:T(1,128)}, f32[2,50,1,128]{3,2,0,1:T(1,128)S(1)}, u32[]{:S(2)}, u32[]{:S(2)}) collective-permute-start(f32[2,50,1,128]{3,2,0,1:T(1,128)} %slice.1075), channel_id=1, source_target_pairs={{4,0},{0,4},{5,1},{1,5},{6,2},{2,6},{7,3},{3,7},{12,8},{8,12},{13,... | collective-permute-start | bytes 153608 | tf_op jit(solution)/shard_map/ppermute | solution.py:16
  128.8 12.1 %collective-permute-start.5 = (f32[2,50,32,1]{1,2,3,0:T(8,128)}, f32[2,50,32,1]{1,2,3,0:T(8,128)}, u32[]{:S(2)}, u32[]{:S(2)}) collective-permute-start(f32[2,50,32,1]{1,2,3,0:T(8,128)} %copy.794), channel_id=1, source_target_pairs={{1,0},{2,1},{3,2},{0,3},{5,4},{6,5},{7,6},{4,7},{9,8},{10,9},{11,1... | collective-permute-start | bytes 38408 | tf_op jit(solution)/shard_map/ppermute | solution.py:16
  130.8 13.8 %collective-permute-start.7 = (f32[2,50,1,128]{3,2,0,1:T(1,128)}, f32[2,50,1,128]{3,2,0,1:T(1,128)}, u32[]{:S(2)}, u32[]{:S(2)}) collective-permute-start(f32[2,50,1,128]{3,2,0,1:T(1,128)} %slice.1078), channel_id=1, source_target_pairs={{4,0},{0,4},{5,1},{1,5},{6,2},{2,6},{7,3},{3,7},{12,8},{8,12},{13,... | collective-permute-start | bytes 153608 | tf_op jit(solution)/shard_map/ppermute | solution.py:16
  160.1 57.5 %copy-start.214 = (s32[8]{0:T(128)S(1)}, s32[8]{0:T(128)}, u32[]{:S(2)}) copy-start(s32[8]{0:T(128)} %param.13) | copy-start | bytes 100
  (175 other events, 1667.4 us)
where the time goes:
time: 222 us; the launch traced here: 219 us
  other arithmetic  69 us (31%)
  local copies, waits for them, and re-layouts  68.2 us (31%)
  blocking collectives  55 us (25%)
  starting transfers between devices  10.6 us (5%)
  matrix products  8.58 us (4%)
  waiting for transfers between devices  3.6 us (2%)
  between operations  3.49 us (2%)
    unnamed x528, local copies, waits for them, and re-layouts  38.2 us
    all_gather x1, blocking collectives, local(): lax.all_gather(stats[None], ('ty', 'tx'), axis=0, tiled=True)  33.3 us
    mul x42, other arithmetic, column_solve(): solved.insert(0, values[position] - factors[position] * solved[0])  26.3 us
    psum x2, blocking collectives, local(): first_sum, second_sum = lax.psum((first_local, second_local), 'mem')  21.7 us
    ppermute x4, local copies, waits for them, and re-layouts, shifted(): return lax.ppermute(block, axis, route)  11.6 us
    ppermute x8, starting transfers between devices, shifted(): return lax.ppermute(block, axis, route)  10.6 us
    div x4, other arithmetic, column_solve(): (rhs_list[position] + coeff[position] * values[position - 1]) / pivot  9.91 us
    sub x2, other arithmetic, substep_run(): east_wind = east_wind - horiz_ratio * (pressure - pressure_west)  9.56 us
  transfers between devices with their start and end apart: 8, of which 1 were waited for; matrix products, arithmetic and copies ran while one was open for 28% of the time, Pallas kernels for 0%

commit v1 on v0

v1 whole, which is shorter than its diff:
```python
import functools

import jax
import jax.numpy as jnp
from jax import lax
from jax.experimental import pallas as pl
from jax.experimental.pallas import tpu as pltpu
from jax.sharding import PartitionSpec as P

HORIZ = 0.35
VERT = 1.5

VMEM = pl.BlockSpec(memory_space=pltpu.VMEM)
SMEM = pl.BlockSpec(memory_space=pltpu.SMEM)


def divisor(count, most):
    return max(d for d in range(1, most + 1) if count % d == 0)


def lanes_of(shape):
    return lax.broadcasted_iota(jnp.int32, shape, len(shape) - 1)


def rows_of(shape):
    return lax.broadcasted_iota(jnp.int32, shape, len(shape) - 2)


def west_roll(x):
    return pltpu.roll(x, 1, 1)


def east_roll(x):
    return pltpu.roll(x, x.shape[1] - 1, 1)


def south_roll(x):
    return pltpu.roll(x, 1, 0)


def north_roll(x):
    return pltpu.roll(x, x.shape[0] - 1, 0)


def pack_kernel(p_ref, u_ref, v_ref, cols_ref, rows_ref):
    members, levels, rows, cols = p_ref.shape
    lane = lanes_of((rows, cols))
    for m in range(members):
        packed = jnp.zeros((rows, cols), jnp.float32)
        for k in range(levels):
            p = p_ref[m, k]
            z = u_ref[m, k] - HORIZ * p
            edge = pltpu.roll(jnp.where(lane == cols - 1, p, z), 2 * k + 1, 1)
            packed = jnp.where(lane >= 2 * k, edge, packed)
            rows_ref[0, m, k : k + 1, :] = p[rows - 1 : rows, :]
            rows_ref[1, m, k : k + 1, :] = v_ref[m, k, 0:1, :] - HORIZ * p[0:1, :]
        cols_ref[m] = packed


def main_kernel(
    p_ref, u_ref, v_ref, w_ref, c_ref, th_ref, from_west, from_east, from_rows,
    sums_ref, cols_ref, rows_ref, hcols_ref, hrows_ref,
    e_s, inv_s, s_s, g_s, h_s, hw_s, he_s, hs_s, hn_s, part_s, v_s, u1_s, v1_s,
):
    members, levels, rows, cols = p_ref.shape
    inner = levels - 1
    shape = (rows, cols)
    lane = lanes_of(shape)
    row = rows_of(shape)
    first_lane, last_lane = lane == 0, lane == cols - 1
    first_row, last_row = row == 0, row == rows - 1
    zero = jnp.zeros(shape, jnp.float32)
    vsq = VERT * VERT

    step = divisor(inner, 8)

    def factor(chunk, carry):
        e_prev, s_prev, c_here = carry
        for sub in range(step):
            i = chunk * step + sub
            c_next = c_ref[i + 1]
            b_next = vsq * c_next
            pivot = (1.0 + b_next) + (vsq * c_here) * (1.0 - e_prev)
            inv = 1.0 / pivot
            s_prev = VERT * (th_ref[i + 1] * c_next - th_ref[i] * c_here) + e_prev * s_prev
            e_prev = b_next * inv
            e_s[i] = e_prev
            inv_s[i] = inv
            s_s[i] = s_prev * inv
            c_here = c_next
        return e_prev, s_prev, c_here

    lax.fori_loop(0, inner // step, factor, (zero, zero, c_ref[0]))

    def weights(k, y_above, y_here):
        g = th_ref[k] + VERT * (y_above - y_here)
        h = g * (HORIZ * c_ref[k])
        g_s[k] = g - (2 * HORIZ) * h
        h_s[k] = h
        h35 = HORIZ * h
        hw_s[k] = jnp.where(first_lane, 0.0, west_roll(h))
        he_s[k] = jnp.where(last_lane, 0.0, east_roll(h35))
        hs_s[k] = jnp.where(first_row, 0.0, south_roll(h))
        hn_s[k] = jnp.where(last_row, 0.0, north_roll(h35))
        hrows_ref[0, pl.ds(k, 1), :] = h35[0:1, :]
        hrows_ref[1, pl.ds(k, 1), :] = h[rows - 1 : rows, :]
        return west_roll(jnp.where(last_lane, -h, h35))

    def adjoint(chunk, carry):
        y_above, packed = carry
        for sub in range(step):
            i = inner - 1 - (chunk * step + sub)
            y_here = s_s[i] + e_s[i] * y_above
            s_s[i] = y_here
            edge = weights(i + 1, y_above, y_here)
            packed = jnp.where(lane < 2, edge, pltpu.roll(packed, 2, 1))
            y_above = y_here
        return y_above, packed

    y_low, packed = lax.fori_loop(0, inner // step, adjoint, (zero, zero))
    edge = weights(0, y_low, zero)
    hcols_ref[...] = jnp.where(lane < 2, edge, pltpu.roll(packed, 2, 1))

    step1 = divisor(levels, 5)
    halo = []
    even = lane % 2 == 0
    for m in range(members):
        mixed = jnp.where(even, east_roll(from_east[m]), HORIZ * west_roll(from_west[m]))
        halo.append(east_roll(mixed))

    def upward(chunk, carry):
        part_prev, v_prev, halo = (list(x) for x in carry)
        for sub in range(step1):
            k = chunk * step1 + sub
            c = c_ref[k]
            c35 = HORIZ * c
            below = jnp.maximum(k - 1, 0)
            before = jnp.maximum(k - 2, 0)
            e = e_s[before]
            for m in range(members):
                p = p_ref[m, k]
                q = HORIZ * p
                zu = u_ref[m, k] - q
                zv = v_ref[m, k] - q
                edge = halo[m] if sub == 0 else pltpu.roll(halo[m], cols - 2 * sub, 1)
                q_west = jnp.where(first_lane, edge, west_roll(q))
                zu_east = jnp.where(last_lane, edge, east_roll(zu))
                q_south = jnp.where(first_row, HORIZ * from_rows[0, m, pl.ds(k, 1), :], south_roll(q))
                zv_north = jnp.where(last_row, from_rows[1, m, pl.ds(k, 1), :], north_roll(zv))
                u1 = zu + q_west
                v1 = zv + q_south
                u1_s[m, k] = u1
                v1_s[m, k] = v1
                div = ((zu_east + q) - u1) + ((zv_north + q) - v1)
                part = p - c35 * div
                part_s[m, k] = part
                rhs = w_ref[m, below] - VERT * (part - part_prev[m])
                v_new = rhs + e * v_prev[m]
                v_s[m, below] = v_new
                if sub == 0:
                    v_new = jnp.where(k == 0, 0.0, v_new)
                v_prev[m] = v_new
                part_prev[m] = part
        halo = [pltpu.roll(x, cols - 2 * step1, 1) for x in halo]
        return tuple(part_prev), tuple(v_prev), tuple(halo)

    zeros = (zero,) * members
    lax.fori_loop(0, levels // step1, upward, (zeros, zeros, tuple(halo)))

    group = 8
    gshape = (group, cols)
    glane = lanes_of(gshape)
    glast = glane == cols - 1
    gzero = jnp.zeros(gshape, jnp.float32)
    for r in range(rows // group):
        rs = slice(r * group, (r + 1) * group)

        def downward(chunk, carry, r=r, rs=rs):
            state = [list(x) for x in carry]
            for sub in range(step1):
                k = levels - 1 - (chunk * step1 + sub)
                below = jnp.maximum(k - 1, 0)
                inv = inv_s[below, rs]
                e = e_s[below, rs]
                c15 = VERT * c_ref[k, rs]
                g = g_s[k, rs]
                y = s_s[below, rs]
                h = h_s[k, rs]
                hw, he, hs, hn = hw_s[k, rs], he_s[k, rs], hs_s[k, rs], hn_s[k, rs]
                th = th_ref[k]
                for m in range(members):
                    w, mass, ps, us, vs, ce, cw, cn, cs, packed = state[m]
                    w_low = v_s[m, below, rs] * inv + e * w
                    if sub == step1 - 1:
                        w_low = jnp.where(k == 0, 0.0, w_low)
                    p = part_s[m, k, rs] - c15 * (w - w_low)
                    q = HORIZ * p
                    zu = u1_s[m, k, rs] - q
                    zv = v1_s[m, k, rs] - q
                    mass = mass + ((g * p + y * w_low) + h * (zu + zv))
                    ps = ps + th * p
                    us = us + th * zu
                    vs = vs + th * zv
                    ce = ce + hw * zu
                    cw = cw + he * p
                    cn = cn + hs * zv
                    cs = cs + hn * p
                    edge = pltpu.roll(jnp.where(glast, p, zu), 1, 1)
                    packed = jnp.where(glane < 2, edge, pltpu.roll(packed, 2, 1))
                    if r == rows // group - 1:
                        rows_ref[0, m, pl.ds(k, 1), :] = p[group - 1 : group, :]
                    if r == 0:
                        rows_ref[1, m, pl.ds(k, 1), :] = zv[0:1, :]
                    state[m] = [w_low, mass, ps, us, vs, ce, cw, cn, cs, packed]
            return tuple(tuple(x) for x in state)

        init = ((gzero,) * 10,) * members
        out = lax.fori_loop(0, levels // step1, downward, init)
        for m in range(members):
            w, mass, ps, us, vs, ce, cw, cn, cs, packed = out[m]
            sums_ref[m, 0, rs] = mass - east_roll(ce) + west_roll(cw)
            sums_ref[m, 1, rs] = us + jnp.where(glane == 0, 0.0, HORIZ * west_roll(ps))
            sums_ref[m, 2, rs] = vs
            tail = pltpu.roll(ps, 2 * levels + 1, 1)
            cols_ref[m, rs] = jnp.where(glane == 2 * levels, tail, packed)
            part_s[m, 0, rs] = ps
            part_s[m, 1, rs] = cn
            part_s[m, 2, rs] = cs
    for m in range(members):
        ps, cn, cs = part_s[m, 0], part_s[m, 1], part_s[m, 2]
        sums_ref[m, 0] = sums_ref[m, 0] - north_roll(cn) + south_roll(cs)
        sums_ref[m, 2] = sums_ref[m, 2] + jnp.where(first_row, 0.0, HORIZ * south_roll(ps))
        rows_ref[0, m, levels : levels + 1, :] = ps[rows - 1 : rows, :]
        rows_ref[1, m, levels : levels + 1, :] = jnp.zeros((1, cols), jnp.float32)


def edge_kernel(sums_ref, from_west, from_east, from_rows, hcols_ref, hrows_ref, out_ref):
    members, fields, rows, cols = sums_ref.shape
    levels = hrows_ref.shape[1]
    quarters = out_ref.shape[0]
    height = rows // quarters
    lane = lanes_of((rows, cols))
    row = rows_of((rows, cols))
    even = lane % 2 == 0
    used = lane < 2 * levels
    for m in range(members):
        west = from_west[m]
        east = east_roll(from_east[m])
        products = jnp.where(used, hcols_ref[...] * jnp.where(even, east, west_roll(west)), 0.0)
        at_east = jnp.sum(jnp.where(even, products, 0.0), axis=1, keepdims=True)
        at_west = jnp.sum(jnp.where(even, 0.0, products), axis=1, keepdims=True)
        at_south = jnp.sum(hrows_ref[0] * from_rows[0, m, :levels, :], axis=0, keepdims=True)
        at_north = jnp.sum(hrows_ref[1] * from_rows[1, m, :levels, :], axis=0, keepdims=True)
        ps_west = pltpu.roll(west, cols - 2 * levels, 1)
        ps_south = from_rows[0, m, levels : levels + 1, :]
        mass = sums_ref[m, 0] + jnp.where(lane == 0, at_west, 0.0) + jnp.where(lane == cols - 1, at_east, 0.0)
        mass = mass + jnp.where(row == 0, at_south, 0.0) - jnp.where(row == rows - 1, at_north, 0.0)
        east_total = sums_ref[m, 1] + jnp.where(lane == 0, HORIZ * ps_west, 0.0)
        north_total = sums_ref[m, 2] + jnp.where(row == 0, HORIZ * ps_south, 0.0)
        for f, total in enumerate((mass, east_total, north_total)):
            for q in range(quarters):
                out_ref[q, m, f] = total[q * height : (q + 1) * height, :]


def stats_kernel(in_ref, out_ref):
    ranks, members, fields, height, cols = in_ref.shape
    slots = out_ref.shape[0]
    count = ranks * members
    for f in range(fields):
        values = [in_ref[r, m, f] for r in range(ranks) for m in range(members)]
        mean = functools.reduce(jnp.add, values) / count
        square = functools.reduce(jnp.add, [(v - mean) * (v - mean) for v in values]) / (count - 1)
        for s in range(slots):
            out_ref[s, f] = mean
            out_ref[s, fields + f] = square


def pick_kernel(owner_ref, me_ref, in_ref, out_ref):
    me = me_ref[0]
    source = jnp.int32(0)
    for t in range(in_ref.shape[0]):
        source = jnp.where(owner_ref[t] == me, t, source)
    out_ref[0, 0] = in_ref[source]


def call(kernel, outs, in_specs, scratch=(), limit=None):
    return pl.pallas_call(
        kernel,
        out_shape=[jax.ShapeDtypeStruct(s, jnp.float32) for s in outs],
        in_specs=in_specs,
        out_specs=[VMEM] * len(outs),
        scratch_shapes=list(scratch),
        compiler_params=pltpu.CompilerParams(vmem_limit_bytes=limit),
    )


def shifted(block, axis, distance):
    count = lax.axis_size(axis)
    return lax.ppermute(block, axis, [((i - distance) % count, i) for i in range(count)])


def exchange(columns, edge_rows):
    west = shifted(columns, "tx", 1)
    east = shifted(columns, "tx", -1)
    if lax.axis_size("ty") <= 2:
        both = shifted(edge_rows, "ty", 1)
    else:
        south = shifted(edge_rows[0], "ty", 1)
        north = shifted(edge_rows[1], "ty", -1)
        both = jnp.stack([south, north])
    return west, east, both


def local(pressure, east_wind, north_wind, vertical_wind, sound_squared, thickness, owner_map):
    members, levels, rows, cols = pressure.shape
    ranks = lax.axis_size("mem")
    tiles = lax.axis_size("ty") * lax.axis_size("tx")
    height = rows // ranks
    mib = 1024 * 1024
    plane = (members, rows, cols)
    columns, edge_rows = call(
        pack_kernel, [plane, (2, members, levels + 1, cols)], [VMEM] * 3, limit=16 * mib
    )(pressure, east_wind, north_wind)
    west, east, both = exchange(columns, edge_rows)
    field = pltpu.VMEM((levels, rows, cols), jnp.float32)
    many = pltpu.VMEM((members, levels, rows, cols), jnp.float32)
    sums, columns, edge_rows, hcols, hrows = call(
        main_kernel,
        [
            (members, 3, rows, cols),
            plane,
            (2, members, levels + 1, cols),
            (rows, cols),
            (2, levels, cols),
        ],
        [VMEM] * 5 + [SMEM] + [VMEM] * 3,
        [field] * 9 + [many] * 4,
        limit=32 * mib,
    )(
        pressure, east_wind, north_wind, vertical_wind, sound_squared, thickness, west, east, both
    )
    west, east, both = exchange(columns, edge_rows)
    (integrals,) = call(
        edge_kernel, [(ranks, members, 3, height, cols)], [VMEM] * 6, limit=16 * mib
    )(sums, west, east, both, hcols, hrows)
    gathered = lax.all_to_all(integrals, "mem", 0, 0)
    (slots,) = call(stats_kernel, [(tiles, 6, height, cols)], [VMEM], limit=16 * mib)(gathered)
    routed = lax.all_to_all(slots, ("ty", "tx"), 0, 0)
    me = lax.axis_index(("ty", "tx")).astype(jnp.int32).reshape(1)
    (result,) = call(
        pick_kernel, [(1, 1, 6, height, cols)], [SMEM, SMEM, VMEM], limit=16 * mib
    )(owner_map, me, routed)
    return result


def solution(mesh):
    placed = (
        P("mem", None, "ty", "tx"),
        P("mem", None, "ty", "tx"),
        P("mem", None, "ty", "tx"),
        P("mem", None, "ty", "tx"),
        P(None, "ty", "tx"),
        P(),
        P(),
    )
    return jax.shard_map(
        local,
        mesh=mesh,
        in_specs=placed,
        out_specs=P("ty", "tx", None, "mem", None),
        check_vma=False,
    )
```

time: 222 us -> 67.7 us (0.30); the launches traced: 219 us -> 67.3 us
  other arithmetic: 69 us -> 0 us
  local copies, waits for them, and re-layouts: 68.2 us -> 6.87 us
  blocking collectives: 55 us -> 6.98 us
  Pallas kernels: 0 us -> 23.7 us
  waiting for transfers between devices: 3.6 us -> 12.5 us
  matrix products: 8.58 us -> 0 us
  starting transfers between devices: 10.6 us -> 17.2 us
  between operations: 3.49 us -> 0.07 us
    all_gather x1 -> x0, blocking collectives: 33.3 us -> none  [local(): lax.all_gather(stats[None], ('ty', 'tx'), axis=0, tiled=True)]
    unnamed x528 -> x20, local copies, waits for them, and re-layouts: 38.2 us -> 6.87 us
    mul x43 -> x0, other arithmetic: 28.9 us -> none  [the longest x42 26.3 us: column_solve(): solved.insert(0, values[position] - factors[position] * solved[0])]
    pallas_call x0 -> x5, Pallas kernels: none -> 23.7 us  [the longest x1 21.1 us: local(): call(main_kernel, [(members, 3, rows, cols), plane, (2, members, levels +...]
    psum x2 -> x0, blocking collectives: 21.7 us -> none  [local(): first_sum, second_sum = lax.psum((first_local, second_local), 'mem')]
    sub x6 -> x0, other arithmetic: 20.3 us -> none  [the longest x2 9.56 us: substep_run(): east_wind = east_wind - horiz_ratio * (pressure - pressure_west)]
    slice x13 -> x0, local copies, waits for them, and re-layouts: 18.3 us -> none  [the longest x3 4.18 us: substep_run(): western = shifted(pressure[..., -1:], 'tx', 1)]
    ppermute x4 -> x0, local copies, waits for them, and re-layouts: 11.6 us -> none  [shifted(): return lax.ppermute(block, axis, route)]
  transfers between devices with their start and end apart: 8 -> 7, of which waited for: 1 -> 3; matrix products, arithmetic and copies ran while one was open for 28% -> 0% of each run, Pallas kernels for 0% -> 0%
where the time goes in v1:
time: 67.7 us; the launch traced here: 67.3 us
  Pallas kernels  23.7 us (35%)
  starting transfers between devices  17.2 us (25%)
  waiting for transfers between devices  12.5 us (18%)
  blocking collectives  6.98 us (10%)
  local copies, waits for them, and re-layouts  6.87 us (10%)
    pallas_call x1, Pallas kernels, local(): call(main_kernel, [(members, 3, rows, cols), plane, (2, members, levels +...  21.1 us
    ppermute x6, starting transfers between devices, shifted(): lax.ppermute(block, axis, [((i - distance) % count, i) for i in range(cou...  11.2 us
    all_to_all x1, waiting for transfers between devices, local(): routed = lax.all_to_all(slots, ('ty', 'tx'), 0, 0)  8.46 us
    all_to_all x1, blocking collectives, local(): gathered = lax.all_to_all(integrals, 'mem', 0, 0)  6.98 us
    unnamed x20, local copies, waits for them, and re-layouts  6.87 us
    all_to_all x1, starting transfers between devices, local(): routed = lax.all_to_all(slots, ('ty', 'tx'), 0, 0)  6.05 us
    ppermute x6, waiting for transfers between devices, shifted(): lax.ppermute(block, axis, [((i - distance) % count, i) for i in range(cou...  4.03 us
  transfers between devices with their start and end apart: 7, of which 3 were waited for; matrix products, arithmetic and copies ran while one was open for 0% of the time, Pallas kernels for 0%

profile of v1, /device:TPU:0, one launch (start us, length us, event | category | flops | bytes accessed | tf_op | source)
XLA Modules:
  0.0 67.3 jit_solution(4325636109456212328)
XLA Ops:
  0.0 0.0 copy-start
  0.0 1.4 %copy-done = f32[2,50,32,128]{3,2,1,0:T(8,128)S(1)} copy-done((f32[2,50,32,128]{3,2,1,0:T(8,128)S(1)}, f32[2,50,32,128]{3,2,1,0:T(8,128)}, u32[]{:S(2)}) %copy-start) | copy-done | bytes 1638424
  1.4 0.0 copy-start.2
  1.4 1.4 %copy-done.2 = f32[2,50,32,128]{3,2,1,0:T(8,128)S(1)} copy-done((f32[2,50,32,128]{3,2,1,0:T(8,128)S(1)}, f32[2,50,32,128]{3,2,1,0:T(8,128)}, u32[]{:S(2)}) %copy-start.2) | copy-done | bytes 1638424
  2.9 0.0 copy-start.4
  2.9 1.4 %copy-done.4 = f32[2,50,32,128]{3,2,1,0:T(8,128)S(1)} copy-done((f32[2,50,32,128]{3,2,1,0:T(8,128)S(1)}, f32[2,50,32,128]{3,2,1,0:T(8,128)}, u32[]{:S(2)}) %copy-start.4) | copy-done | bytes 1638424
  4.3 0.0 copy-start.1
  4.3 0.0 copy-start.3
  4.3 0.0 copy-start.5
  4.3 0.0 copy-start.9
  4.3 0.5 shard_map.73
  4.8 3.1 %collective-permute-start.2 = (f32[2,2,51,128]{3,2,1,0:T(8,128)S(1)}, f32[2,2,51,128]{3,2,1,0:T(8,128)S(1)}, u32[]{:S(2)}, u32[]{:S(2)}) collective-permute-start(f32[2,2,51,128]{3,2,1,0:T(8,128)S(1)} %get-tuple-element.13), channel_id=1, source_target_pairs={{4,0},{0,4},{5,1},{1,5},{6,2},{2,6},{7,3},{3,7},{12,8},{8,12},{13,... | collective-permute-start | bytes 313352 | tf_op jit(solution)/shard_map/ppermute | solution.py:299
  7.9 0.0 copy-start.8
  7.9 1.6 %collective-permute-start = (f32[2,32,128]{2,1,0:T(8,128)S(1)}, f32[2,32,128]{2,1,0:T(8,128)S(1)}, u32[]{:S(2)}, u32[]{:S(2)}) collective-permute-start(f32[2,32,128]{2,1,0:T(8,128)S(1)} %get-tuple-element.12), channel_id=1, source_target_pairs={{3,0},{0,1},{1,2},{2,3},{7,4},{4,5},{5,6},{6,7},{11,8},{8,9},{9,10... | collective-permute-start | bytes 98312 | tf_op jit(solution)/shard_map/ppermute | solution.py:299
  9.5 2.2 %collective-permute-start.1 = (f32[2,32,128]{2,1,0:T(8,128)S(1)}, f32[2,32,128]{2,1,0:T(8,128)S(1)}, u32[]{:S(2)}, u32[]{:S(2)}) collective-permute-start(f32[2,32,128]{2,1,0:T(8,128)S(1)} %get-tuple-element.12), channel_id=1, source_target_pairs={{1,0},{2,1},{3,2},{0,3},{5,4},{6,5},{7,6},{4,7},{9,8},{10,9},{11,1... | collective-permute-start | bytes 98312 | tf_op jit(solution)/shard_map/ppermute | solution.py:299
  11.7 2.1 %collective-permute-done.from_west = f32[2,32,128]{2,1,0:T(8,128)S(1)} collective-permute-done((f32[2,32,128]{2,1,0:T(8,128)S(1)}, f32[2,32,128]{2,1,0:T(8,128)S(1)}, u32[]{:S(2)}, u32[]{:S(2)}) %collective-permute-start) | collective-permute-done | bytes 32800 | tf_op jit(solution)/shard_map/ppermute | solution.py:299
  13.8 0.0 collective-permute-done.1.from_east
  13.8 0.0 collective-permute-done.2.from_rows
  13.8 0.0 copy-done.1
  13.8 0.0 copy-done.3
  13.9 0.0 copy-done.5
  13.9 0.0 copy-done.9
  13.9 0.0 copy-start.6
  13.9 1.4 %copy-done.6 = f32[2,49,32,128]{3,2,1,0:T(8,128)S(1)} copy-done((f32[2,49,32,128]{3,2,1,0:T(8,128)S(1)}, f32[2,49,32,128]{3,2,1,0:T(8,128)}, u32[]{:S(2)}) %copy-start.6) | copy-done | bytes 1605656
  15.3 0.0 copy-start.7
  15.3 1.1 %copy-done.7 = f32[50,32,128]{2,1,0:T(8,128)S(1)} copy-done((f32[50,32,128]{2,1,0:T(8,128)S(1)}, f32[50,32,128]{2,1,0:T(8,128)}, u32[]{:S(2)}) %copy-start.7) | copy-done | bytes 819224
  16.4 21.1 %shard_map.74 = (f32[2,3,32,128]{3,2,1,0:T(8,128)S(1)}, f32[2,32,128]{2,1,0:T(8,128)S(1)}, f32[2,2,51,128]{3,2,1,0:T(8,128)S(1)}, f32[32,128]{1,0:T(8,128)S(1)}, f32[2,50,128]{2,1,0:T(8,128)S(1)}) custom-call(f32[2,50,32,128]{3,2,1,0:T(8,128)S(1)} %copy-done.1, f32[2,50,32,128]{3,2,1,0:T(8,128)S(1)} %copy-done.3, f32[2,50,32,128]{3,2,1,0:T(8,128)S(1)} %copy-done.5, ...), custom_call_target="tpu_custom_call" | custom-call | tf_op jit(solution)/shard_map/pallas_call | solution.py:327
  37.6 0.4 collective-permute-start.5
  38.0 1.2 %collective-permute-start.3 = (f32[2,32,128]{2,1,0:T(8,128)S(1)}, f32[2,32,128]{2,1,0:T(8,128)S(1)}, u32[]{:S(2)}, u32[]{:S(2)}) collective-permute-start(f32[2,32,128]{2,1,0:T(8,128)S(1)} %get-tuple-element.15), channel_id=1, source_target_pairs={{3,0},{0,1},{1,2},{2,3},{7,4},{4,5},{5,6},{6,7},{11,8},{8,9},{9,10... | collective-permute-start | bytes 98312 | tf_op jit(solution)/shard_map/ppermute | solution.py:299
  39.3 2.6 %collective-permute-start.4 = (f32[2,32,128]{2,1,0:T(8,128)S(1)}, f32[2,32,128]{2,1,0:T(8,128)S(1)}, u32[]{:S(2)}, u32[]{:S(2)}) collective-permute-start(f32[2,32,128]{2,1,0:T(8,128)S(1)} %get-tuple-element.15), channel_id=1, source_target_pairs={{1,0},{2,1},{3,2},{0,3},{5,4},{6,5},{7,6},{4,7},{9,8},{10,9},{11,1... | collective-permute-start | bytes 98312 | tf_op jit(solution)/shard_map/ppermute | solution.py:299
  41.9 1.9 %collective-permute-done.3.from_west = f32[2,32,128]{2,1,0:T(8,128)S(1)} collective-permute-done((f32[2,32,128]{2,1,0:T(8,128)S(1)}, f32[2,32,128]{2,1,0:T(8,128)S(1)}, u32[]{:S(2)}, u32[]{:S(2)}) %collective-permute-start.3) | collective-permute-done | bytes 32800 | tf_op jit(solution)/shard_map/ppermute | solution.py:299
  43.8 0.0 collective-permute-done.4.from_east
  43.8 0.0 collective-permute-done.5.from_rows
  43.8 0.2 shard_map.75
  43.9 7.0 %all_to_all.10.in_ref = f32[4,2,3,8,128]{4,3,2,1,0:T(8,128)S(1)} all-to-all(f32[4,2,3,8,128]{4,3,2,1,0:T(8,128)S(1)} %shard_map.75), channel_id=1, replica_groups=mesh['mem'=4,'ty'=2,'tx'=4] {'mem'}, dimensions={0} | all-to-all | bytes 196608 | tf_op jit(solution)/shard_map/all_to_all | solution.py:346
  50.9 0.7 %shard_map.76 = f32[8,6,8,128]{3,2,1,0:T(8,128)} custom-call(f32[4,2,3,8,128]{4,3,2,1,0:T(8,128)S(1)} %all_to_all.10.in_ref), custom_call_target="tpu_custom_call" | custom-call | tf_op jit(solution)/shard_map/pallas_call | solution.py:347
  51.6 6.1 %all-to-all-start.1 = ((f32[8,6,8,128]{3,2,1,0:T(8,128)}), f32[8,6,8,128]{3,2,1,0:T(8,128)S(1)}, u32[]{:S(2)}, u32[]{:S(2)}) async-start(f32[8,6,8,128]{3,2,1,0:T(8,128)} %shard_map.76), calls=%async_computation.1 | async-start | bytes 393216 | tf_op jit(solution)/shard_map/all_to_all | solution.py:348
  57.7 8.5 %all-to-all-done.1.in_ref = f32[8,6,8,128]{3,2,1,0:T(8,128)S(1)} async-done(((f32[8,6,8,128]{3,2,1,0:T(8,128)}), f32[8,6,8,128]{3,2,1,0:T(8,128)S(1)}, u32[]{:S(2)}, u32[]{:S(2)}) %all-to-all-start.1) | async-done | bytes 196640 | tf_op jit(solution)/shard_map/all_to_all | solution.py:348
  66.1 0.0 copy-done.8
  66.1 1.2 %shard_map.77 = f32[1,1,6,8,128]{4,3,2,1,0:T(8,128)} custom-call(s32[8]{0:T(128)S(1)} %copy-done.8, s32[1]{0:T(128)} %bitcast.me_ref, f32[8,6,8,128]{3,2,1,0:T(8,128)S(1)} %all-to-all-done.1.in_ref), custom_call_target="tpu_custom_call" | custom-call | tf_op jit(solution)/shard_map/pallas_call | solution.py:350
Async XLA Ops:
  0.0 1.4 %copy-start = (f32[2,50,32,128]{3,2,1,0:T(8,128)S(1)}, f32[2,50,32,128]{3,2,1,0:T(8,128)}, u32[]{:S(2)}) copy-start(f32[2,50,32,128]{3,2,1,0:T(8,128)} %p_ref.3) | copy-start | bytes 4915204
  1.4 1.4 %copy-start.2 = (f32[2,50,32,128]{3,2,1,0:T(8,128)S(1)}, f32[2,50,32,128]{3,2,1,0:T(8,128)}, u32[]{:S(2)}) copy-start(f32[2,50,32,128]{3,2,1,0:T(8,128)} %u_ref.3) | copy-start | bytes 4915204
  2.9 1.4 %copy-start.4 = (f32[2,50,32,128]{3,2,1,0:T(8,128)S(1)}, f32[2,50,32,128]{3,2,1,0:T(8,128)}, u32[]{:S(2)}) copy-start(f32[2,50,32,128]{3,2,1,0:T(8,128)} %v_ref.3) | copy-start | bytes 4915204
  4.3 9.5 %copy-start.1 = (f32[2,50,32,128]{3,2,1,0:T(8,128)S(1)}, f32[2,50,32,128]{3,2,1,0:T(8,128)}, u32[]{:S(2)}) copy-start(f32[2,50,32,128]{3,2,1,0:T(8,128)} %p_ref.3) | copy-start | bytes 4915204
  4.3 9.5 %copy-start.3 = (f32[2,50,32,128]{3,2,1,0:T(8,128)S(1)}, f32[2,50,32,128]{3,2,1,0:T(8,128)}, u32[]{:S(2)}) copy-start(f32[2,50,32,128]{3,2,1,0:T(8,128)} %u_ref.3) | copy-start | bytes 4915204
  4.3 9.6 %copy-start.5 = (f32[2,50,32,128]{3,2,1,0:T(8,128)S(1)}, f32[2,50,32,128]{3,2,1,0:T(8,128)}, u32[]{:S(2)}) copy-start(f32[2,50,32,128]{3,2,1,0:T(8,128)} %v_ref.3) | copy-start | bytes 4915204
  4.3 9.6 %copy-start.9 = (f32[50]{0:T(128)S(1)}, f32[50]{0:T(128)}, u32[]{:S(2)}) copy-start(f32[50]{0:T(128)} %th_ref.1) | copy-start | bytes 604
  4.8 9.0 %collective-permute-start.2 = (f32[2,2,51,128]{3,2,1,0:T(8,128)S(1)}, f32[2,2,51,128]{3,2,1,0:T(8,128)S(1)}, u32[]{:S(2)}, u32[]{:S(2)}) collective-permute-start(f32[2,2,51,128]{3,2,1,0:T(8,128)S(1)} %get-tuple-element.13), channel_id=1, source_target_pairs={{4,0},{0,4},{5,1},{1,5},{6,2},{2,6},{7,3},{3,7},{12,8},{8,12},{13,... | collective-permute-start | bytes 313352 | tf_op jit(solution)/shard_map/ppermute | solution.py:299
  7.9 58.3 %copy-start.8 = (s32[8]{0:T(128)S(1)}, s32[8]{0:T(128)}, u32[]{:S(2)}) copy-start(s32[8]{0:T(128)} %owner_ref.1) | copy-start | bytes 100
  7.9 6.0 %collective-permute-start = (f32[2,32,128]{2,1,0:T(8,128)S(1)}, f32[2,32,128]{2,1,0:T(8,128)S(1)}, u32[]{:S(2)}, u32[]{:S(2)}) collective-permute-start(f32[2,32,128]{2,1,0:T(8,128)S(1)} %get-tuple-element.12), channel_id=1, source_target_pairs={{3,0},{0,1},{1,2},{2,3},{7,4},{4,5},{5,6},{6,7},{11,8},{8,9},{9,10... | collective-permute-start | bytes 98312 | tf_op jit(solution)/shard_map/ppermute | solution.py:299
  9.5 4.4 %collective-permute-start.1 = (f32[2,32,128]{2,1,0:T(8,128)S(1)}, f32[2,32,128]{2,1,0:T(8,128)S(1)}, u32[]{:S(2)}, u32[]{:S(2)}) collective-permute-start(f32[2,32,128]{2,1,0:T(8,128)S(1)} %get-tuple-element.12), channel_id=1, source_target_pairs={{1,0},{2,1},{3,2},{0,3},{5,4},{6,5},{7,6},{4,7},{9,8},{10,9},{11,1... | collective-permute-start | bytes 98312 | tf_op jit(solution)/shard_map/ppermute | solution.py:299
  13.9 1.4 %copy-start.6 = (f32[2,49,32,128]{3,2,1,0:T(8,128)S(1)}, f32[2,49,32,128]{3,2,1,0:T(8,128)}, u32[]{:S(2)}) copy-start(f32[2,49,32,128]{3,2,1,0:T(8,128)} %w_ref.1) | copy-start | bytes 4816900
  15.3 1.1 %copy-start.7 = (f32[50,32,128]{2,1,0:T(8,128)S(1)}, f32[50,32,128]{2,1,0:T(8,128)}, u32[]{:S(2)}) copy-start(f32[50,32,128]{2,1,0:T(8,128)} %c_ref.1) | copy-start | bytes 2457604
  37.6 6.2 %collective-permute-start.5 = (f32[2,2,51,128]{3,2,1,0:T(8,128)S(1)}, f32[2,2,51,128]{3,2,1,0:T(8,128)S(1)}, u32[]{:S(2)}, u32[]{:S(2)}) collective-permute-start(f32[2,2,51,128]{3,2,1,0:T(8,128)S(1)} %get-tuple-element.16), channel_id=1, source_target_pairs={{4,0},{0,4},{5,1},{1,5},{6,2},{2,6},{7,3},{3,7},{12,8},{8,12},{13,... | collective-permute-start | bytes 313352 | tf_op jit(solution)/shard_map/ppermute | solution.py:299
  38.0 5.7 %collective-permute-start.3 = (f32[2,32,128]{2,1,0:T(8,128)S(1)}, f32[2,32,128]{2,1,0:T(8,128)S(1)}, u32[]{:S(2)}, u32[]{:S(2)}) collective-permute-start(f32[2,32,128]{2,1,0:T(8,128)S(1)} %get-tuple-element.15), channel_id=1, source_target_pairs={{3,0},{0,1},{1,2},{2,3},{7,4},{4,5},{5,6},{6,7},{11,8},{8,9},{9,10... | collective-permute-start | bytes 98312 | tf_op jit(solution)/shard_map/ppermute | solution.py:299
  39.3 4.5 %collective-permute-start.4 = (f32[2,32,128]{2,1,0:T(8,128)S(1)}, f32[2,32,128]{2,1,0:T(8,128)S(1)}, u32[]{:S(2)}, u32[]{:S(2)}) collective-permute-start(f32[2,32,128]{2,1,0:T(8,128)S(1)} %get-tuple-element.15), channel_id=1, source_target_pairs={{1,0},{2,1},{3,2},{0,3},{5,4},{6,5},{7,6},{4,7},{9,8},{10,9},{11,1... | collective-permute-start | bytes 98312 | tf_op jit(solution)/shard_map/ppermute | solution.py:299
  51.6 14.5 %all-to-all-start.1 = ((f32[8,6,8,128]{3,2,1,0:T(8,128)}), f32[8,6,8,128]{3,2,1,0:T(8,128)S(1)}, u32[]{:S(2)}, u32[]{:S(2)}) async-start(f32[8,6,8,128]{3,2,1,0:T(8,128)} %shard_map.76), calls=%async_computation.1 | async-start | bytes 393216 | tf_op jit(solution)/shard_map/all_to_all | solution.py:348

commit v2 on v1

--- a/solution.py
+++ b/solution.py
@@ -9,9 +9,12 @@
 
 HORIZ = 0.35
 VERT = 1.5
+STEP_A = 50
+STEP_B = 25
 
 VMEM = pl.BlockSpec(memory_space=pltpu.VMEM)
 SMEM = pl.BlockSpec(memory_space=pltpu.SMEM)
+HBM = pl.BlockSpec(memory_space=pltpu.HBM)
 
 
 def divisor(count, most):
@@ -42,10 +45,22 @@
     return pltpu.roll(x, x.shape[0] - 1, 0)
 
 
-def pack_kernel(p_ref, u_ref, v_ref, cols_ref, rows_ref):
+def pack_kernel(p_hbm, u_hbm, v_hbm, cols_ref, rows_ref, p_ref, u_ref, v_s, sems):
     members, levels, rows, cols = p_ref.shape
+    copies = []
+    for m in range(members):
+        pair = [
+            pltpu.make_async_copy(p_hbm.at[m], p_ref.at[m], sems.at[m, 0]),
+            pltpu.make_async_copy(u_hbm.at[m], u_ref.at[m], sems.at[m, 1]),
+            pltpu.make_async_copy(v_hbm.at[m, :, 0:8], v_s.at[m], sems.at[m, 2]),
+        ]
+        for copy in pair:
+            copy.start()
+        copies.append(pair)
     lane = lanes_of((rows, cols))
     for m in range(members):
+        for copy in copies[m]:
+            copy.wait()
         packed = jnp.zeros((rows, cols), jnp.float32)
         for k in range(levels):
             p = p_ref[m, k]
@@ -53,16 +68,23 @@
             edge = pltpu.roll(jnp.where(lane == cols - 1, p, z), 2 * k + 1, 1)
             packed = jnp.where(lane >= 2 * k, edge, packed)
             rows_ref[0, m, k : k + 1, :] = p[rows - 1 : rows, :]
-            rows_ref[1, m, k : k + 1, :] = v_ref[m, k, 0:1, :] - HORIZ * p[0:1, :]
+            rows_ref[1, m, k : k + 1, :] = v_s[m, k, 0:1, :] - HORIZ * p[0:1, :]
+        rows_ref[0, m, levels : levels + 1, :] = jnp.zeros((1, cols), jnp.float32)
+        rows_ref[1, m, levels : levels + 1, :] = jnp.zeros((1, cols), jnp.float32)
         cols_ref[m] = packed
 
 
-def main_kernel(
-    p_ref, u_ref, v_ref, w_ref, c_ref, th_ref, from_west, from_east, from_rows,
-    sums_ref, cols_ref, rows_ref, hcols_ref, hrows_ref,
-    e_s, inv_s, s_s, g_s, h_s, hw_s, he_s, hs_s, hn_s, part_s, v_s, u1_s, v1_s,
+def weight_kernel(
+    c_ref, v_hbm, w_hbm, th_ref,
+    hcols_ref, hrows_ref, e_s, inv_s, s_s, g_s, h_s, hw_s, he_s, hs_s, hn_s, v_ref, w_ref, sems,
 ):
-    members, levels, rows, cols = p_ref.shape
+    levels, rows, cols = c_ref.shape
+    copies = [
+        pltpu.make_async_copy(v_hbm, v_ref, sems.at[0]),
+        pltpu.make_async_copy(w_hbm, w_ref, sems.at[1]),
+    ]
+    for copy in copies:
+        copy.start()
     inner = levels - 1
     shape = (rows, cols)
     lane = lanes_of(shape)
@@ -72,7 +94,7 @@
     zero = jnp.zeros(shape, jnp.float32)
     vsq = VERT * VERT
 
-    step = divisor(inner, 8)
+    step = divisor(inner, STEP_A)
 
     def factor(chunk, carry):
         e_prev, s_prev, c_here = carry
@@ -104,24 +126,43 @@
         hn_s[k] = jnp.where(last_row, 0.0, north_roll(h35))
         hrows_ref[0, pl.ds(k, 1), :] = h35[0:1, :]
         hrows_ref[1, pl.ds(k, 1), :] = h[rows - 1 : rows, :]
-        return west_roll(jnp.where(last_lane, -h, h35))
+        return jnp.where(last_lane, -h, h35)
 
     def adjoint(chunk, carry):
         y_above, packed = carry
+        packed = pltpu.roll(packed, 2 * step, 1)
         for sub in range(step):
             i = inner - 1 - (chunk * step + sub)
             y_here = s_s[i] + e_s[i] * y_above
             s_s[i] = y_here
             edge = weights(i + 1, y_above, y_here)
-            packed = jnp.where(lane < 2, edge, pltpu.roll(packed, 2, 1))
+            place = 2 * (step - 1 - sub)
+            packed = jnp.where(lane < place + 2, pltpu.roll(edge, place + 1, 1), packed)
             y_above = y_here
         return y_above, packed
 
     y_low, packed = lax.fori_loop(0, inner // step, adjoint, (zero, zero))
     edge = weights(0, y_low, zero)
-    hcols_ref[...] = jnp.where(lane < 2, edge, pltpu.roll(packed, 2, 1))
-
-    step1 = divisor(levels, 5)
+    hcols_ref[...] = jnp.where(lane < 2, pltpu.roll(edge, 1, 1), pltpu.roll(packed, 2, 1))
+    for copy in copies:
+        copy.wait()
+
+
+def main_kernel(
+    p_ref, u_ref, v_ref, w_ref, c_ref, th_ref, e_s, inv_s, s_s, g_s, h_s, hw_s, he_s, hs_s, hn_s,
+    from_west, from_east, from_rows,
+    sums_ref, cols_ref, rows_ref,
+    part_s, v_s, u1_s, v1_s,
+):
+    members, levels, rows, cols = p_ref.shape
+    shape = (rows, cols)
+    lane = lanes_of(shape)
+    row = rows_of(shape)
+    first_lane, last_lane = lane == 0, lane == cols - 1
+    first_row, last_row = row == 0, row == rows - 1
+    zero = jnp.zeros(shape, jnp.float32)
+
+    step1 = divisor(levels, STEP_B)
     halo = []
     even = lane % 2 == 0
     for m in range(members):
@@ -205,8 +246,11 @@
                     cw = cw + he * p
                     cn = cn + hs * zv
                     cs = cs + hn * p
-                    edge = pltpu.roll(jnp.where(glast, p, zu), 1, 1)
-                    packed = jnp.where(glane < 2, edge, pltpu.roll(packed, 2, 1))
+                    place = 2 * (step1 - 1 - sub)
+                    edge = pltpu.roll(jnp.where(glast, p, zu), place + 1, 1)
+                    if sub == 0:
+                        packed = pltpu.roll(packed, 2 * step1, 1)
+                    packed = jnp.where(glane < place + 2, edge, packed)
                     if r == rows // group - 1:
                         rows_ref[0, m, pl.ds(k, 1), :] = p[group - 1 : group, :]
                     if r == 0:
@@ -234,11 +278,12 @@
         rows_ref[1, m, levels : levels + 1, :] = jnp.zeros((1, cols), jnp.float32)
 
 
-def edge_kernel(sums_ref, from_west, from_east, from_rows, hcols_ref, hrows_ref, out_ref):
+def edge_kernel(sums_ref, from_west, from_east, from_rows, hcols_ref, hrows_ref, *rest):
+    outs, total_s = rest[:-1], rest[-1]
     members, fields, rows, cols = sums_ref.shape
     levels = hrows_ref.shape[1]
-    quarters = out_ref.shape[0]
-    height = rows // quarters
+    height = rows // len(outs)
+    mine = lax.axis_index("mem")
     lane = lanes_of((rows, cols))
     row = rows_of((rows, cols))
     even = lane % 2 == 0
@@ -255,101 +300,139 @@
         ps_south = from_rows[0, m, levels : levels + 1, :]
         mass = sums_ref[m, 0] + jnp.where(lane == 0, at_west, 0.0) + jnp.where(lane == cols - 1, at_east, 0.0)
         mass = mass + jnp.where(row == 0, at_south, 0.0) - jnp.where(row == rows - 1, at_north, 0.0)
-        east_total = sums_ref[m, 1] + jnp.where(lane == 0, HORIZ * ps_west, 0.0)
-        north_total = sums_ref[m, 2] + jnp.where(row == 0, HORIZ * ps_south, 0.0)
-        for f, total in enumerate((mass, east_total, north_total)):
-            for q in range(quarters):
-                out_ref[q, m, f] = total[q * height : (q + 1) * height, :]
-
-
-def stats_kernel(in_ref, out_ref):
-    ranks, members, fields, height, cols = in_ref.shape
-    slots = out_ref.shape[0]
-    count = ranks * members
+        total_s[m, 0] = mass
+        total_s[m, 1] = sums_ref[m, 1] + jnp.where(lane == 0, HORIZ * ps_west, 0.0)
+        total_s[m, 2] = sums_ref[m, 2] + jnp.where(row == 0, HORIZ * ps_south, 0.0)
+    for d, out_ref in enumerate(outs):
+        start = pl.multiple_of((mine ^ d) * height, height)
+        out_ref[...] = total_s[:, :, pl.ds(start, height), :]
+
+
+def stats_kernel(*refs):
+    ins, out_ref = refs[:-1], refs[-1]
+    members, fields = ins[0].shape[:2]
+    count = len(ins) * members
     for f in range(fields):
-        values = [in_ref[r, m, f] for r in range(ranks) for m in range(members)]
+        values = [ref[m, f] for ref in ins for m in range(members)]
         mean = functools.reduce(jnp.add, values) / count
         square = functools.reduce(jnp.add, [(v - mean) * (v - mean) for v in values]) / (count - 1)
-        for s in range(slots):
-            out_ref[s, f] = mean
-            out_ref[s, fields + f] = square
-
-
-def pick_kernel(owner_ref, me_ref, in_ref, out_ref):
-    me = me_ref[0]
-    source = jnp.int32(0)
-    for t in range(in_ref.shape[0]):
-        source = jnp.where(owner_ref[t] == me, t, source)
-    out_ref[0, 0] = in_ref[source]
-
-
-def call(kernel, outs, in_specs, scratch=(), limit=None):
+        out_ref[f] = mean
+        out_ref[fields + f] = square
+
+
+def select_kernel(width, owner_ref, *refs):
+    tiles, outs = refs[: -width], refs[-width :]
+    row, column = lax.axis_index("ty"), lax.axis_index("tx")
+    for d, out_ref in enumerate(outs):
+        target = row * width + (column ^ d)
+        value = tiles[0][...]
+        for j in range(1, len(tiles)):
+            here = owner_ref[(row ^ j) * width + column] == target
+            value = jnp.where(here, tiles[j][...], value)
+        out_ref[...] = value
+
+
+def pick_kernel(height_count, owner_ref, *refs):
+    ins, out_ref = refs[:-1], refs[-1]
+    width = len(ins)
+    row, column = lax.axis_index("ty"), lax.axis_index("tx")
+    me = row * width + column
+    value = ins[0][...]
+    for d in range(1, width):
+        source = column ^ d
+        here = owner_ref[source] == me
+        for j in range(1, height_count):
+            here = here | (owner_ref[j * width + source] == me)
+        value = jnp.where(here, ins[d][...], value)
+    out_ref[0, 0] = value
+
+
+def call(kernel, outs, in_specs, scratch=(), limit=16):
     return pl.pallas_call(
         kernel,
         out_shape=[jax.ShapeDtypeStruct(s, jnp.float32) for s in outs],
         in_specs=in_specs,
         out_specs=[VMEM] * len(outs),
         scratch_shapes=list(scratch),
-        compiler_params=pltpu.CompilerParams(vmem_limit_bytes=limit),
+        compiler_params=pltpu.CompilerParams(vmem_limit_bytes=limit * 1024 * 1024),
     )
 
 
-def shifted(block, axis, distance):
+def permuted(block, axis, source):
     count = lax.axis_size(axis)
-    return lax.ppermute(block, axis, [((i - distance) % count, i) for i in range(count)])
+    return lax.ppermute(block, axis, [(source(i) % count, i) for i in range(count)])
 
 
 def exchange(columns, edge_rows):
-    west = shifted(columns, "tx", 1)
-    east = shifted(columns, "tx", -1)
     if lax.axis_size("ty") <= 2:
-        both = shifted(edge_rows, "ty", 1)
+        both = permuted(edge_rows, "ty", lambda i: i - 1)
     else:
-        south = shifted(edge_rows[0], "ty", 1)
-        north = shifted(edge_rows[1], "ty", -1)
+        south = permuted(edge_rows[0], "ty", lambda i: i - 1)
+        north = permuted(edge_rows[1], "ty", lambda i: i + 1)
         both = jnp.stack([south, north])
+    west = permuted(columns, "tx", lambda i: i - 1)
+    east = permuted(columns, "tx", lambda i: i + 1)
     return west, east, both
 
 
 def local(pressure, east_wind, north_wind, vertical_wind, sound_squared, thickness, owner_map):
     members, levels, rows, cols = pressure.shape
-    ranks = lax.axis_size("mem")
-    tiles = lax.axis_size("ty") * lax.axis_size("tx")
+    ranks, height_count, width = (lax.axis_size(a) for a in ("mem", "ty", "tx"))
     height = rows // ranks
-    mib = 1024 * 1024
     plane = (members, rows, cols)
+    many = (members, levels, rows, cols)
+    field = (levels, rows, cols)
+    lines = (2, members, levels + 1, cols)
+    part = (6, height, cols)
     columns, edge_rows = call(
-        pack_kernel, [plane, (2, members, levels + 1, cols)], [VMEM] * 3, limit=16 * mib
+        pack_kernel,
+        [plane, lines],
+        [HBM] * 3,
+        [
+            pltpu.VMEM(many, jnp.float32),
+            pltpu.VMEM(many, jnp.float32),
+            pltpu.VMEM((members, levels, 8, cols), jnp.float32),
+            pltpu.SemaphoreType.DMA((members, 3)),
+        ],
+        limit=60,
     )(pressure, east_wind, north_wind)
     west, east, both = exchange(columns, edge_rows)
-    field = pltpu.VMEM((levels, rows, cols), jnp.float32)
-    many = pltpu.VMEM((members, levels, rows, cols), jnp.float32)
-    sums, columns, edge_rows, hcols, hrows = call(
+    hcols, hrows, *weights = call(
+        weight_kernel,
+        [(rows, cols), (2, levels, cols)] + [field] * 9 + [many, vertical_wind.shape],
+        [VMEM, HBM, HBM, SMEM],
+        [pltpu.SemaphoreType.DMA((2,))],
+        limit=24,
+    )(sound_squared, north_wind, vertical_wind, thickness)
+    *weights, north_wind, vertical_wind = weights
+    sums, columns, edge_rows = call(
         main_kernel,
-        [
-            (members, 3, rows, cols),
-            plane,
-            (2, members, levels + 1, cols),
-            (rows, cols),
-            (2, levels, cols),
-        ],
-        [VMEM] * 5 + [SMEM] + [VMEM] * 3,
-        [field] * 9 + [many] * 4,
-        limit=32 * mib,
+        [(members, 3, rows, cols), plane, lines],
+        [VMEM] * 5 + [SMEM] + [VMEM] * 12,
+        [pltpu.VMEM(many, jnp.float32)] * 4,
+        limit=32,
     )(
-        pressure, east_wind, north_wind, vertical_wind, sound_squared, thickness, west, east, both
+        pressure, east_wind, north_wind, vertical_wind, sound_squared, thickness, *weights, west, east, both
     )
     west, east, both = exchange(columns, edge_rows)
-    (integrals,) = call(
-        edge_kernel, [(ranks, members, 3, height, cols)], [VMEM] * 6, limit=16 * mib
+    quarters = call(
+        edge_kernel,
+        [(members, 3, height, cols)] * ranks,
+        [VMEM] * 6,
+        [pltpu.VMEM((members, 3, rows, cols), jnp.float32)],
     )(sums, west, east, both, hcols, hrows)
-    gathered = lax.all_to_all(integrals, "mem", 0, 0)
-    (slots,) = call(stats_kernel, [(tiles, 6, height, cols)], [VMEM], limit=16 * mib)(gathered)
-    routed = lax.all_to_all(slots, ("ty", "tx"), 0, 0)
-    me = lax.axis_index(("ty", "tx")).astype(jnp.int32).reshape(1)
+    quarters = [
+        permuted(x, "mem", lambda i, d=d: i ^ d) if d else x for d, x in enumerate(quarters)
+    ]
+    (stats,) = call(stats_kernel, [part], [VMEM] * ranks)(*quarters)
+    tiles = [permuted(stats, "ty", lambda i, j=j: i ^ j) if j else stats for j in range(height_count)]
+    chosen = call(
+        functools.partial(select_kernel, width), [part] * width, [SMEM] + [VMEM] * height_count
+    )(owner_map, *tiles)
+    routed = [permuted(x, "tx", lambda i, d=d: i ^ d) if d else x for d, x in enumerate(chosen)]
     (result,) = call(
-        pick_kernel, [(1, 1, 6, height, cols)], [SMEM, SMEM, VMEM], limit=16 * mib
-    )(owner_map, me, routed)
+        functools.partial(pick_kernel, height_count), [(1, 1) + part], [SMEM] + [VMEM] * width
+    )(owner_map, *routed)
     return result
 
 

time: 67.7 us -> 45.2 us (0.67)
  Pallas kernels: 23.7 us -> 12.8 us
  blocking collectives: 6.98 us -> 0 us
  local copies, waits for them, and re-layouts: 6.87 us -> 0.03 us
  waiting for transfers between devices: 12.5 us -> 14.9 us
    pallas_call x5 -> x7, Pallas kernels: 23.7 us -> 12.8 us  [the longest x1 5.44 us: local(): call(main_kernel, [(members, 3, rows, cols), plane, lines], [VMEM] * 5 +...]
    ppermute x6 -> x13, waiting for transfers between devices: 4.03 us -> 14.9 us  [permuted(): lax.ppermute(block, axis, [(source(i) % count, i) for i in range(count)])]
    all_to_all x1 -> x0, waiting for transfers between devices: 8.46 us -> none  [local(): routed = lax.all_to_all(slots, ('ty', 'tx'), 0, 0)]
    all_to_all x1 -> x0, blocking collectives: 6.98 us -> none  [local(): gathered = lax.all_to_all(integrals, 'mem', 0, 0)]
    unnamed x20 -> x14, local copies, waits for them, and re-layouts: 6.87 us -> 0.03 us
    ppermute x6 -> x13, starting transfers between devices: 11.2 us -> 17.2 us  [permuted(): lax.ppermute(block, axis, [(source(i) % count, i) for i in range(count)])]
    all_to_all x1 -> x0, starting transfers between devices: 6.05 us -> none  [local(): routed = lax.all_to_all(slots, ('ty', 'tx'), 0, 0)]
  transfers between devices with their start and end apart: 7 -> 13, of which waited for: 3 -> 8; matrix products, arithmetic and copies ran while one was open for 0% -> 0% of each run, Pallas kernels for 0% -> 5%
where the time goes in v2:
time: 45.2 us; the launch traced here: 45 us
  starting transfers between devices  17.2 us (38%)
  waiting for transfers between devices  14.9 us (33%)
  Pallas kernels  12.8 us (28%)
    ppermute x13, starting transfers between devices, permuted(): lax.ppermute(block, axis, [(source(i) % count, i) for i in range(count)])  17.2 us
    ppermute x13, waiting for transfers between devices, permuted(): lax.ppermute(block, axis, [(source(i) % count, i) for i in range(count)])  14.9 us
    pallas_call x1, Pallas kernels, local(): call(main_kernel, [(members, 3, rows, cols), plane, lines], [VMEM] * 5 +...  5.44 us
    pallas_call x1, Pallas kernels, local(): call(pack_kernel, [plane, lines], [HBM] * 3, [pltpu.VMEM(many, jnp.float3...  3.08 us
    pallas_call x1, Pallas kernels, local(): call(weight_kernel, [(rows, cols), (2, levels, cols)] + [field] * 9 + [ma...  2.33 us
    pallas_call x1, Pallas kernels, local(): call(functools.partial(pick_kernel, height_count), [(1, 1) + part], [SMEM...  1.17 us
  transfers between devices with their start and end apart: 13, of which 8 were waited for; matrix products, arithmetic and copies ran while one was open for 0% of the time, Pallas kernels for 5%

profile of v2, /device:TPU:0, one launch (start us, length us, event | category | flops | bytes accessed | tf_op | source)
XLA Modules:
  0.0 45.0 jit_solution(14029867107570503047)
XLA Ops:
  0.0 0.0 copy-start
  0.0 0.0 copy-start.5
  0.0 0.0 copy-start.3
  0.0 0.0 copy-start.4
  0.0 3.1 %shard_map.74 = (f32[2,32,128]{2,1,0:T(8,128)}, f32[2,2,51,128]{3,2,1,0:T(8,128)}) custom-call(f32[2,50,32,128]{3,2,1,0:T(8,128)} %p_ref.1, f32[2,50,32,128]{3,2,1,0:T(8,128)} %u_ref.1, f32[2,50,32,128]{3,2,1,0:T(8,128)} %v_hbm.3), custom_call_target="tpu_custom_call" | custom-call | tf_op jit(solution)/shard_map/pallas_call | solution.py:387
  3.1 3.1 %collective-permute-start.2 = (f32[2,2,51,128]{3,2,1,0:T(8,128)}, f32[2,2,51,128]{3,2,1,0:T(8,128)S(1)}, u32[]{:S(2)}, u32[]{:S(2)}) collective-permute-start(f32[2,2,51,128]{3,2,1,0:T(8,128)} %get-tuple-element.43), channel_id=1, source_target_pairs={{4,0},{0,4},{5,1},{1,5},{6,2},{2,6},{7,3},{3,7},{12,8},{8,12},{13,... | collective-permute-start | bytes 313352 | tf_op jit(solution)/shard_map/ppermute | solution.py:363
  6.2 0.0 copy-start.1
  6.2 0.0 copy-start.2
  6.2 3.6 %collective-permute-start.1 = (f32[2,32,128]{2,1,0:T(8,128)}, f32[2,32,128]{2,1,0:T(8,128)S(1)}, u32[]{:S(2)}, u32[]{:S(2)}) collective-permute-start(f32[2,32,128]{2,1,0:T(8,128)} %get-tuple-element.42), channel_id=1, source_target_pairs={{1,0},{2,1},{3,2},{0,3},{5,4},{6,5},{7,6},{4,7},{9,8},{10,9},{11,1... | collective-permute-start | bytes 98312 | tf_op jit(solution)/shard_map/ppermute | solution.py:363
  9.8 0.0 collective-permute-start
  9.8 0.0 copy-done
  9.8 0.0 copy-done.5
  9.8 0.0 copy-done.3
  9.8 0.0 copy-done.4
  9.8 2.3 %shard_map.73 = (f32[32,128]{1,0:T(8,128)S(1)}, f32[2,50,128]{2,1,0:T(8,128)S(1)}, f32[50,32,128]{2,1,0:T(8,128)S(1)}, f32[50,32,128]{2,1,0:T(8,128)S(1)}, f32[5...) custom-call(f32[50,32,128]{2,1,0:T(8,128)S(1)} %copy-done.3, ...), custom_call_target="tpu_custom_call" | custom-call | tf_op jit(solution)/shard_map/pallas_call | solution.py:400
  12.1 0.0 collective-permute-done.1.from_east
  12.2 3.5 %collective-permute-done.from_west = f32[2,32,128]{2,1,0:T(8,128)S(1)} collective-permute-done((f32[2,32,128]{2,1,0:T(8,128)}, f32[2,32,128]{2,1,0:T(8,128)S(1)}, u32[]{:S(2)}, u32[]{:S(2)}) %collective-permute-start) | collective-permute-done | bytes 32800 | tf_op jit(solution)/shard_map/ppermute | solution.py:363
  15.7 0.0 collective-permute-done.2.from_rows
  15.7 0.0 copy-done.1
  15.7 0.0 copy-done.2
  15.7 0.0 copy-start.6
  15.7 5.4 %shard_map.75 = (f32[2,3,32,128]{3,2,1,0:T(8,128)S(1)}, f32[2,32,128]{2,1,0:T(8,128)S(1)}, f32[2,2,51,128]{3,2,1,0:T(8,128)S(1)}) custom-call(f32[2,50,32,128]{3,2,1,0:T(8,128)S(1)} %copy-done.1, f32[2,50,32,128]{3,2,1,0:T(8,128)S(1)} %copy-done.2, f32[2,50,32,128]{3,2,1,0:T(8,128)S(1)} %get-tuple-element.31.v_ref, ...), custom_call_target="tpu_custom_call" | custom-call | tf_op jit(solution)/shard_map/pallas_call | solution.py:408
  21.2 0.6 %collective-permute-start.5 = (f32[2,2,51,128]{3,2,1,0:T(8,128)S(1)}, f32[2,2,51,128]{3,2,1,0:T(8,128)S(1)}, u32[]{:S(2)}, u32[]{:S(2)}) collective-permute-start(f32[2,2,51,128]{3,2,1,0:T(8,128)S(1)} %get-tuple-element.46), channel_id=1, source_target_pairs={{4,0},{0,4},{5,1},{1,5},{6,2},{2,6},{7,3},{3,7},{12,8},{8,12},{13,... | collective-permute-start | bytes 313352 | tf_op jit(solution)/shard_map/ppermute | solution.py:363
  21.7 0.3 collective-permute-start.4
  22.0 1.7 %collective-permute-start.3 = (f32[2,32,128]{2,1,0:T(8,128)S(1)}, f32[2,32,128]{2,1,0:T(8,128)S(1)}, u32[]{:S(2)}, u32[]{:S(2)}) collective-permute-start(f32[2,32,128]{2,1,0:T(8,128)S(1)} %get-tuple-element.45), channel_id=1, source_target_pairs={{3,0},{0,1},{1,2},{2,3},{7,4},{4,5},{5,6},{6,7},{11,8},{8,9},{9,10... | collective-permute-start | bytes 98312 | tf_op jit(solution)/shard_map/ppermute | solution.py:363
  23.8 1.9 %collective-permute-done.4.from_east = f32[2,32,128]{2,1,0:T(8,128)S(1)} collective-permute-done((f32[2,32,128]{2,1,0:T(8,128)S(1)}, f32[2,32,128]{2,1,0:T(8,128)S(1)}, u32[]{:S(2)}, u32[]{:S(2)}) %collective-permute-start.4) | collective-permute-done | bytes 32800 | tf_op jit(solution)/shard_map/ppermute | solution.py:363
  25.7 2.1 %collective-permute-done.3.from_west = f32[2,32,128]{2,1,0:T(8,128)S(1)} collective-permute-done((f32[2,32,128]{2,1,0:T(8,128)S(1)}, f32[2,32,128]{2,1,0:T(8,128)S(1)}, u32[]{:S(2)}, u32[]{:S(2)}) %collective-permute-start.3) | collective-permute-done | bytes 32800 | tf_op jit(solution)/shard_map/ppermute | solution.py:363
  27.7 0.0 collective-permute-done.5.from_rows
  27.8 0.2 shard_map.76
  27.9 0.1 collective-permute-start.6
  28.0 1.6 %collective-permute-start.7 = (f32[2,3,8,128]{3,2,1,0:T(8,128)S(1)}, f32[2,3,8,128]{3,2,1,0:T(8,128)S(1)}, u32[]{:S(2)}, u32[]{:S(2)}) collective-permute-start(f32[2,3,8,128]{3,2,1,0:T(8,128)S(1)} %get-tuple-element.51), channel_id=1, source_target_pairs={{16,0},{24,8},{0,16},{8,24},{17,1},{25,9},{1,17},{9,25},{18,2},{26... | collective-permute-start | bytes 73736 | tf_op jit(solution)/shard_map/ppermute | solution.py:363
  29.6 0.3 collective-permute-start.8
  29.9 0.0 collective-permute-done.6.refs_1_
  29.9 2.0 %collective-permute-done.7.refs_2_ = f32[2,3,8,128]{3,2,1,0:T(8,128)S(1)} collective-permute-done((f32[2,3,8,128]{3,2,1,0:T(8,128)S(1)}, f32[2,3,8,128]{3,2,1,0:T(8,128)S(1)}, u32[]{:S(2)}, u32[]{:S(2)}) %collective-permute-start.7) | collective-permute-done | bytes 24608 | tf_op jit(solution)/shard_map/ppermute | solution.py:363
  31.9 0.9 %collective-permute-done.8.refs_3_ = f32[2,3,8,128]{3,2,1,0:T(8,128)S(1)} collective-permute-done((f32[2,3,8,128]{3,2,1,0:T(8,128)S(1)}, f32[2,3,8,128]{3,2,1,0:T(8,128)S(1)}, u32[]{:S(2)}, u32[]{:S(2)}) %collective-permute-start.8) | collective-permute-done | bytes 24608 | tf_op jit(solution)/shard_map/ppermute | solution.py:363
  32.9 1.6 %collective-permute-start.9 = (f32[6,8,128]{2,1,0:T(8,128)S(1)}, f32[6,8,128]{2,1,0:T(8,128)S(1)}, u32[]{:S(2)}, u32[]{:S(2)}) collective-permute-start(f32[6,8,128]{2,1,0:T(8,128)S(1)} %shard_map.77.refs_0_), channel_id=1, source_target_pairs={{4,0},{0,4},{5,1},{1,5},{6,2},{2,6},{7,3},{3,7},{12,8},{8,12},{13,... | collective-permute-start | bytes 73736 | tf_op jit(solution)/shard_map/ppermute | solution.py:363
  34.4 2.3 %collective-permute-done.9.refs_1_ = f32[6,8,128]{2,1,0:T(8,128)S(1)} collective-permute-done((f32[6,8,128]{2,1,0:T(8,128)S(1)}, f32[6,8,128]{2,1,0:T(8,128)S(1)}, u32[]{:S(2)}, u32[]{:S(2)}) %collective-permute-start.9) | collective-permute-done | bytes 24608 | tf_op jit(solution)/shard_map/ppermute | solution.py:363
  36.8 0.0 copy-done.6
  36.8 0.6 %shard_map.78 = (f32[6,8,128]{2,1,0:T(8,128)S(1)}, f32[6,8,128]{2,1,0:T(8,128)S(1)}, f32[6,8,128]{2,1,0:T(8,128)S(1)}, f32[6,8,128]{2,1,0:T(8,128)S(1)}) custom-call(s32[8]{0:T(128)S(1)} %copy-done.6, f32[6,8,128]{2,1,0:T(8,128)S(1)} %shard_map.77.refs_0_, f32[6,8,128]{2,1,0:T(8,128)S(1)} %collective-permute-done.9.refs_1_), custom_call_target="tpu_custom_call" | custom-call | tf_op jit(solution)/shard_map/pallas_call | solution.py:429
  37.3 0.1 collective-permute-start.10
  37.4 0.6 %collective-permute-start.11 = (f32[6,8,128]{2,1,0:T(8,128)S(1)}, f32[6,8,128]{2,1,0:T(8,128)S(1)}, u32[]{:S(2)}, u32[]{:S(2)}) collective-permute-start(f32[6,8,128]{2,1,0:T(8,128)S(1)} %get-tuple-element.55), channel_id=1, source_target_pairs={{2,0},{3,1},{0,2},{1,3},{6,4},{7,5},{4,6},{5,7},{10,8},{11,9},{8,1... | collective-permute-start | bytes 73736 | tf_op jit(solution)/shard_map/ppermute | solution.py:363
  38.0 3.8 %collective-permute-start.12 = (f32[6,8,128]{2,1,0:T(8,128)S(1)}, f32[6,8,128]{2,1,0:T(8,128)S(1)}, u32[]{:S(2)}, u32[]{:S(2)}) collective-permute-start(f32[6,8,128]{2,1,0:T(8,128)S(1)} %get-tuple-element.56), channel_id=1, source_target_pairs={{3,0},{2,1},{1,2},{0,3},{7,4},{6,5},{5,6},{4,7},{11,8},{10,9},{9,1... | collective-permute-start | bytes 73736 | tf_op jit(solution)/shard_map/ppermute | solution.py:363
  41.8 0.0 collective-permute-done.10.refs_1_
  41.8 0.4 collective-permute-done.11.refs_2_
  42.2 1.6 %collective-permute-done.12.refs_3_ = f32[6,8,128]{2,1,0:T(8,128)S(1)} collective-permute-done((f32[6,8,128]{2,1,0:T(8,128)S(1)}, f32[6,8,128]{2,1,0:T(8,128)S(1)}, u32[]{:S(2)}, u32[]{:S(2)}) %collective-permute-start.12) | collective-permute-done | bytes 24608 | tf_op jit(solution)/shard_map/ppermute | solution.py:363
  43.8 1.2 %shard_map.79 = f32[1,1,6,8,128]{4,3,2,1,0:T(8,128)} custom-call(s32[8]{0:T(128)S(1)} %copy-done.6, f32[6,8,128]{2,1,0:T(8,128)S(1)} %get-tuple-element.53.refs_0_, f32[6,8,128]{2,1,0:T(8,128)S(1)} %collective-permute-done.10.refs_1_, f32[6,8,128]{2,1,0:T(8,128)S(1)} %collective-permute-done.11.refs_2_, f32[6,8,128]{2,1,0:T(8,128)S(1)} %collective-permute-done.12.refs_3_), custom_call_target="tpu_custom_call" | custom-call | tf_op jit(solution)/shard_map/pallas_call | solution.py:433
  (1 shorter events, 0.0 us)
Async XLA Ops:
  0.0 9.8 %copy-start = (f32[2,50,32,128]{3,2,1,0:T(8,128)S(1)}, f32[2,50,32,128]{3,2,1,0:T(8,128)}, u32[]{:S(2)}) copy-start(f32[2,50,32,128]{3,2,1,0:T(8,128)} %v_hbm.3) | copy-start | bytes 4915204
  0.0 9.8 %copy-start.5 = (f32[50]{0:T(128)S(1)}, f32[50]{0:T(128)}, u32[]{:S(2)}) copy-start(f32[50]{0:T(128)} %th_ref.3) | copy-start | bytes 604
  0.0 9.8 %copy-start.3 = (f32[50,32,128]{2,1,0:T(8,128)S(1)}, f32[50,32,128]{2,1,0:T(8,128)}, u32[]{:S(2)}) copy-start(f32[50,32,128]{2,1,0:T(8,128)} %c_ref.3) | copy-start | bytes 2457604
  0.0 9.8 %copy-start.4 = (f32[2,49,32,128]{3,2,1,0:T(8,128)S(1)}, f32[2,49,32,128]{3,2,1,0:T(8,128)}, u32[]{:S(2)}) copy-start(f32[2,49,32,128]{3,2,1,0:T(8,128)} %w_hbm.1) | copy-start | bytes 4816900
  3.1 12.6 %collective-permute-start.2 = (f32[2,2,51,128]{3,2,1,0:T(8,128)}, f32[2,2,51,128]{3,2,1,0:T(8,128)S(1)}, u32[]{:S(2)}, u32[]{:S(2)}) collective-permute-start(f32[2,2,51,128]{3,2,1,0:T(8,128)} %get-tuple-element.43), channel_id=1, source_target_pairs={{4,0},{0,4},{5,1},{1,5},{6,2},{2,6},{7,3},{3,7},{12,8},{8,12},{13,... | collective-permute-start | bytes 313352 | tf_op jit(solution)/shard_map/ppermute | solution.py:363
  6.2 9.5 %copy-start.1 = (f32[2,50,32,128]{3,2,1,0:T(8,128)S(1)}, f32[2,50,32,128]{3,2,1,0:T(8,128)}, u32[]{:S(2)}) copy-start(f32[2,50,32,128]{3,2,1,0:T(8,128)} %p_ref.1) | copy-start | bytes 4915204
  6.2 9.5 %copy-start.2 = (f32[2,50,32,128]{3,2,1,0:T(8,128)S(1)}, f32[2,50,32,128]{3,2,1,0:T(8,128)}, u32[]{:S(2)}) copy-start(f32[2,50,32,128]{3,2,1,0:T(8,128)} %u_ref.1) | copy-start | bytes 4915204
  6.2 6.0 %collective-permute-start.1 = (f32[2,32,128]{2,1,0:T(8,128)}, f32[2,32,128]{2,1,0:T(8,128)S(1)}, u32[]{:S(2)}, u32[]{:S(2)}) collective-permute-start(f32[2,32,128]{2,1,0:T(8,128)} %get-tuple-element.42), channel_id=1, source_target_pairs={{1,0},{2,1},{3,2},{0,3},{5,4},{6,5},{7,6},{4,7},{9,8},{10,9},{11,1... | collective-permute-start | bytes 98312 | tf_op jit(solution)/shard_map/ppermute | solution.py:363
  9.8 5.9 %collective-permute-start = (f32[2,32,128]{2,1,0:T(8,128)}, f32[2,32,128]{2,1,0:T(8,128)S(1)}, u32[]{:S(2)}, u32[]{:S(2)}) collective-permute-start(f32[2,32,128]{2,1,0:T(8,128)} %get-tuple-element.42), channel_id=1, source_target_pairs={{3,0},{0,1},{1,2},{2,3},{7,4},{4,5},{5,6},{6,7},{11,8},{8,9},{9,10... | collective-permute-start | bytes 98312 | tf_op jit(solution)/shard_map/ppermute | solution.py:363
  15.7 21.1 %copy-start.6 = (s32[8]{0:T(128)S(1)}, s32[8]{0:T(128)}, u32[]{:S(2)}) copy-start(s32[8]{0:T(128)} %owner_ref.3) | copy-start | bytes 100
  21.2 6.6 %collective-permute-start.5 = (f32[2,2,51,128]{3,2,1,0:T(8,128)S(1)}, f32[2,2,51,128]{3,2,1,0:T(8,128)S(1)}, u32[]{:S(2)}, u32[]{:S(2)}) collective-permute-start(f32[2,2,51,128]{3,2,1,0:T(8,128)S(1)} %get-tuple-element.46), channel_id=1, source_target_pairs={{4,0},{0,4},{5,1},{1,5},{6,2},{2,6},{7,3},{3,7},{12,8},{8,12},{13,... | collective-permute-start | bytes 313352 | tf_op jit(solution)/shard_map/ppermute | solution.py:363
  21.7 3.9 %collective-permute-start.4 = (f32[2,32,128]{2,1,0:T(8,128)S(1)}, f32[2,32,128]{2,1,0:T(8,128)S(1)}, u32[]{:S(2)}, u32[]{:S(2)}) collective-permute-start(f32[2,32,128]{2,1,0:T(8,128)S(1)} %get-tuple-element.45), channel_id=1, source_target_pairs={{1,0},{2,1},{3,2},{0,3},{5,4},{6,5},{7,6},{4,7},{9,8},{10,9},{11,1... | collective-permute-start | bytes 98312 | tf_op jit(solution)/shard_map/ppermute | solution.py:363
  22.0 5.7 %collective-permute-start.3 = (f32[2,32,128]{2,1,0:T(8,128)S(1)}, f32[2,32,128]{2,1,0:T(8,128)S(1)}, u32[]{:S(2)}, u32[]{:S(2)}) collective-permute-start(f32[2,32,128]{2,1,0:T(8,128)S(1)} %get-tuple-element.45), channel_id=1, source_target_pairs={{3,0},{0,1},{1,2},{2,3},{7,4},{4,5},{5,6},{6,7},{11,8},{8,9},{9,10... | collective-permute-start | bytes 98312 | tf_op jit(solution)/shard_map/ppermute | solution.py:363
  27.9 1.9 %collective-permute-start.6 = (f32[2,3,8,128]{3,2,1,0:T(8,128)S(1)}, f32[2,3,8,128]{3,2,1,0:T(8,128)S(1)}, u32[]{:S(2)}, u32[]{:S(2)}) collective-permute-start(f32[2,3,8,128]{3,2,1,0:T(8,128)S(1)} %get-tuple-element.50), channel_id=1, source_target_pairs={{8,0},{0,8},{24,16},{16,24},{9,1},{1,9},{25,17},{17,25},{10,2},{2,... | collective-permute-start | bytes 73736 | tf_op jit(solution)/shard_map/ppermute | solution.py:363
  28.0 3.9 %collective-permute-start.7 = (f32[2,3,8,128]{3,2,1,0:T(8,128)S(1)}, f32[2,3,8,128]{3,2,1,0:T(8,128)S(1)}, u32[]{:S(2)}, u32[]{:S(2)}) collective-permute-start(f32[2,3,8,128]{3,2,1,0:T(8,128)S(1)} %get-tuple-element.51), channel_id=1, source_target_pairs={{16,0},{24,8},{0,16},{8,24},{17,1},{25,9},{1,17},{9,25},{18,2},{26... | collective-permute-start | bytes 73736 | tf_op jit(solution)/shard_map/ppermute | solution.py:363
  29.6 3.3 %collective-permute-start.8 = (f32[2,3,8,128]{3,2,1,0:T(8,128)S(1)}, f32[2,3,8,128]{3,2,1,0:T(8,128)S(1)}, u32[]{:S(2)}, u32[]{:S(2)}) collective-permute-start(f32[2,3,8,128]{3,2,1,0:T(8,128)S(1)} %get-tuple-element.52), channel_id=1, source_target_pairs={{24,0},{16,8},{8,16},{0,24},{25,1},{17,9},{9,17},{1,25},{26,2},{18... | collective-permute-start | bytes 73736 | tf_op jit(solution)/shard_map/ppermute | solution.py:363
  32.9 3.9 %collective-permute-start.9 = (f32[6,8,128]{2,1,0:T(8,128)S(1)}, f32[6,8,128]{2,1,0:T(8,128)S(1)}, u32[]{:S(2)}, u32[]{:S(2)}) collective-permute-start(f32[6,8,128]{2,1,0:T(8,128)S(1)} %shard_map.77.refs_0_), channel_id=1, source_target_pairs={{4,0},{0,4},{5,1},{1,5},{6,2},{2,6},{7,3},{3,7},{12,8},{8,12},{13,... | collective-permute-start | bytes 73736 | tf_op jit(solution)/shard_map/ppermute | solution.py:363
  37.3 4.5 %collective-permute-start.10 = (f32[6,8,128]{2,1,0:T(8,128)S(1)}, f32[6,8,128]{2,1,0:T(8,128)S(1)}, u32[]{:S(2)}, u32[]{:S(2)}) collective-permute-start(f32[6,8,128]{2,1,0:T(8,128)S(1)} %get-tuple-element.54), channel_id=1, source_target_pairs={{1,0},{0,1},{3,2},{2,3},{5,4},{4,5},{7,6},{6,7},{9,8},{8,9},{11,10... | collective-permute-start | bytes 73736 | tf_op jit(solution)/shard_map/ppermute | solution.py:363
  37.4 4.8 %collective-permute-start.11 = (f32[6,8,128]{2,1,0:T(8,128)S(1)}, f32[6,8,128]{2,1,0:T(8,128)S(1)}, u32[]{:S(2)}, u32[]{:S(2)}) collective-permute-start(f32[6,8,128]{2,1,0:T(8,128)S(1)} %get-tuple-element.55), channel_id=1, source_target_pairs={{2,0},{3,1},{0,2},{1,3},{6,4},{7,5},{4,6},{5,7},{10,8},{11,9},{8,1... | collective-permute-start | bytes 73736 | tf_op jit(solution)/shard_map/ppermute | solution.py:363
  38.0 5.9 %collective-permute-start.12 = (f32[6,8,128]{2,1,0:T(8,128)S(1)}, f32[6,8,128]{2,1,0:T(8,128)S(1)}, u32[]{:S(2)}, u32[]{:S(2)}) collective-permute-start(f32[6,8,128]{2,1,0:T(8,128)S(1)} %get-tuple-element.56), channel_id=1, source_target_pairs={{3,0},{2,1},{1,2},{0,3},{7,4},{6,5},{5,6},{4,7},{11,8},{10,9},{9,1... | collective-permute-start | bytes 73736 | tf_op jit(solution)/shard_map/ppermute | solution.py:363

commit v3 on v2

v3 whole, which is shorter than its diff:
```python
import functools

import jax
import jax.numpy as jnp
from jax import lax
from jax.experimental import pallas as pl
from jax.experimental.pallas import tpu as pltpu
from jax.sharding import PartitionSpec as P


HORIZ = 0.35
VERT = 1.5
STEP_A = 50
STEP_P = 10
STEP_B = 25
STEP_S = 25
PACK_LIMIT = 16
PREP_LIMIT = 24

VMEM = pl.BlockSpec(memory_space=pltpu.VMEM)
SMEM = pl.BlockSpec(memory_space=pltpu.SMEM)
HBM = pl.BlockSpec(memory_space=pltpu.HBM)


def divisor(count, most):
    return max(d for d in range(1, most + 1) if count % d == 0)


def lanes_of(shape):
    return lax.broadcasted_iota(jnp.int32, shape, len(shape) - 1)


def rows_of(shape):
    return lax.broadcasted_iota(jnp.int32, shape, len(shape) - 2)


def west_roll(x):
    return pltpu.roll(x, 1, 1)


def east_roll(x):
    return pltpu.roll(x, x.shape[1] - 1, 1)


def south_roll(x):
    return pltpu.roll(x, 1, 0)


def north_roll(x):
    return pltpu.roll(x, x.shape[0] - 1, 0)


def sides(far_ref, near_ref):
    odd = lax.axis_index("tx") % 2 == 1
    far = [far_ref[m] for m in range(far_ref.shape[0])]
    near = [near_ref[m] for m in range(near_ref.shape[0])]
    west = [jnp.where(odd, a, b) for a, b in zip(near, far)]
    east = [jnp.where(odd, b, a) for a, b in zip(near, far)]
    return west, east


def pack_kernel(p_hbm, u_hbm, v_hbm, cols_ref, rows_ref, p_ref, u_ref, v_s, sems):
    members, levels, rows, cols = p_ref.shape
    copies = []
    for m in range(members):
        pair = [
            pltpu.make_async_copy(p_hbm.at[m], p_ref.at[m], sems.at[m, 0]),
            pltpu.make_async_copy(u_hbm.at[m], u_ref.at[m], sems.at[m, 1]),
            pltpu.make_async_copy(v_hbm.at[m, :, 0:8], v_s.at[m], sems.at[m, 2]),
        ]
        for copy in pair:
            copy.start()
        copies.append(pair)
    lane = lanes_of((rows, cols))
    for m in range(members):
        for copy in copies[m]:
            copy.wait()
        packed = jnp.zeros((rows, cols), jnp.float32)
        for k in range(levels):
            p = p_ref[m, k]
            z = u_ref[m, k] - HORIZ * p
            edge = pltpu.roll(jnp.where(lane == cols - 1, p, z), 2 * k + 1, 1)
            packed = jnp.where(lane >= 2 * k, edge, packed)
            rows_ref[0, m, k : k + 1, :] = p[rows - 1 : rows, :]
            rows_ref[1, m, k : k + 1, :] = v_s[m, k, 0:1, :] - HORIZ * p[0:1, :]
        cols_ref[m] = packed


def prepare_kernel(
    c_ref, p_ref, u0_ref, v_hbm, w_hbm, th_ref, owner_ref,
    hcols_ref, hrows_ref, hth_ref, masks_ref,
    e_s, inv_s, s_s, g_s, h_s, hw_s, he_s, hs_s, hn_s, part_ref, u_ref, v_ref, w_ref, sems,
):
    members, levels, rows, cols = part_ref.shape
    copies = [
        pltpu.make_async_copy(source.at[m], target.at[m], sems.at[i, m])
        for i, (source, target) in enumerate([(v_hbm, v_ref), (w_hbm, w_ref)])
        for m in range(members)
    ]
    for copy in copies:
        copy.start()
    inner = levels - 1
    shape = (rows, cols)
    lane = lanes_of(shape)
    row = rows_of(shape)
    first_lane, last_lane = lane == 0, lane == cols - 1
    first_row, last_row = row == 0, row == rows - 1
    zero = jnp.zeros(shape, jnp.float32)
    vsq = VERT * VERT

    height, width = lax.axis_size("ty"), lax.axis_size("tx")
    my_row, my_column = lax.axis_index("ty"), lax.axis_index("tx")
    mask = (8, cols)
    for j in range(height):
        for d in range(width):
            here = owner_ref[(my_row ^ j) * width + my_column] == my_row * width + (my_column ^ d)
            masks_ref[j * width + d] = jnp.full(mask, jnp.where(here, 1.0, 0.0), jnp.float32)
    for d in range(width):
        here = jnp.float32(0.0)
        for j in range(height):
            mine = owner_ref[j * width + (my_column ^ d)] == my_row * width + my_column
            here = jnp.where(mine, 1.0, here)
        masks_ref[height * width + d] = jnp.full(mask, here, jnp.float32)

    for ref in (e_s, inv_s, s_s):
        ref[0] = zero

    step = divisor(inner, STEP_A)

    def factor(chunk, carry):
        e_prev, s_prev, c_here = carry
        for sub in range(step):
            i = chunk * step + sub
            c_next = c_ref[i + 1]
            b_next = vsq * c_next
            pivot = (1.0 + b_next) + (vsq * c_here) * (1.0 - e_prev)
            inv = 1.0 / pivot
            s_prev = VERT * (th_ref[i + 1] * c_next - th_ref[i] * c_here) + e_prev * s_prev
            e_prev = b_next * inv
            e_s[i + 1] = e_prev
            inv_s[i + 1] = inv
            s_s[i + 1] = s_prev * inv
            c_here = c_next
        return e_prev, s_prev, c_here

    lax.fori_loop(0, inner // step, factor, (zero, zero, c_ref[0]))

    def weights(k, y_above, y_here):
        g = th_ref[k] + VERT * (y_above - y_here)
        h = g * (HORIZ * c_ref[k])
        g_s[k] = g - (2 * HORIZ) * h
        h_s[k] = h
        h35 = HORIZ * h
        hw_s[k] = jnp.where(first_lane, 0.0, west_roll(h))
        he_s[k] = jnp.where(last_lane, 0.0, east_roll(h35))
        hs_s[k] = jnp.where(first_row, 0.0, south_roll(h))
        hn_s[k] = jnp.where(last_row, 0.0, north_roll(h35))
        hrows_ref[0, pl.ds(k, 1), :] = h35[0:1, :]
        hrows_ref[1, pl.ds(k, 1), :] = h[rows - 1 : rows, :]
        hrows_ref[2, pl.ds(k, 1), :] = jnp.full((1, cols), HORIZ * th_ref[k], jnp.float32)
        return jnp.where(last_lane, -h, h35)

    def adjoint(chunk, carry):
        y_above, packed = carry
        packed = pltpu.roll(packed, 2 * step, 1)
        for sub in range(step):
            i = inner - 1 - (chunk * step + sub)
            y_here = s_s[i + 1] + e_s[i + 1] * y_above
            s_s[i + 1] = y_here
            edge = weights(i + 1, y_above, y_here)
            place = 2 * (step - 1 - sub)
            packed = jnp.where(lane < place + 2, pltpu.roll(edge, place + 1, 1), packed)
            y_above = y_here
        return y_above, packed

    y_low, packed = lax.fori_loop(0, inner // step, adjoint, (zero, zero))
    edge = weights(0, y_low, zero)
    hcols_ref[...] = jnp.where(lane < 2, pltpu.roll(edge, 1, 1), pltpu.roll(packed, 2, 1))
    hth = jnp.zeros(mask, jnp.float32)
    for k in range(levels):
        hth = jnp.where(lanes_of(mask) == 2 * k + 1, HORIZ * th_ref[k], hth)
    hth_ref[...] = hth

    for copy in copies[:members]:
        copy.wait()
    step1 = divisor(levels, STEP_P)

    def first_winds(chunk, carry):
        for sub in range(step1):
            k = chunk * step1 + sub
            c35 = HORIZ * c_ref[k]
            for m in range(members):
                p = p_ref[m, k]
                q = HORIZ * p
                zu = u0_ref[m, k] - q
                zv = v_ref[m, k] - q
                u1 = zu + jnp.where(first_lane, 0.0, west_roll(q))
                v1 = zv + jnp.where(first_row, 0.0, south_roll(q))
                u_ref[m, k] = u1
                v_ref[m, k] = v1
                zu_east = jnp.where(last_lane, 0.0, east_roll(zu))
                zv_north = jnp.where(last_row, 0.0, north_roll(zv))
                div = ((zu_east + q) - u1) + ((zv_north + q) - v1)
                part_ref[m, k] = p - c35 * div
        return carry

    lax.fori_loop(0, levels // step1, first_winds, 0)
    for copy in copies[members:]:
        copy.wait()


def solve_kernel(
    c_ref, part_ref, u_ref, v_ref, w_ref, e_s, inv_s, far_ref, near_ref, from_rows,
    cols_ref, rows_ref, p1_ref, zu_ref, zv_ref, w1_ref,
):
    members, levels, rows, cols = part_ref.shape
    group = 8
    groups = rows // group
    gshape = (group, cols)
    slices = [slice(g * group, (g + 1) * group) for g in range(groups)]
    lane, row = lanes_of(gshape), rows_of(gshape)
    zero = jnp.zeros(gshape, jnp.float32)
    at_first = jnp.where(lane == 0, 1.0, 0.0)
    signed = jnp.where(lane == cols - 1, -1.0, at_first)
    even = lane % 2 == 0
    from_west, from_east = sides(far_ref, near_ref)
    halo = []
    for m in range(members):
        for rs in slices:
            mixed = jnp.where(even, east_roll(from_east[m][rs]), HORIZ * west_roll(from_west[m][rs]))
            halo.append(east_roll(mixed))
    step1 = divisor(levels, STEP_B)

    def upward(chunk, carry):
        part_prev, v_prev, halo = (list(x) for x in carry)
        for sub in range(step1):
            k = chunk * step1 + sub
            below = jnp.maximum(k - 1, 0)
            for g, rs in enumerate(slices):
                c35 = HORIZ * c_ref[k, rs]
                e = e_s[below, rs]
                for m in range(members):
                    at = m * groups + g
                    edge = halo[at] if sub == 0 else pltpu.roll(halo[at], cols - 2 * sub, 1)
                    zu_ref[m, k, rs] = u_ref[m, k, rs] + edge * at_first
                    delta = edge * signed
                    if g == 0:
                        delta = delta + jnp.where(row == 0, HORIZ * from_rows[0, m, pl.ds(k, 1), :], 0.0)
                    if g == groups - 1:
                        delta = delta - jnp.where(row == group - 1, from_rows[1, m, pl.ds(k, 1), :], 0.0)
                    part = part_ref[m, k, rs] + c35 * delta
                    p1_ref[m, k, rs] = part
                    rhs = w_ref[m, below, rs] - VERT * (part - part_prev[at])
                    v_new = rhs + e * v_prev[at]
                    w1_ref[m, k, rs] = v_new
                    v_prev[at] = v_new
                    part_prev[at] = part
        halo = [pltpu.roll(x, cols - 2 * step1, 1) for x in halo]
        return tuple(part_prev), tuple(v_prev), tuple(halo)

    zeros = (zero,) * (members * groups)
    lax.fori_loop(0, levels // step1, upward, (zeros, zeros, tuple(halo)))

    last = lane == cols - 1
    for g, rs in enumerate(slices):

        def downward(chunk, carry, g=g, rs=rs):
            ws, packs = list(carry[0]), list(carry[1])
            base = levels - step1 - chunk * step1
            for sub in range(step1):
                k = base + (step1 - 1 - sub)
                inv, e = inv_s[k, rs], e_s[k, rs]
                c15 = VERT * c_ref[k, rs]
                for m in range(members):
                    w = ws[m]
                    w_low = w1_ref[m, k, rs] * inv + e * w
                    w1_ref[m, k, rs] = w_low
                    p = p1_ref[m, k, rs] - c15 * (w - w_low)
                    p1_ref[m, k, rs] = p
                    q = HORIZ * p
                    zu = zu_ref[m, k, rs] - q
                    zu_ref[m, k, rs] = zu
                    v1 = v_ref[m, k, rs]
                    if g == 0:
                        v1 = v1 + jnp.where(row == 0, HORIZ * from_rows[0, m, pl.ds(k, 1), :], 0.0)
                    zv = v1 - q
                    zv_ref[m, k, rs] = zv
                    place = 2 * (step1 - 1 - sub)
                    edge = pltpu.roll(jnp.where(last, p, zu), place + 1, 1)
                    if sub == 0:
                        packs[m] = pltpu.roll(packs[m], 2 * step1, 1)
                    packs[m] = jnp.where(lane < place + 2, edge, packs[m])
                    if g == groups - 1:
                        rows_ref[0, m, pl.ds(k, 1), :] = p[group - 1 : group, :]
                    if g == 0:
                        rows_ref[1, m, pl.ds(k, 1), :] = zv[0:1, :]
                    ws[m] = w_low
            return tuple(ws), tuple(packs)

        init = ((zero,) * members,) * 2
        _, packs = lax.fori_loop(0, levels // step1, downward, init)
        for m in range(members):
            cols_ref[m, rs] = packs[m]


def sum_kernel(
    p1_ref, zu_ref, zv_ref, w1_ref, th_ref, s_s, g_s, h_s, hw_s, he_s, hs_s, hn_s, sums_ref, keep_s
):
    members, levels, rows, cols = p1_ref.shape
    group = 8
    gshape = (group, cols)
    glane = lanes_of(gshape)
    gzero = jnp.zeros(gshape, jnp.float32)
    step1 = divisor(levels, STEP_S)
    for r in range(rows // group):
        rs = slice(r * group, (r + 1) * group)

        def downward(chunk, carry, rs=rs):
            state = [list(x) for x in carry]
            base = levels - step1 - chunk * step1
            for sub in range(step1):
                k = base + (step1 - 1 - sub)
                g, h, th = g_s[k, rs], h_s[k, rs], th_ref[k]
                y = s_s[k, rs]
                hw, he, hs, hn = hw_s[k, rs], he_s[k, rs], hs_s[k, rs], hn_s[k, rs]
                for m in range(members):
                    mass, ps, us, vs, ce, cw, cn, cs = state[m]
                    p, zu, zv = p1_ref[m, k, rs], zu_ref[m, k, rs], zv_ref[m, k, rs]
                    mass = mass + ((g * p + y * w1_ref[m, k, rs]) + h * (zu + zv))
                    ps = ps + th * p
                    us = us + th * zu
                    vs = vs + th * zv
                    ce = ce + hw * zu
                    cw = cw + he * p
                    cn = cn + hs * zv
                    cs = cs + hn * p
                    state[m] = [mass, ps, us, vs, ce, cw, cn, cs]
            return tuple(tuple(x) for x in state)

        out = lax.fori_loop(0, levels // step1, downward, ((gzero,) * 8,) * members)
        for m in range(members):
            mass, ps, us, vs, ce, cw, cn, cs = out[m]
            sums_ref[m, 0, rs] = mass - east_roll(ce) + west_roll(cw)
            sums_ref[m, 1, rs] = us + jnp.where(glane == 0, 0.0, HORIZ * west_roll(ps))
            sums_ref[m, 2, rs] = vs
            keep_s[m, 0, rs] = ps
            keep_s[m, 1, rs] = cn
            keep_s[m, 2, rs] = cs
    row = rows_of((rows, cols))
    for m in range(members):
        ps, cn, cs = keep_s[m, 0], keep_s[m, 1], keep_s[m, 2]
        sums_ref[m, 0] = sums_ref[m, 0] - north_roll(cn) + south_roll(cs)
        sums_ref[m, 2] = sums_ref[m, 2] + jnp.where(row == 0, 0.0, HORIZ * south_roll(ps))


def edge_kernel(sums_ref, far_ref, near_ref, from_rows, hcols_ref, hrows_ref, hth_ref, *rest):
    outs, total_s = rest[:-1], rest[-1]
    from_west, from_east = sides(far_ref, near_ref)
    members, _, rows, cols = sums_ref.shape
    levels = hrows_ref.shape[1]
    height = rows // len(outs)
    mine = lax.axis_index("mem")
    lane = lanes_of((rows, cols))
    row = rows_of((rows, cols))
    even = lane % 2 == 0
    used = lane < 2 * levels
    hth = jnp.concatenate([hth_ref[...]] * (rows // 8), axis=0)
    for m in range(members):
        west = west_roll(from_west[m])
        products = jnp.where(used, hcols_ref[...] * jnp.where(even, east_roll(from_east[m]), west), 0.0)
        at_east = jnp.sum(jnp.where(even, products, 0.0), axis=1, keepdims=True)
        at_west = jnp.sum(jnp.where(even, 0.0, products), axis=1, keepdims=True)
        u_west = jnp.sum(hth * west, axis=1, keepdims=True)
        at_south = jnp.sum(hrows_ref[0] * from_rows[0, m], axis=0, keepdims=True)
        at_north = jnp.sum(hrows_ref[1] * from_rows[1, m], axis=0, keepdims=True)
        v_south = jnp.sum(hrows_ref[2] * from_rows[0, m], axis=0, keepdims=True)
        mass = sums_ref[m, 0] + jnp.where(lane == 0, at_west, 0.0) + jnp.where(lane == cols - 1, at_east, 0.0)
        mass = mass + jnp.where(row == 0, at_south, 0.0) - jnp.where(row == rows - 1, at_north, 0.0)
        total_s[m, 0] = mass
        total_s[m, 1] = sums_ref[m, 1] + jnp.where(lane == 0, u_west, 0.0)
        total_s[m, 2] = sums_ref[m, 2] + jnp.where(row == 0, v_south, 0.0)
    for d, out_ref in enumerate(outs):
        start = pl.multiple_of((mine ^ d) * height, height)
        out_ref[...] = total_s[:, :, pl.ds(start, height), :]


def stats_kernel(*refs):
    ins, out_ref = refs[:-1], refs[-1]
    members, fields = ins[0].shape[:2]
    count = len(ins) * members
    for f in range(fields):
        values = [ref[m, f] for ref in ins for m in range(members)]
        mean = functools.reduce(jnp.add, values) / count
        square = functools.reduce(jnp.add, [(v - mean) * (v - mean) for v in values]) / (count - 1)
        out_ref[f] = mean
        out_ref[fields + f] = square


def select_kernel(width, masks_ref, *refs):
    tiles, outs = refs[:-width], refs[-width:]
    for d, out_ref in enumerate(outs):
        for f in range(out_ref.shape[0]):
            value = tiles[0][f]
            for j in range(1, len(tiles)):
                value = jnp.where(masks_ref[j * width + d] > 0.5, tiles[j][f], value)
            out_ref[f] = value


def pick_kernel(masks_ref, *refs):
    ins, out_ref = refs[:-1], refs[-1]
    width = len(ins)
    base = masks_ref.shape[0] - width
    for f in range(ins[0].shape[0]):
        value = ins[0][f]
        for d in range(1, width):
            value = jnp.where(masks_ref[base + d] > 0.5, ins[d][f], value)
        out_ref[0, 0, f] = value


def call(kernel, outs, in_specs, scratch=(), limit=16):
    return pl.pallas_call(
        kernel,
        out_shape=[jax.ShapeDtypeStruct(s, jnp.float32) for s in outs],
        in_specs=in_specs,
        out_specs=[VMEM] * len(outs),
        scratch_shapes=list(scratch),
        compiler_params=pltpu.CompilerParams(vmem_limit_bytes=limit * 1024 * 1024),
    )


def permuted(block, axis, source):
    count = lax.axis_size(axis)
    return lax.ppermute(block, axis, [(source(i) % count, i) for i in range(count)])


def exchange(columns, edge_rows):
    far = permuted(columns, "tx", lambda i: i + 1 if i % 2 else i - 1)
    near = permuted(columns, "tx", lambda i: i ^ 1)
    if lax.axis_size("ty") <= 2:
        both = permuted(edge_rows, "ty", lambda i: i - 1)
    else:
        south = permuted(edge_rows[0], "ty", lambda i: i - 1)
        north = permuted(edge_rows[1], "ty", lambda i: i + 1)
        both = jnp.stack([south, north])
    return far, near, both


def steps(pressure, east_wind, north_wind, vertical_wind, sound_squared, thickness, owner_map):
    members, levels, rows, cols = pressure.shape
    ranks, height_count, width = (lax.axis_size(a) for a in ("mem", "ty", "tx"))
    height = rows // ranks
    plane = (members, rows, cols)
    many = (members, levels, rows, cols)
    field = (levels, rows, cols)
    lines = (2, members, levels, cols)
    part = (6, height, cols)
    pressure, east_wind, north_wind, vertical_wind = (
        pltpu.with_memory_space_constraint(x, pltpu.HBM)
        for x in (pressure, east_wind, north_wind, vertical_wind)
    )
    columns, edge_rows, p0, u0 = call(
        pack_kernel,
        [plane, lines, many, many],
        [HBM] * 3,
        [
            pltpu.VMEM((members, levels, 8, cols), jnp.float32),
            pltpu.SemaphoreType.DMA((members, 3)),
        ],
        limit=PACK_LIMIT,
    )(pressure, east_wind, north_wind)
    far, near, both = exchange(columns, edge_rows)
    hcols, hrows, hth, masks, e, inv, *weights, part0, u0, v0, w0 = call(
        prepare_kernel,
        [
            (rows, cols),
            (3, levels, cols),
            (8, cols),
            (height_count * width + width, 8, cols),
            *[field] * 9,
            *[many] * 3,
            vertical_wind.shape,
        ],
        [VMEM, VMEM, VMEM, HBM, HBM, SMEM, SMEM],
        [pltpu.SemaphoreType.DMA((2, members))],
        limit=PREP_LIMIT,
    )(sound_squared, p0, u0, north_wind, vertical_wind, thickness, owner_map)
    columns, edge_rows, p1, zu, zv, w1 = call(
        solve_kernel, [plane, lines, *[many] * 4], [VMEM] * 10
    )(sound_squared, part0, u0, v0, w0, e, inv, far, near, both)
    far, near, both = exchange(columns, edge_rows)
    (sums,) = call(
        sum_kernel,
        [(members, 3, rows, cols)],
        [VMEM] * 4 + [SMEM] + [VMEM] * 7,
        [pltpu.VMEM((members, 3, rows, cols), jnp.float32)],
    )(p1, zu, zv, w1, thickness, *weights)
    quarters = call(
        edge_kernel,
        [(members, 3, height, cols)] * ranks,
        [VMEM] * 7,
        [pltpu.VMEM((members, 3, rows, cols), jnp.float32)],
    )(sums, far, near, both, hcols, hrows, hth)
    quarters = [
        permuted(x, "mem", lambda i, d=d: i ^ d) if d else x for d, x in enumerate(quarters)
    ]
    (stats,) = call(stats_kernel, [part], [VMEM] * ranks)(*quarters)
    tiles = [
        permuted(stats, "ty", lambda i, j=j: i ^ j) if j else stats
        for j in range(height_count)
    ]
    chosen = call(
        functools.partial(select_kernel, width), [part] * width, [VMEM] * (1 + height_count)
    )(masks, *tiles)
    routed = [permuted(x, "tx", lambda i, d=d: i ^ d) if d else x for d, x in enumerate(chosen)]
    (result,) = call(pick_kernel, [(1, 1) + part], [VMEM] * (1 + width))(masks, *routed)
    return result


def solution(mesh):
    placed = (
        P("mem", None, "ty", "tx"),
        P("mem", None, "ty", "tx"),
        P("mem", None, "ty", "tx"),
        P("mem", None, "ty", "tx"),
        P(None, "ty", "tx"),
        P(),
        P(),
    )
    return jax.shard_map(
        steps,
        mesh=mesh,
        in_specs=placed,
        out_specs=P("ty", "tx", None, "mem", None),
        check_vma=False,
    )
```

time: 45.2 us -> 41.3 us (0.914)
  waiting for transfers between devices: 14.9 us -> 10.3 us
  Pallas kernels: 12.8 us -> 13.5 us
    ppermute x13, waiting for transfers between devices: 14.9 us -> 10.3 us  [permuted(): lax.ppermute(block, axis, [(source(i) % count, i) for i in range(count)])]
    pallas_call x7 -> x8, Pallas kernels: 12.8 us -> 13.5 us  [the longest x1 4.92 us: steps(): call(prepare_kernel, [(rows, cols), (3, levels, cols), (8, cols), (height...]
  transfers between devices with their start and end apart: 13 -> 13, of which waited for: 8 -> 7; matrix products, arithmetic and copies ran while one was open for 0% -> 0% of each run, Pallas kernels for 5% -> 18%
where the time goes in v3:
time: 41.3 us; the launch traced here: 41.2 us
  starting transfers between devices  17.2 us (42%)
  Pallas kernels  13.5 us (33%)
  waiting for transfers between devices  10.3 us (25%)
    ppermute x13, starting transfers between devices, permuted(): lax.ppermute(block, axis, [(source(i) % count, i) for i in range(count)])  17.2 us
    ppermute x13, waiting for transfers between devices, permuted(): lax.ppermute(block, axis, [(source(i) % count, i) for i in range(count)])  10.3 us
    pallas_call x1, Pallas kernels, steps(): call(prepare_kernel, [(rows, cols), (3, levels, cols), (8, cols), (height...  4.92 us
    pallas_call x1, Pallas kernels, steps(): call(solve_kernel, [plane, lines, *[many] * 4], [VMEM] * 10)  2.92 us
    pallas_call x1, Pallas kernels, steps(): call(sum_kernel, [(members, 3, rows, cols)], [VMEM] * 4 + [SMEM] + [VMEM]...  2.44 us
    pallas_call x1, Pallas kernels, steps(): call(pack_kernel, [plane, lines, many, many], [HBM] * 3, [pltpu.VMEM((mem...  2.4 us
  transfers between devices with their start and end apart: 13, of which 7 were waited for; matrix products, arithmetic and copies ran while one was open for 0% of the time, Pallas kernels for 18%

profile of v3, /device:TPU:0, one launch (start us, length us, event | category | flops | bytes accessed | tf_op | source)
XLA Modules:
  0.0 41.2 jit_solution(13322513507415936780)
XLA Ops:
  0.0 0.0 copy-start.1
  0.0 0.0 copy-start
  0.0 0.0 copy-start.2
  0.0 2.4 %shard_map.73 = (f32[2,32,128]{2,1,0:T(8,128)S(1)}, f32[2,2,50,128]{3,2,1,0:T(8,128)S(1)}, f32[2,50,32,128]{3,2,1,0:T(8,128)S(1)}, f32[2,50,32,128]{3,2,1,0:T(8,128)S(1)}) custom-call(f32[2,50,32,128]{3,2,1,0:T(8,128)} %p_hbm.1, f32[2,50,32,128]{3,2,1,0:T(8,128)} %u_hbm.1, f32[2,50,32,128]{3,2,1,0:T(8,128)} %v_hbm.3), custom_call_target="tpu_custom_call" | custom-call | tf_op jit(solution)/shard_map/pallas_call | solution.py:461
  2.4 3.1 %collective-permute-start.2 = (f32[2,2,50,128]{3,2,1,0:T(8,128)S(1)}, f32[2,2,50,128]{3,2,1,0:T(8,128)S(1)}, u32[]{:S(2)}, u32[]{:S(2)}) collective-permute-start(f32[2,2,50,128]{3,2,1,0:T(8,128)S(1)} %get-tuple-element.50), channel_id=1, source_target_pairs={{4,0},{0,4},{5,1},{1,5},{6,2},{2,6},{7,3},{3,7},{12,8},{8,12},{13,... | collective-permute-start | bytes 307208 | tf_op jit(solution)/shard_map/ppermute | solution.py:433
  5.5 1.6 %collective-permute-start.1 = (f32[2,32,128]{2,1,0:T(8,128)S(1)}, f32[2,32,128]{2,1,0:T(8,128)S(1)}, u32[]{:S(2)}, u32[]{:S(2)}) collective-permute-start(f32[2,32,128]{2,1,0:T(8,128)S(1)} %get-tuple-element.49), channel_id=1, source_target_pairs={{1,0},{0,1},{3,2},{2,3},{5,4},{4,5},{7,6},{6,7},{9,8},{8,9},{11,10... | collective-permute-start | bytes 98312 | tf_op jit(solution)/shard_map/ppermute | solution.py:433
  7.1 2.5 %collective-permute-start = (f32[2,32,128]{2,1,0:T(8,128)S(1)}, f32[2,32,128]{2,1,0:T(8,128)S(1)}, u32[]{:S(2)}, u32[]{:S(2)}) collective-permute-start(f32[2,32,128]{2,1,0:T(8,128)S(1)} %get-tuple-element.49), channel_id=1, source_target_pairs={{3,0},{2,1},{1,2},{0,3},{7,4},{6,5},{5,6},{4,7},{11,8},{10,9},{9,1... | collective-permute-start | bytes 98312 | tf_op jit(solution)/shard_map/ppermute | solution.py:433
  9.5 0.0 copy-done.1
  9.5 0.0 copy-done
  9.5 0.0 copy-done.2
  9.5 4.9 %shard_map.74 = (f32[32,128]{1,0:T(8,128)S(1)}, f32[3,50,128]{2,1,0:T(8,128)S(1)}, f32[8,128]{1,0:T(8,128)S(1)}, f32[12,8,128]{2,1,0:T(8,128)S(1)}, f32[50,32,12...) custom-call(f32[50,32,128]{2,1,0:T(8,128)S(1)} %copy-done, ...), custom_call_target="tpu_custom_call" | custom-call | tf_op jit(solution)/shard_map/pallas_call | solution.py:472
  14.5 0.0 collective-permute-done.1.near_ref
  14.5 0.0 collective-permute-done.far_ref
  14.5 0.0 collective-permute-done.2.from_rows
  14.5 2.9 %shard_map.75 = (f32[2,32,128]{2,1,0:T(8,128)S(1)}, f32[2,2,50,128]{3,2,1,0:T(8,128)S(1)}, f32[2,50,32,128]{3,2,1,0:T(8,128)S(1)}, f32[2,50,32,128]{3,2,1,0:T(8,...) custom-call(f32[50,32,128]{2,1,0:T(8,128)S(1)} %copy-done, ...), custom_call_target="tpu_custom_call" | custom-call | tf_op jit(solution)/shard_map/pallas_call | solution.py:487
  17.4 0.6 %collective-permute-start.5 = (f32[2,2,50,128]{3,2,1,0:T(8,128)S(1)}, f32[2,2,50,128]{3,2,1,0:T(8,128)S(1)}, u32[]{:S(2)}, u32[]{:S(2)}) collective-permute-start(f32[2,2,50,128]{3,2,1,0:T(8,128)S(1)} %get-tuple-element.63), channel_id=1, source_target_pairs={{4,0},{0,4},{5,1},{1,5},{6,2},{2,6},{7,3},{3,7},{12,8},{8,12},{13,... | collective-permute-start | bytes 307208 | tf_op jit(solution)/shard_map/ppermute | solution.py:433
  18.0 0.7 %collective-permute-start.4 = (f32[2,32,128]{2,1,0:T(8,128)S(1)}, f32[2,32,128]{2,1,0:T(8,128)S(1)}, u32[]{:S(2)}, u32[]{:S(2)}) collective-permute-start(f32[2,32,128]{2,1,0:T(8,128)S(1)} %get-tuple-element.62), channel_id=1, source_target_pairs={{1,0},{0,1},{3,2},{2,3},{5,4},{4,5},{7,6},{6,7},{9,8},{8,9},{11,10... | collective-permute-start | bytes 98312 | tf_op jit(solution)/shard_map/ppermute | solution.py:433
  18.6 0.9 %collective-permute-start.3 = (f32[2,32,128]{2,1,0:T(8,128)S(1)}, f32[2,32,128]{2,1,0:T(8,128)S(1)}, u32[]{:S(2)}, u32[]{:S(2)}) collective-permute-start(f32[2,32,128]{2,1,0:T(8,128)S(1)} %get-tuple-element.62), channel_id=1, source_target_pairs={{3,0},{2,1},{1,2},{0,3},{7,4},{6,5},{5,6},{4,7},{11,8},{10,9},{9,1... | collective-permute-start | bytes 98312 | tf_op jit(solution)/shard_map/ppermute | solution.py:433
  19.6 2.4 %shard_map.76.sums_ref = f32[2,3,32,128]{3,2,1,0:T(8,128)S(1)} custom-call(f32[2,50,32,128]{3,2,1,0:T(8,128)S(1)} %get-tuple-element.51.p1_ref, f32[2,50,32,128]{3,2,1,0:T(8,128)S(1)} %get-tuple-element.52.zu_ref, f32[2,50,32,128]{3,2,1,0:T(8,128)S(1)} %get-tuple-element.53.zv_ref, f32[2,50,32,128]{3,2,1,0:T(8,128)S(1)} %get-tuple-element.54.w1_ref, ...), custom_call_target="tpu_custom_call" | custom-call | tf_op jit(solution)/shard_map/pallas_call | solution.py:491
  22.0 0.2 collective-permute-done.4.near_ref
  22.2 2.2 %collective-permute-done.3.far_ref = f32[2,32,128]{2,1,0:T(8,128)S(1)} collective-permute-done((f32[2,32,128]{2,1,0:T(8,128)S(1)}, f32[2,32,128]{2,1,0:T(8,128)S(1)}, u32[]{:S(2)}, u32[]{:S(2)}) %collective-permute-start.3) | collective-permute-done | bytes 32800 | tf_op jit(solution)/shard_map/ppermute | solution.py:433
  24.4 0.0 collective-permute-done.5.from_rows
  24.4 0.2 shard_map.77
  24.6 0.1 collective-permute-start.6
  24.7 1.6 %collective-permute-start.7 = (f32[2,3,8,128]{3,2,1,0:T(8,128)S(1)}, f32[2,3,8,128]{3,2,1,0:T(8,128)S(1)}, u32[]{:S(2)}, u32[]{:S(2)}) collective-permute-start(f32[2,3,8,128]{3,2,1,0:T(8,128)S(1)} %get-tuple-element.69), channel_id=1, source_target_pairs={{16,0},{24,8},{0,16},{8,24},{17,1},{25,9},{1,17},{9,25},{18,2},{26... | collective-permute-start | bytes 73736 | tf_op jit(solution)/shard_map/ppermute | solution.py:433
  26.2 0.3 collective-permute-start.8
  26.5 0.0 collective-permute-done.6.refs_1_
  26.5 2.0 %collective-permute-done.7.refs_2_ = f32[2,3,8,128]{3,2,1,0:T(8,128)S(1)} collective-permute-done((f32[2,3,8,128]{3,2,1,0:T(8,128)S(1)}, f32[2,3,8,128]{3,2,1,0:T(8,128)S(1)}, u32[]{:S(2)}, u32[]{:S(2)}) %collective-permute-start.7) | collective-permute-done | bytes 24608 | tf_op jit(solution)/shard_map/ppermute | solution.py:433
  28.5 0.9 %collective-permute-done.8.refs_3_ = f32[2,3,8,128]{3,2,1,0:T(8,128)S(1)} collective-permute-done((f32[2,3,8,128]{3,2,1,0:T(8,128)S(1)}, f32[2,3,8,128]{3,2,1,0:T(8,128)S(1)}, u32[]{:S(2)}, u32[]{:S(2)}) %collective-permute-start.8) | collective-permute-done | bytes 24608 | tf_op jit(solution)/shard_map/ppermute | solution.py:433
  29.5 1.6 %collective-permute-start.9 = (f32[6,8,128]{2,1,0:T(8,128)S(1)}, f32[6,8,128]{2,1,0:T(8,128)S(1)}, u32[]{:S(2)}, u32[]{:S(2)}) collective-permute-start(f32[6,8,128]{2,1,0:T(8,128)S(1)} %shard_map.78.refs_0_), channel_id=1, source_target_pairs={{4,0},{0,4},{5,1},{1,5},{6,2},{2,6},{7,3},{3,7},{12,8},{8,12},{13,... | collective-permute-start | bytes 73736 | tf_op jit(solution)/shard_map/ppermute | solution.py:433
  31.1 2.3 %collective-permute-done.9.refs_1_ = f32[6,8,128]{2,1,0:T(8,128)S(1)} collective-permute-done((f32[6,8,128]{2,1,0:T(8,128)S(1)}, f32[6,8,128]{2,1,0:T(8,128)S(1)}, u32[]{:S(2)}, u32[]{:S(2)}) %collective-permute-start.9) | collective-permute-done | bytes 24608 | tf_op jit(solution)/shard_map/ppermute | solution.py:433
  33.4 0.1 collective-permute-start.10
  33.5 1.5 %collective-permute-start.11 = (f32[6,8,128]{2,1,0:T(8,128)S(1)}, f32[6,8,128]{2,1,0:T(8,128)S(1)}, u32[]{:S(2)}, u32[]{:S(2)}) collective-permute-start(f32[6,8,128]{2,1,0:T(8,128)S(1)} %get-tuple-element.73), channel_id=1, source_target_pairs={{2,0},{3,1},{0,2},{1,3},{6,4},{7,5},{4,6},{5,7},{10,8},{11,9},{8,1... | collective-permute-start | bytes 73736 | tf_op jit(solution)/shard_map/ppermute | solution.py:433
  34.9 2.9 %collective-permute-start.12 = (f32[6,8,128]{2,1,0:T(8,128)S(1)}, f32[6,8,128]{2,1,0:T(8,128)S(1)}, u32[]{:S(2)}, u32[]{:S(2)}) collective-permute-start(f32[6,8,128]{2,1,0:T(8,128)S(1)} %get-tuple-element.74), channel_id=1, source_target_pairs={{3,0},{2,1},{1,2},{0,3},{7,4},{6,5},{5,6},{4,7},{11,8},{10,9},{9,1... | collective-permute-start | bytes 73736 | tf_op jit(solution)/shard_map/ppermute | solution.py:433
  37.9 0.0 collective-permute-done.10.refs_1_
  37.9 0.4 %collective-permute-done.11.refs_2_ = f32[6,8,128]{2,1,0:T(8,128)S(1)} collective-permute-done((f32[6,8,128]{2,1,0:T(8,128)S(1)}, f32[6,8,128]{2,1,0:T(8,128)S(1)}, u32[]{:S(2)}, u32[]{:S(2)}) %collective-permute-start.11) | collective-permute-done | bytes 24608 | tf_op jit(solution)/shard_map/ppermute | solution.py:433
  38.3 2.3 %collective-permute-done.12.refs_3_ = f32[6,8,128]{2,1,0:T(8,128)S(1)} collective-permute-done((f32[6,8,128]{2,1,0:T(8,128)S(1)}, f32[6,8,128]{2,1,0:T(8,128)S(1)}, u32[]{:S(2)}, u32[]{:S(2)}) %collective-permute-start.12) | collective-permute-done | bytes 24608 | tf_op jit(solution)/shard_map/ppermute | solution.py:433
  40.6 0.6 %shard_map.80 = f32[1,1,6,8,128]{4,3,2,1,0:T(8,128)} custom-call(f32[12,8,128]{2,1,0:T(8,128)S(1)} %get-tuple-element.42.masks_ref, f32[6,8,128]{2,1,0:T(8,128)S(1)} %get-tuple-element.71.refs_0_, f32[6,8,128]{2,1,0:T(8,128)S(1)} %collective-permute-done.10.refs_1_, f32[6,8,128]{2,1,0:T(8,128)S(1)} %collective-permute-done.11.refs_2_, ...), custom_call_target="tpu_custom_call" | custom-call | tf_op jit(solution)/shard_map/pallas_call | solution.py:515
  (2 shorter events, 0.0 us)
Async XLA Ops:
  0.0 9.5 %copy-start.1 = (f32[50]{0:T(128)S(1)}, f32[50]{0:T(128)}, u32[]{:S(2)}) copy-start(f32[50]{0:T(128)} %th_ref.3) | copy-start | bytes 604
  0.0 9.5 %copy-start = (f32[50,32,128]{2,1,0:T(8,128)S(1)}, f32[50,32,128]{2,1,0:T(8,128)}, u32[]{:S(2)}) copy-start(f32[50,32,128]{2,1,0:T(8,128)} %c_ref.3) | copy-start | bytes 2457604
  0.0 9.5 %copy-start.2 = (s32[8]{0:T(128)S(1)}, s32[8]{0:T(128)}, u32[]{:S(2)}) copy-start(s32[8]{0:T(128)} %owner_ref.1) | copy-start | bytes 100
  2.4 12.1 %collective-permute-start.2 = (f32[2,2,50,128]{3,2,1,0:T(8,128)S(1)}, f32[2,2,50,128]{3,2,1,0:T(8,128)S(1)}, u32[]{:S(2)}, u32[]{:S(2)}) collective-permute-start(f32[2,2,50,128]{3,2,1,0:T(8,128)S(1)} %get-tuple-element.50), channel_id=1, source_target_pairs={{4,0},{0,4},{5,1},{1,5},{6,2},{2,6},{7,3},{3,7},{12,8},{8,12},{13,... | collective-permute-start | bytes 307208 | tf_op jit(solution)/shard_map/ppermute | solution.py:433
  5.5 9.0 %collective-permute-start.1 = (f32[2,32,128]{2,1,0:T(8,128)S(1)}, f32[2,32,128]{2,1,0:T(8,128)S(1)}, u32[]{:S(2)}, u32[]{:S(2)}) collective-permute-start(f32[2,32,128]{2,1,0:T(8,128)S(1)} %get-tuple-element.49), channel_id=1, source_target_pairs={{1,0},{0,1},{3,2},{2,3},{5,4},{4,5},{7,6},{6,7},{9,8},{8,9},{11,10... | collective-permute-start | bytes 98312 | tf_op jit(solution)/shard_map/ppermute | solution.py:433
  7.1 7.4 %collective-permute-start = (f32[2,32,128]{2,1,0:T(8,128)S(1)}, f32[2,32,128]{2,1,0:T(8,128)S(1)}, u32[]{:S(2)}, u32[]{:S(2)}) collective-permute-start(f32[2,32,128]{2,1,0:T(8,128)S(1)} %get-tuple-element.49), channel_id=1, source_target_pairs={{3,0},{2,1},{1,2},{0,3},{7,4},{6,5},{5,6},{4,7},{11,8},{10,9},{9,1... | collective-permute-start | bytes 98312 | tf_op jit(solution)/shard_map/ppermute | solution.py:433
  17.4 6.9 %collective-permute-start.5 = (f32[2,2,50,128]{3,2,1,0:T(8,128)S(1)}, f32[2,2,50,128]{3,2,1,0:T(8,128)S(1)}, u32[]{:S(2)}, u32[]{:S(2)}) collective-permute-start(f32[2,2,50,128]{3,2,1,0:T(8,128)S(1)} %get-tuple-element.63), channel_id=1, source_target_pairs={{4,0},{0,4},{5,1},{1,5},{6,2},{2,6},{7,3},{3,7},{12,8},{8,12},{13,... | collective-permute-start | bytes 307208 | tf_op jit(solution)/shard_map/ppermute | solution.py:433
  18.0 4.2 %collective-permute-start.4 = (f32[2,32,128]{2,1,0:T(8,128)S(1)}, f32[2,32,128]{2,1,0:T(8,128)S(1)}, u32[]{:S(2)}, u32[]{:S(2)}) collective-permute-start(f32[2,32,128]{2,1,0:T(8,128)S(1)} %get-tuple-element.62), channel_id=1, source_target_pairs={{1,0},{0,1},{3,2},{2,3},{5,4},{4,5},{7,6},{6,7},{9,8},{8,9},{11,10... | collective-permute-start | bytes 98312 | tf_op jit(solution)/shard_map/ppermute | solution.py:433
  18.6 5.7 %collective-permute-start.3 = (f32[2,32,128]{2,1,0:T(8,128)S(1)}, f32[2,32,128]{2,1,0:T(8,128)S(1)}, u32[]{:S(2)}, u32[]{:S(2)}) collective-permute-start(f32[2,32,128]{2,1,0:T(8,128)S(1)} %get-tuple-element.62), channel_id=1, source_target_pairs={{3,0},{2,1},{1,2},{0,3},{7,4},{6,5},{5,6},{4,7},{11,8},{10,9},{9,1... | collective-permute-start | bytes 98312 | tf_op jit(solution)/shard_map/ppermute | solution.py:433
  24.6 1.9 %collective-permute-start.6 = (f32[2,3,8,128]{3,2,1,0:T(8,128)S(1)}, f32[2,3,8,128]{3,2,1,0:T(8,128)S(1)}, u32[]{:S(2)}, u32[]{:S(2)}) collective-permute-start(f32[2,3,8,128]{3,2,1,0:T(8,128)S(1)} %get-tuple-element.68), channel_id=1, source_target_pairs={{8,0},{0,8},{24,16},{16,24},{9,1},{1,9},{25,17},{17,25},{10,2},{2,... | collective-permute-start | bytes 73736 | tf_op jit(solution)/shard_map/ppermute | solution.py:433
  24.7 3.9 %collective-permute-start.7 = (f32[2,3,8,128]{3,2,1,0:T(8,128)S(1)}, f32[2,3,8,128]{3,2,1,0:T(8,128)S(1)}, u32[]{:S(2)}, u32[]{:S(2)}) collective-permute-start(f32[2,3,8,128]{3,2,1,0:T(8,128)S(1)} %get-tuple-element.69), channel_id=1, source_target_pairs={{16,0},{24,8},{0,16},{8,24},{17,1},{25,9},{1,17},{9,25},{18,2},{26... | collective-permute-start | bytes 73736 | tf_op jit(solution)/shard_map/ppermute | solution.py:433
  26.2 3.3 %collective-permute-start.8 = (f32[2,3,8,128]{3,2,1,0:T(8,128)S(1)}, f32[2,3,8,128]{3,2,1,0:T(8,128)S(1)}, u32[]{:S(2)}, u32[]{:S(2)}) collective-permute-start(f32[2,3,8,128]{3,2,1,0:T(8,128)S(1)} %get-tuple-element.70), channel_id=1, source_target_pairs={{24,0},{16,8},{8,16},{0,24},{25,1},{17,9},{9,17},{1,25},{26,2},{18... | collective-permute-start | bytes 73736 | tf_op jit(solution)/shard_map/ppermute | solution.py:433
  29.5 3.9 %collective-permute-start.9 = (f32[6,8,128]{2,1,0:T(8,128)S(1)}, f32[6,8,128]{2,1,0:T(8,128)S(1)}, u32[]{:S(2)}, u32[]{:S(2)}) collective-permute-start(f32[6,8,128]{2,1,0:T(8,128)S(1)} %shard_map.78.refs_0_), channel_id=1, source_target_pairs={{4,0},{0,4},{5,1},{1,5},{6,2},{2,6},{7,3},{3,7},{12,8},{8,12},{13,... | collective-permute-start | bytes 73736 | tf_op jit(solution)/shard_map/ppermute | solution.py:433
  33.4 4.5 %collective-permute-start.10 = (f32[6,8,128]{2,1,0:T(8,128)S(1)}, f32[6,8,128]{2,1,0:T(8,128)S(1)}, u32[]{:S(2)}, u32[]{:S(2)}) collective-permute-start(f32[6,8,128]{2,1,0:T(8,128)S(1)} %get-tuple-element.72), channel_id=1, source_target_pairs={{1,0},{0,1},{3,2},{2,3},{5,4},{4,5},{7,6},{6,7},{9,8},{8,9},{11,10... | collective-permute-start | bytes 73736 | tf_op jit(solution)/shard_map/ppermute | solution.py:433
  33.5 4.8 %collective-permute-start.11 = (f32[6,8,128]{2,1,0:T(8,128)S(1)}, f32[6,8,128]{2,1,0:T(8,128)S(1)}, u32[]{:S(2)}, u32[]{:S(2)}) collective-permute-start(f32[6,8,128]{2,1,0:T(8,128)S(1)} %get-tuple-element.73), channel_id=1, source_target_pairs={{2,0},{3,1},{0,2},{1,3},{6,4},{7,5},{4,6},{5,7},{10,8},{11,9},{8,1... | collective-permute-start | bytes 73736 | tf_op jit(solution)/shard_map/ppermute | solution.py:433
  34.9 5.6 %collective-permute-start.12 = (f32[6,8,128]{2,1,0:T(8,128)S(1)}, f32[6,8,128]{2,1,0:T(8,128)S(1)}, u32[]{:S(2)}, u32[]{:S(2)}) collective-permute-start(f32[6,8,128]{2,1,0:T(8,128)S(1)} %get-tuple-element.74), channel_id=1, source_target_pairs={{3,0},{2,1},{1,2},{0,3},{7,4},{6,5},{5,6},{4,7},{11,8},{10,9},{9,1... | collective-permute-start | bytes 73736 | tf_op jit(solution)/shard_map/ppermute | solution.py:433

commit v4 on v3

--- a/solution.py
+++ b/solution.py
@@ -10,9 +10,10 @@
 
 HORIZ = 0.35
 VERT = 1.5
-STEP_A = 50
+STEP_A = 8
 STEP_P = 10
 STEP_B = 25
+STEP_D = 25
 STEP_S = 25
 PACK_LIMIT = 16
 PREP_LIMIT = 24
@@ -262,17 +263,19 @@
     lax.fori_loop(0, levels // step1, upward, (zeros, zeros, tuple(halo)))
 
     last = lane == cols - 1
-    for g, rs in enumerate(slices):
-
-        def downward(chunk, carry, g=g, rs=rs):
-            ws, packs = list(carry[0]), list(carry[1])
-            base = levels - step1 - chunk * step1
-            for sub in range(step1):
-                k = base + (step1 - 1 - sub)
+
+    def downward(chunk, carry):
+        ws, packs = list(carry[0]), list(carry[1])
+        base = levels - step2 - chunk * step2
+        for sub in range(step2):
+            place = 2 * (step2 - 1 - sub)
+            k = base + (step2 - 1 - sub)
+            for g, rs in enumerate(slices):
                 inv, e = inv_s[k, rs], e_s[k, rs]
                 c15 = VERT * c_ref[k, rs]
                 for m in range(members):
-                    w = ws[m]
+                    at = m * groups + g
+                    w = ws[at]
                     w_low = w1_ref[m, k, rs] * inv + e * w
                     w1_ref[m, k, rs] = w_low
                     p = p1_ref[m, k, rs] - c15 * (w - w_low)
@@ -285,22 +288,22 @@
                         v1 = v1 + jnp.where(row == 0, HORIZ * from_rows[0, m, pl.ds(k, 1), :], 0.0)
                     zv = v1 - q
                     zv_ref[m, k, rs] = zv
-                    place = 2 * (step1 - 1 - sub)
                     edge = pltpu.roll(jnp.where(last, p, zu), place + 1, 1)
                     if sub == 0:
-                        packs[m] = pltpu.roll(packs[m], 2 * step1, 1)
-                    packs[m] = jnp.where(lane < place + 2, edge, packs[m])
+                        packs[at] = pltpu.roll(packs[at], 2 * step2, 1)
+                    packs[at] = jnp.where(lane < place + 2, edge, packs[at])
                     if g == groups - 1:
                         rows_ref[0, m, pl.ds(k, 1), :] = p[group - 1 : group, :]
                     if g == 0:
                         rows_ref[1, m, pl.ds(k, 1), :] = zv[0:1, :]
-                    ws[m] = w_low
-            return tuple(ws), tuple(packs)
-
-        init = ((zero,) * members,) * 2
-        _, packs = lax.fori_loop(0, levels // step1, downward, init)
-        for m in range(members):
-            cols_ref[m, rs] = packs[m]
+                    ws[at] = w_low
+        return tuple(ws), tuple(packs)
+
+    step2 = divisor(levels, STEP_D)
+    _, packs = lax.fori_loop(0, levels // step2, downward, (zeros, zeros))
+    for m in range(members):
+        for g, rs in enumerate(slices):
+            cols_ref[m, rs] = packs[m * groups + g]
 
 
 def sum_kernel(

time: 41.3 us -> 39.5 us (0.956)
  Pallas kernels: 13.5 us -> 11.6 us
    pallas_call x1, Pallas kernels: 2.92 us -> 1.88 us  [steps(): call(solve_kernel, [plane, lines, *[many] * 4], [VMEM] * 10)]
    pallas_call x1, Pallas kernels: 4.92 us -> 3.98 us  [steps(): call(prepare_kernel, [(rows, cols), (3, levels, cols), (8, cols), (height...]
  transfers between devices with their start and end apart: 13 -> 13, of which waited for: 7 -> 7; matrix products, arithmetic and copies ran while one was open for 0% -> 0% of each run, Pallas kernels for 18% -> 16%
where the time goes in v4:
time: 39.5 us; the launch traced here: 39.3 us
  starting transfers between devices  17.3 us (44%)
  Pallas kernels  11.6 us (29%)
  waiting for transfers between devices  10.4 us (26%)
    ppermute x13, starting transfers between devices, permuted(): lax.ppermute(block, axis, [(source(i) % count, i) for i in range(count)])  17.3 us
    ppermute x13, waiting for transfers between devices, permuted(): lax.ppermute(block, axis, [(source(i) % count, i) for i in range(count)])  10.4 us
    pallas_call x1, Pallas kernels, steps(): call(prepare_kernel, [(rows, cols), (3, levels, cols), (8, cols), (height...  3.98 us
    pallas_call x1, Pallas kernels, steps(): call(sum_kernel, [(members, 3, rows, cols)], [VMEM] * 4 + [SMEM] + [VMEM]...  2.44 us
    pallas_call x1, Pallas kernels, steps(): call(pack_kernel, [plane, lines, many, many], [HBM] * 3, [pltpu.VMEM((mem...  2.4 us
    pallas_call x1, Pallas kernels, steps(): call(solve_kernel, [plane, lines, *[many] * 4], [VMEM] * 10)  1.88 us
  transfers between devices with their start and end apart: 13, of which 7 were waited for; matrix products, arithmetic and copies ran while one was open for 0% of the time, Pallas kernels for 16%

profile of v4, /device:TPU:0, one launch (start us, length us, event | category | flops | bytes accessed | tf_op | source)
XLA Modules:
  0.0 39.3 jit_solution(16360330428910039847)
XLA Ops:
  0.0 0.0 copy-start.1
  0.0 0.0 copy-start
  0.0 0.0 copy-start.2
  0.0 2.4 %shard_map.73 = (f32[2,32,128]{2,1,0:T(8,128)S(1)}, f32[2,2,50,128]{3,2,1,0:T(8,128)S(1)}, f32[2,50,32,128]{3,2,1,0:T(8,128)S(1)}, f32[2,50,32,128]{3,2,1,0:T(8,128)S(1)}) custom-call(f32[2,50,32,128]{3,2,1,0:T(8,128)} %p_hbm.1, f32[2,50,32,128]{3,2,1,0:T(8,128)} %u_hbm.1, f32[2,50,32,128]{3,2,1,0:T(8,128)} %v_hbm.3), custom_call_target="tpu_custom_call" | custom-call | tf_op jit(solution)/shard_map/pallas_call | solution.py:464
  2.4 3.1 %collective-permute-start.2 = (f32[2,2,50,128]{3,2,1,0:T(8,128)S(1)}, f32[2,2,50,128]{3,2,1,0:T(8,128)S(1)}, u32[]{:S(2)}, u32[]{:S(2)}) collective-permute-start(f32[2,2,50,128]{3,2,1,0:T(8,128)S(1)} %get-tuple-element.50), channel_id=1, source_target_pairs={{4,0},{0,4},{5,1},{1,5},{6,2},{2,6},{7,3},{3,7},{12,8},{8,12},{13,... | collective-permute-start | bytes 307208 | tf_op jit(solution)/shard_map/ppermute | solution.py:436
  5.5 1.6 %collective-permute-start.1 = (f32[2,32,128]{2,1,0:T(8,128)S(1)}, f32[2,32,128]{2,1,0:T(8,128)S(1)}, u32[]{:S(2)}, u32[]{:S(2)}) collective-permute-start(f32[2,32,128]{2,1,0:T(8,128)S(1)} %get-tuple-element.49), channel_id=1, source_target_pairs={{1,0},{0,1},{3,2},{2,3},{5,4},{4,5},{7,6},{6,7},{9,8},{8,9},{11,10... | collective-permute-start | bytes 98312 | tf_op jit(solution)/shard_map/ppermute | solution.py:436
  7.1 2.5 %collective-permute-start = (f32[2,32,128]{2,1,0:T(8,128)S(1)}, f32[2,32,128]{2,1,0:T(8,128)S(1)}, u32[]{:S(2)}, u32[]{:S(2)}) collective-permute-start(f32[2,32,128]{2,1,0:T(8,128)S(1)} %get-tuple-element.49), channel_id=1, source_target_pairs={{3,0},{2,1},{1,2},{0,3},{7,4},{6,5},{5,6},{4,7},{11,8},{10,9},{9,1... | collective-permute-start | bytes 98312 | tf_op jit(solution)/shard_map/ppermute | solution.py:436
  9.5 0.0 copy-done.1
  9.5 0.0 copy-done
  9.5 0.0 copy-done.2
  9.5 4.0 %shard_map.74 = (f32[32,128]{1,0:T(8,128)S(1)}, f32[3,50,128]{2,1,0:T(8,128)S(1)}, f32[8,128]{1,0:T(8,128)S(1)}, f32[12,8,128]{2,1,0:T(8,128)S(1)}, f32[50,32,12...) custom-call(f32[50,32,128]{2,1,0:T(8,128)S(1)} %copy-done, ...), custom_call_target="tpu_custom_call" | custom-call | tf_op jit(solution)/shard_map/pallas_call | solution.py:475
  13.5 0.0 collective-permute-done.1.near_ref
  13.5 0.0 collective-permute-done.far_ref
  13.6 0.0 collective-permute-done.2.from_rows
  13.6 1.9 %shard_map.75 = (f32[2,32,128]{2,1,0:T(8,128)S(1)}, f32[2,2,50,128]{3,2,1,0:T(8,128)S(1)}, f32[2,50,32,128]{3,2,1,0:T(8,128)S(1)}, f32[2,50,32,128]{3,2,1,0:T(8,...) custom-call(f32[50,32,128]{2,1,0:T(8,128)S(1)} %copy-done, ...), custom_call_target="tpu_custom_call" | custom-call | tf_op jit(solution)/shard_map/pallas_call | solution.py:490
  15.5 0.6 %collective-permute-start.5 = (f32[2,2,50,128]{3,2,1,0:T(8,128)S(1)}, f32[2,2,50,128]{3,2,1,0:T(8,128)S(1)}, u32[]{:S(2)}, u32[]{:S(2)}) collective-permute-start(f32[2,2,50,128]{3,2,1,0:T(8,128)S(1)} %get-tuple-element.63), channel_id=1, source_target_pairs={{4,0},{0,4},{5,1},{1,5},{6,2},{2,6},{7,3},{3,7},{12,8},{8,12},{13,... | collective-permute-start | bytes 307208 | tf_op jit(solution)/shard_map/ppermute | solution.py:436
  16.0 0.7 %collective-permute-start.4 = (f32[2,32,128]{2,1,0:T(8,128)S(1)}, f32[2,32,128]{2,1,0:T(8,128)S(1)}, u32[]{:S(2)}, u32[]{:S(2)}) collective-permute-start(f32[2,32,128]{2,1,0:T(8,128)S(1)} %get-tuple-element.62), channel_id=1, source_target_pairs={{1,0},{0,1},{3,2},{2,3},{5,4},{4,5},{7,6},{6,7},{9,8},{8,9},{11,10... | collective-permute-start | bytes 98312 | tf_op jit(solution)/shard_map/ppermute | solution.py:436
  16.7 1.0 %collective-permute-start.3 = (f32[2,32,128]{2,1,0:T(8,128)S(1)}, f32[2,32,128]{2,1,0:T(8,128)S(1)}, u32[]{:S(2)}, u32[]{:S(2)}) collective-permute-start(f32[2,32,128]{2,1,0:T(8,128)S(1)} %get-tuple-element.62), channel_id=1, source_target_pairs={{3,0},{2,1},{1,2},{0,3},{7,4},{6,5},{5,6},{4,7},{11,8},{10,9},{9,1... | collective-permute-start | bytes 98312 | tf_op jit(solution)/shard_map/ppermute | solution.py:436
  17.7 2.4 %shard_map.76.sums_ref = f32[2,3,32,128]{3,2,1,0:T(8,128)S(1)} custom-call(f32[2,50,32,128]{3,2,1,0:T(8,128)S(1)} %get-tuple-element.51.p1_ref, f32[2,50,32,128]{3,2,1,0:T(8,128)S(1)} %get-tuple-element.52.zu_ref, f32[2,50,32,128]{3,2,1,0:T(8,128)S(1)} %get-tuple-element.53.zv_ref, f32[2,50,32,128]{3,2,1,0:T(8,128)S(1)} %get-tuple-element.54.w1_ref, ...), custom_call_target="tpu_custom_call" | custom-call | tf_op jit(solution)/shard_map/pallas_call | solution.py:494
  20.2 0.1 collective-permute-done.4.near_ref
  20.3 2.2 %collective-permute-done.3.far_ref = f32[2,32,128]{2,1,0:T(8,128)S(1)} collective-permute-done((f32[2,32,128]{2,1,0:T(8,128)S(1)}, f32[2,32,128]{2,1,0:T(8,128)S(1)}, u32[]{:S(2)}, u32[]{:S(2)}) %collective-permute-start.3) | collective-permute-done | bytes 32800 | tf_op jit(solution)/shard_map/ppermute | solution.py:436
  22.4 0.0 collective-permute-done.5.from_rows
  22.4 0.2 shard_map.77
  22.6 0.1 collective-permute-start.6
  22.7 1.6 %collective-permute-start.7 = (f32[2,3,8,128]{3,2,1,0:T(8,128)S(1)}, f32[2,3,8,128]{3,2,1,0:T(8,128)S(1)}, u32[]{:S(2)}, u32[]{:S(2)}) collective-permute-start(f32[2,3,8,128]{3,2,1,0:T(8,128)S(1)} %get-tuple-element.69), channel_id=1, source_target_pairs={{16,0},{24,8},{0,16},{8,24},{17,1},{25,9},{1,17},{9,25},{18,2},{26... | collective-permute-start | bytes 73736 | tf_op jit(solution)/shard_map/ppermute | solution.py:436
  24.3 0.3 collective-permute-start.8
  24.6 0.0 collective-permute-done.6.refs_1_
  24.6 2.0 %collective-permute-done.7.refs_2_ = f32[2,3,8,128]{3,2,1,0:T(8,128)S(1)} collective-permute-done((f32[2,3,8,128]{3,2,1,0:T(8,128)S(1)}, f32[2,3,8,128]{3,2,1,0:T(8,128)S(1)}, u32[]{:S(2)}, u32[]{:S(2)}) %collective-permute-start.7) | collective-permute-done | bytes 24608 | tf_op jit(solution)/shard_map/ppermute | solution.py:436
  26.6 0.9 %collective-permute-done.8.refs_3_ = f32[2,3,8,128]{3,2,1,0:T(8,128)S(1)} collective-permute-done((f32[2,3,8,128]{3,2,1,0:T(8,128)S(1)}, f32[2,3,8,128]{3,2,1,0:T(8,128)S(1)}, u32[]{:S(2)}, u32[]{:S(2)}) %collective-permute-start.8) | collective-permute-done | bytes 24608 | tf_op jit(solution)/shard_map/ppermute | solution.py:436
  27.5 1.6 %collective-permute-start.9 = (f32[6,8,128]{2,1,0:T(8,128)S(1)}, f32[6,8,128]{2,1,0:T(8,128)S(1)}, u32[]{:S(2)}, u32[]{:S(2)}) collective-permute-start(f32[6,8,128]{2,1,0:T(8,128)S(1)} %shard_map.78.refs_0_), channel_id=1, source_target_pairs={{4,0},{0,4},{5,1},{1,5},{6,2},{2,6},{7,3},{3,7},{12,8},{8,12},{13,... | collective-permute-start | bytes 73736 | tf_op jit(solution)/shard_map/ppermute | solution.py:436
  29.1 2.3 %collective-permute-done.9.refs_1_ = f32[6,8,128]{2,1,0:T(8,128)S(1)} collective-permute-done((f32[6,8,128]{2,1,0:T(8,128)S(1)}, f32[6,8,128]{2,1,0:T(8,128)S(1)}, u32[]{:S(2)}, u32[]{:S(2)}) %collective-permute-start.9) | collective-permute-done | bytes 24608 | tf_op jit(solution)/shard_map/ppermute | solution.py:436
  31.5 0.1 collective-permute-start.10
  31.5 1.6 %collective-permute-start.11 = (f32[6,8,128]{2,1,0:T(8,128)S(1)}, f32[6,8,128]{2,1,0:T(8,128)S(1)}, u32[]{:S(2)}, u32[]{:S(2)}) collective-permute-start(f32[6,8,128]{2,1,0:T(8,128)S(1)} %get-tuple-element.73), channel_id=1, source_target_pairs={{2,0},{3,1},{0,2},{1,3},{6,4},{7,5},{4,6},{5,7},{10,8},{11,9},{8,1... | collective-permute-start | bytes 73736 | tf_op jit(solution)/shard_map/ppermute | solution.py:436
  33.1 2.8 %collective-permute-start.12 = (f32[6,8,128]{2,1,0:T(8,128)S(1)}, f32[6,8,128]{2,1,0:T(8,128)S(1)}, u32[]{:S(2)}, u32[]{:S(2)}) collective-permute-start(f32[6,8,128]{2,1,0:T(8,128)S(1)} %get-tuple-element.74), channel_id=1, source_target_pairs={{3,0},{2,1},{1,2},{0,3},{7,4},{6,5},{5,6},{4,7},{11,8},{10,9},{9,1... | collective-permute-start | bytes 73736 | tf_op jit(solution)/shard_map/ppermute | solution.py:436
  35.9 0.0 collective-permute-done.10.refs_1_
  35.9 0.6 %collective-permute-done.11.refs_2_ = f32[6,8,128]{2,1,0:T(8,128)S(1)} collective-permute-done((f32[6,8,128]{2,1,0:T(8,128)S(1)}, f32[6,8,128]{2,1,0:T(8,128)S(1)}, u32[]{:S(2)}, u32[]{:S(2)}) %collective-permute-start.11) | collective-permute-done | bytes 24608 | tf_op jit(solution)/shard_map/ppermute | solution.py:436
  36.5 2.3 %collective-permute-done.12.refs_3_ = f32[6,8,128]{2,1,0:T(8,128)S(1)} collective-permute-done((f32[6,8,128]{2,1,0:T(8,128)S(1)}, f32[6,8,128]{2,1,0:T(8,128)S(1)}, u32[]{:S(2)}, u32[]{:S(2)}) %collective-permute-start.12) | collective-permute-done | bytes 24608 | tf_op jit(solution)/shard_map/ppermute | solution.py:436
  38.7 0.6 %shard_map.80 = f32[1,1,6,8,128]{4,3,2,1,0:T(8,128)} custom-call(f32[12,8,128]{2,1,0:T(8,128)S(1)} %get-tuple-element.42.masks_ref, f32[6,8,128]{2,1,0:T(8,128)S(1)} %get-tuple-element.71.refs_0_, f32[6,8,128]{2,1,0:T(8,128)S(1)} %collective-permute-done.10.refs_1_, f32[6,8,128]{2,1,0:T(8,128)S(1)} %collective-permute-done.11.refs_2_, ...), custom_call_target="tpu_custom_call" | custom-call | tf_op jit(solution)/shard_map/pallas_call | solution.py:518
  (2 shorter events, 0.0 us)
Async XLA Ops:
  0.0 9.5 %copy-start.1 = (f32[50]{0:T(128)S(1)}, f32[50]{0:T(128)}, u32[]{:S(2)}) copy-start(f32[50]{0:T(128)} %th_ref.3) | copy-start | bytes 604
  0.0 9.5 %copy-start = (f32[50,32,128]{2,1,0:T(8,128)S(1)}, f32[50,32,128]{2,1,0:T(8,128)}, u32[]{:S(2)}) copy-start(f32[50,32,128]{2,1,0:T(8,128)} %c_ref.3) | copy-start | bytes 2457604
  0.0 9.5 %copy-start.2 = (s32[8]{0:T(128)S(1)}, s32[8]{0:T(128)}, u32[]{:S(2)}) copy-start(s32[8]{0:T(128)} %owner_ref.1) | copy-start | bytes 100
  2.4 11.1 %collective-permute-start.2 = (f32[2,2,50,128]{3,2,1,0:T(8,128)S(1)}, f32[2,2,50,128]{3,2,1,0:T(8,128)S(1)}, u32[]{:S(2)}, u32[]{:S(2)}) collective-permute-start(f32[2,2,50,128]{3,2,1,0:T(8,128)S(1)} %get-tuple-element.50), channel_id=1, source_target_pairs={{4,0},{0,4},{5,1},{1,5},{6,2},{2,6},{7,3},{3,7},{12,8},{8,12},{13,... | collective-permute-start | bytes 307208 | tf_op jit(solution)/shard_map/ppermute | solution.py:436
  5.5 8.1 %collective-permute-start.1 = (f32[2,32,128]{2,1,0:T(8,128)S(1)}, f32[2,32,128]{2,1,0:T(8,128)S(1)}, u32[]{:S(2)}, u32[]{:S(2)}) collective-permute-start(f32[2,32,128]{2,1,0:T(8,128)S(1)} %get-tuple-element.49), channel_id=1, source_target_pairs={{1,0},{0,1},{3,2},{2,3},{5,4},{4,5},{7,6},{6,7},{9,8},{8,9},{11,10... | collective-permute-start | bytes 98312 | tf_op jit(solution)/shard_map/ppermute | solution.py:436
  7.1 6.5 %collective-permute-start = (f32[2,32,128]{2,1,0:T(8,128)S(1)}, f32[2,32,128]{2,1,0:T(8,128)S(1)}, u32[]{:S(2)}, u32[]{:S(2)}) collective-permute-start(f32[2,32,128]{2,1,0:T(8,128)S(1)} %get-tuple-element.49), channel_id=1, source_target_pairs={{3,0},{2,1},{1,2},{0,3},{7,4},{6,5},{5,6},{4,7},{11,8},{10,9},{9,1... | collective-permute-start | bytes 98312 | tf_op jit(solution)/shard_map/ppermute | solution.py:436
  15.5 7.0 %collective-permute-start.5 = (f32[2,2,50,128]{3,2,1,0:T(8,128)S(1)}, f32[2,2,50,128]{3,2,1,0:T(8,128)S(1)}, u32[]{:S(2)}, u32[]{:S(2)}) collective-permute-start(f32[2,2,50,128]{3,2,1,0:T(8,128)S(1)} %get-tuple-element.63), channel_id=1, source_target_pairs={{4,0},{0,4},{5,1},{1,5},{6,2},{2,6},{7,3},{3,7},{12,8},{8,12},{13,... | collective-permute-start | bytes 307208 | tf_op jit(solution)/shard_map/ppermute | solution.py:436
  16.0 4.2 %collective-permute-start.4 = (f32[2,32,128]{2,1,0:T(8,128)S(1)}, f32[2,32,128]{2,1,0:T(8,128)S(1)}, u32[]{:S(2)}, u32[]{:S(2)}) collective-permute-start(f32[2,32,128]{2,1,0:T(8,128)S(1)} %get-tuple-element.62), channel_id=1, source_target_pairs={{1,0},{0,1},{3,2},{2,3},{5,4},{4,5},{7,6},{6,7},{9,8},{8,9},{11,10... | collective-permute-start | bytes 98312 | tf_op jit(solution)/shard_map/ppermute | solution.py:436
  16.7 5.7 %collective-permute-start.3 = (f32[2,32,128]{2,1,0:T(8,128)S(1)}, f32[2,32,128]{2,1,0:T(8,128)S(1)}, u32[]{:S(2)}, u32[]{:S(2)}) collective-permute-start(f32[2,32,128]{2,1,0:T(8,128)S(1)} %get-tuple-element.62), channel_id=1, source_target_pairs={{3,0},{2,1},{1,2},{0,3},{7,4},{6,5},{5,6},{4,7},{11,8},{10,9},{9,1... | collective-permute-start | bytes 98312 | tf_op jit(solution)/shard_map/ppermute | solution.py:436
  22.6 1.9 %collective-permute-start.6 = (f32[2,3,8,128]{3,2,1,0:T(8,128)S(1)}, f32[2,3,8,128]{3,2,1,0:T(8,128)S(1)}, u32[]{:S(2)}, u32[]{:S(2)}) collective-permute-start(f32[2,3,8,128]{3,2,1,0:T(8,128)S(1)} %get-tuple-element.68), channel_id=1, source_target_pairs={{8,0},{0,8},{24,16},{16,24},{9,1},{1,9},{25,17},{17,25},{10,2},{2,... | collective-permute-start | bytes 73736 | tf_op jit(solution)/shard_map/ppermute | solution.py:436
  22.7 3.9 %collective-permute-start.7 = (f32[2,3,8,128]{3,2,1,0:T(8,128)S(1)}, f32[2,3,8,128]{3,2,1,0:T(8,128)S(1)}, u32[]{:S(2)}, u32[]{:S(2)}) collective-permute-start(f32[2,3,8,128]{3,2,1,0:T(8,128)S(1)} %get-tuple-element.69), channel_id=1, source_target_pairs={{16,0},{24,8},{0,16},{8,24},{17,1},{25,9},{1,17},{9,25},{18,2},{26... | collective-permute-start | bytes 73736 | tf_op jit(solution)/shard_map/ppermute | solution.py:436
  24.3 3.3 %collective-permute-start.8 = (f32[2,3,8,128]{3,2,1,0:T(8,128)S(1)}, f32[2,3,8,128]{3,2,1,0:T(8,128)S(1)}, u32[]{:S(2)}, u32[]{:S(2)}) collective-permute-start(f32[2,3,8,128]{3,2,1,0:T(8,128)S(1)} %get-tuple-element.70), channel_id=1, source_target_pairs={{24,0},{16,8},{8,16},{0,24},{25,1},{17,9},{9,17},{1,25},{26,2},{18... | collective-permute-start | bytes 73736 | tf_op jit(solution)/shard_map/ppermute | solution.py:436
  27.5 3.9 %collective-permute-start.9 = (f32[6,8,128]{2,1,0:T(8,128)S(1)}, f32[6,8,128]{2,1,0:T(8,128)S(1)}, u32[]{:S(2)}, u32[]{:S(2)}) collective-permute-start(f32[6,8,128]{2,1,0:T(8,128)S(1)} %shard_map.78.refs_0_), channel_id=1, source_target_pairs={{4,0},{0,4},{5,1},{1,5},{6,2},{2,6},{7,3},{3,7},{12,8},{8,12},{13,... | collective-permute-start | bytes 73736 | tf_op jit(solution)/shard_map/ppermute | solution.py:436
  31.5 4.5 %collective-permute-start.10 = (f32[6,8,128]{2,1,0:T(8,128)S(1)}, f32[6,8,128]{2,1,0:T(8,128)S(1)}, u32[]{:S(2)}, u32[]{:S(2)}) collective-permute-start(f32[6,8,128]{2,1,0:T(8,128)S(1)} %get-tuple-element.72), channel_id=1, source_target_pairs={{1,0},{0,1},{3,2},{2,3},{5,4},{4,5},{7,6},{6,7},{9,8},{8,9},{11,10... | collective-permute-start | bytes 73736 | tf_op jit(solution)/shard_map/ppermute | solution.py:436
  31.5 4.9 %collective-permute-start.11 = (f32[6,8,128]{2,1,0:T(8,128)S(1)}, f32[6,8,128]{2,1,0:T(8,128)S(1)}, u32[]{:S(2)}, u32[]{:S(2)}) collective-permute-start(f32[6,8,128]{2,1,0:T(8,128)S(1)} %get-tuple-element.73), channel_id=1, source_target_pairs={{2,0},{3,1},{0,2},{1,3},{6,4},{7,5},{4,6},{5,7},{10,8},{11,9},{8,1... | collective-permute-start | bytes 73736 | tf_op jit(solution)/shard_map/ppermute | solution.py:436
  33.1 5.6 %collective-permute-start.12 = (f32[6,8,128]{2,1,0:T(8,128)S(1)}, f32[6,8,128]{2,1,0:T(8,128)S(1)}, u32[]{:S(2)}, u32[]{:S(2)}) collective-permute-start(f32[6,8,128]{2,1,0:T(8,128)S(1)} %get-tuple-element.74), channel_id=1, source_target_pairs={{3,0},{2,1},{1,2},{0,3},{7,4},{6,5},{5,6},{4,7},{11,8},{10,9},{9,1... | collective-permute-start | bytes 73736 | tf_op jit(solution)/shard_map/ppermute | solution.py:436

commit v5 on v4

--- a/solution.py
+++ b/solution.py
@@ -11,7 +11,7 @@
 HORIZ = 0.35
 VERT = 1.5
 STEP_A = 8
-STEP_P = 10
+STEP_P = 25
 STEP_B = 25
 STEP_D = 25
 STEP_S = 25
@@ -51,17 +51,26 @@
     return pltpu.roll(x, x.shape[0] - 1, 0)
 
 
-def sides(far_ref, near_ref):
+def outgoing(packed, far_ref, near_ref):
     odd = lax.axis_index("tx") % 2 == 1
-    far = [far_ref[m] for m in range(far_ref.shape[0])]
-    near = [near_ref[m] for m in range(near_ref.shape[0])]
-    west = [jnp.where(odd, a, b) for a, b in zip(near, far)]
-    east = [jnp.where(odd, b, a) for a, b in zip(near, far)]
-    return west, east
-
-
-def pack_kernel(p_hbm, u_hbm, v_hbm, cols_ref, rows_ref, p_ref, u_ref, v_s, sems):
+    even = lanes_of(packed[0].shape) % 2 == 0
+    eastward = jnp.where(even, packed[0], west_roll(packed[1]))
+    westward = jnp.where(even, east_roll(packed[0]), packed[1])
+    far_ref[...] = jnp.where(odd, eastward, westward)
+    near_ref[...] = jnp.where(odd, westward, eastward)
+
+
+def incoming(far_ref, near_ref):
+    odd = lax.axis_index("tx") % 2 == 1
+    far, near = far_ref[...], near_ref[...]
+    even = lanes_of(far.shape) % 2 == 0
+    west, east = jnp.where(odd, near, far), jnp.where(odd, far, near)
+    return [jnp.where(even, east, west_roll(west)), jnp.where(even, east_roll(east), west)]
+
+
+def pack_kernel(p_hbm, u_hbm, v_hbm, far_ref, near_ref, rows_ref, p_ref, u_ref, v_s, sems):
     members, levels, rows, cols = p_ref.shape
+    planes = []
     copies = []
     for m in range(members):
         pair = [
@@ -84,7 +93,8 @@
             packed = jnp.where(lane >= 2 * k, edge, packed)
             rows_ref[0, m, k : k + 1, :] = p[rows - 1 : rows, :]
             rows_ref[1, m, k : k + 1, :] = v_s[m, k, 0:1, :] - HORIZ * p[0:1, :]
-        cols_ref[m] = packed
+        planes.append(packed)
+    outgoing(planes, far_ref, near_ref)
 
 
 def prepare_kernel(
@@ -186,23 +196,38 @@
         copy.wait()
     step1 = divisor(levels, STEP_P)
 
+    group = 8
+    slices = [slice(at, at + group) for at in range(0, rows, group)]
+    glane, grow = lanes_of((group, cols)), rows_of((group, cols))
+    west_edge, east_edge = glane == 0, glane == cols - 1
+
+    def southern(x):
+        x = [pltpu.roll(v, 1, 0) for v in x]
+        return [jnp.where(grow == 0, x[i - 1] if i else 0.0, v) for i, v in enumerate(x)]
+
+    def northern(x):
+        x = [pltpu.roll(v, group - 1, 0) for v in x]
+        after = x[1:] + [0.0]
+        return [jnp.where(grow == group - 1, after[i], v) for i, v in enumerate(x)]
+
     def first_winds(chunk, carry):
         for sub in range(step1):
             k = chunk * step1 + sub
-            c35 = HORIZ * c_ref[k]
             for m in range(members):
-                p = p_ref[m, k]
-                q = HORIZ * p
-                zu = u0_ref[m, k] - q
-                zv = v_ref[m, k] - q
-                u1 = zu + jnp.where(first_lane, 0.0, west_roll(q))
-                v1 = zv + jnp.where(first_row, 0.0, south_roll(q))
-                u_ref[m, k] = u1
-                v_ref[m, k] = v1
-                zu_east = jnp.where(last_lane, 0.0, east_roll(zu))
-                zv_north = jnp.where(last_row, 0.0, north_roll(zv))
-                div = ((zu_east + q) - u1) + ((zv_north + q) - v1)
-                part_ref[m, k] = p - c35 * div
+                q, zv = [], []
+                for rs in slices:
+                    q.append(HORIZ * p_ref[m, k, rs])
+                    zv.append(v_ref[m, k, rs] - q[-1])
+                q_south, zv_north = southern(q), northern(zv)
+                for i, rs in enumerate(slices):
+                    zu = u0_ref[m, k, rs] - q[i]
+                    u1 = zu + jnp.where(west_edge, 0.0, west_roll(q[i]))
+                    v1 = zv[i] + q_south[i]
+                    u_ref[m, k, rs] = u1
+                    v_ref[m, k, rs] = v1
+                    zu_east = jnp.where(east_edge, 0.0, east_roll(zu))
+                    div = ((zu_east + q[i]) - u1) + ((zv_north[i] + q[i]) - v1)
+                    part_ref[m, k, rs] = p_ref[m, k, rs] - (HORIZ * c_ref[k, rs]) * div
         return carry
 
     lax.fori_loop(0, levels // step1, first_winds, 0)
@@ -212,7 +237,7 @@
 
 def solve_kernel(
     c_ref, part_ref, u_ref, v_ref, w_ref, e_s, inv_s, far_ref, near_ref, from_rows,
-    cols_ref, rows_ref, p1_ref, zu_ref, zv_ref, w1_ref,
+    far_out, near_out, rows_ref, p1_ref, zu_ref, zv_ref, w1_ref,
 ):
     members, levels, rows, cols = part_ref.shape
     group = 8
@@ -224,12 +249,10 @@
     at_first = jnp.where(lane == 0, 1.0, 0.0)
     signed = jnp.where(lane == cols - 1, -1.0, at_first)
     even = lane % 2 == 0
-    from_west, from_east = sides(far_ref, near_ref)
     halo = []
-    for m in range(members):
+    for mixed in incoming(far_ref, near_ref):
         for rs in slices:
-            mixed = jnp.where(even, east_roll(from_east[m][rs]), HORIZ * west_roll(from_west[m][rs]))
-            halo.append(east_roll(mixed))
+            halo.append(east_roll(jnp.where(even, mixed[rs], HORIZ * mixed[rs])))
     step1 = divisor(levels, STEP_B)
 
     def upward(chunk, carry):
@@ -301,9 +324,10 @@
 
     step2 = divisor(levels, STEP_D)
     _, packs = lax.fori_loop(0, levels // step2, downward, (zeros, zeros))
-    for m in range(members):
-        for g, rs in enumerate(slices):
-            cols_ref[m, rs] = packs[m * groups + g]
+    planes = [
+        jnp.concatenate(packs[m * groups : (m + 1) * groups], axis=0) for m in range(members)
+    ]
+    outgoing(planes, far_out, near_out)
 
 
 def sum_kernel(
@@ -358,7 +382,7 @@
 
 def edge_kernel(sums_ref, far_ref, near_ref, from_rows, hcols_ref, hrows_ref, hth_ref, *rest):
     outs, total_s = rest[:-1], rest[-1]
-    from_west, from_east = sides(far_ref, near_ref)
+    mixed = incoming(far_ref, near_ref)
     members, _, rows, cols = sums_ref.shape
     levels = hrows_ref.shape[1]
     height = rows // len(outs)
@@ -369,11 +393,10 @@
     used = lane < 2 * levels
     hth = jnp.concatenate([hth_ref[...]] * (rows // 8), axis=0)
     for m in range(members):
-        west = west_roll(from_west[m])
-        products = jnp.where(used, hcols_ref[...] * jnp.where(even, east_roll(from_east[m]), west), 0.0)
+        products = jnp.where(used, hcols_ref[...] * mixed[m], 0.0)
         at_east = jnp.sum(jnp.where(even, products, 0.0), axis=1, keepdims=True)
         at_west = jnp.sum(jnp.where(even, 0.0, products), axis=1, keepdims=True)
-        u_west = jnp.sum(hth * west, axis=1, keepdims=True)
+        u_west = jnp.sum(hth * mixed[m], axis=1, keepdims=True)
         at_south = jnp.sum(hrows_ref[0] * from_rows[0, m], axis=0, keepdims=True)
         at_north = jnp.sum(hrows_ref[1] * from_rows[1, m], axis=0, keepdims=True)
         v_south = jnp.sum(hrows_ref[2] * from_rows[0, m], axis=0, keepdims=True)
@@ -436,9 +459,9 @@
     return lax.ppermute(block, axis, [(source(i) % count, i) for i in range(count)])
 
 
-def exchange(columns, edge_rows):
-    far = permuted(columns, "tx", lambda i: i + 1 if i % 2 else i - 1)
-    near = permuted(columns, "tx", lambda i: i ^ 1)
+def exchange(far, near, edge_rows):
+    far = permuted(far, "tx", lambda i: i + 1 if i % 2 else i - 1)
+    near = permuted(near, "tx", lambda i: i ^ 1)
     if lax.axis_size("ty") <= 2:
         both = permuted(edge_rows, "ty", lambda i: i - 1)
     else:
@@ -452,7 +475,7 @@
     members, levels, rows, cols = pressure.shape
     ranks, height_count, width = (lax.axis_size(a) for a in ("mem", "ty", "tx"))
     height = rows // ranks
-    plane = (members, rows, cols)
+    plane = (rows, cols)
     many = (members, levels, rows, cols)
     field = (levels, rows, cols)
     lines = (2, members, levels, cols)
@@ -461,9 +484,9 @@
         pltpu.with_memory_space_constraint(x, pltpu.HBM)
         for x in (pressure, east_wind, north_wind, vertical_wind)
     )
-    columns, edge_rows, p0, u0 = call(
+    far, near, edge_rows, p0, u0 = call(
         pack_kernel,
-        [plane, lines, many, many],
+        [plane, plane, lines, many, many],
         [HBM] * 3,
         [
             pltpu.VMEM((members, levels, 8, cols), jnp.float32),
@@ -471,7 +494,7 @@
         ],
         limit=PACK_LIMIT,
     )(pressure, east_wind, north_wind)
-    far, near, both = exchange(columns, edge_rows)
+    far, near, both = exchange(far, near, edge_rows)
     hcols, hrows, hth, masks, e, inv, *weights, part0, u0, v0, w0 = call(
         prepare_kernel,
         [
@@ -487,10 +510,10 @@
         [pltpu.SemaphoreType.DMA((2, members))],
         limit=PREP_LIMIT,
     )(sound_squared, p0, u0, north_wind, vertical_wind, thickness, owner_map)
-    columns, edge_rows, p1, zu, zv, w1 = call(
-        solve_kernel, [plane, lines, *[many] * 4], [VMEM] * 10
+    far, near, edge_rows, p1, zu, zv, w1 = call(
+        solve_kernel, [plane, plane, lines, *[many] * 4], [VMEM] * 10
     )(sound_squared, part0, u0, v0, w0, e, inv, far, near, both)
-    far, near, both = exchange(columns, edge_rows)
+    far, near, both = exchange(far, near, edge_rows)
     (sums,) = call(
         sum_kernel,
         [(members, 3, rows, cols)],

time: 39.5 us -> 39.2 us (level)
  transfers between devices with their start and end apart: 13 -> 13, of which waited for: 7 -> 6; matrix products, arithmetic and copies ran while one was open for 0% -> 0% of each run, Pallas kernels for 16% -> 16%
where the time goes in v5:
time: 39.2 us; the launch traced here: 39 us
  starting transfers between devices  17.2 us (44%)
  Pallas kernels  11.5 us (29%)
  waiting for transfers between devices  10.2 us (26%)
    ppermute x13, starting transfers between devices, permuted(): lax.ppermute(block, axis, [(source(i) % count, i) for i in range(count)])  17.2 us
    ppermute x13, waiting for transfers between devices, permuted(): lax.ppermute(block, axis, [(source(i) % count, i) for i in range(count)])  10.2 us
    pallas_call x1, Pallas kernels, steps(): call(prepare_kernel, [(rows, cols), (3, levels, cols), (8, cols), (height...  3.8 us
    pallas_call x1, Pallas kernels, steps(): call(pack_kernel, [plane, plane, lines, many, many], [HBM] * 3, [pltpu.VM...  2.47 us
    pallas_call x1, Pallas kernels, steps(): call(sum_kernel, [(members, 3, rows, cols)], [VMEM] * 4 + [SMEM] + [VMEM]...  2.44 us
    pallas_call x1, Pallas kernels, steps(): call(solve_kernel, [plane, plane, lines, *[many] * 4], [VMEM] * 10)  1.95 us
  transfers between devices with their start and end apart: 13, of which 6 were waited for; matrix products, arithmetic and copies ran while one was open for 0% of the time, Pallas kernels for 16%

profile of v5, /device:TPU:0, one launch (start us, length us, event | category | flops | bytes accessed | tf_op | source)
XLA Modules:
  0.0 39.0 jit_solution(16619017752400688366)
XLA Ops:
  0.0 0.0 copy-start.1
  0.0 0.0 copy-start
  0.0 0.0 copy-start.2
  0.0 2.5 %shard_map.73 = (f32[32,128]{1,0:T(8,128)S(1)}, f32[32,128]{1,0:T(8,128)S(1)}, f32[2,2,50,128]{3,2,1,0:T(8,128)S(1)}, f32[2,50,32,128]{3,2,1,0:T(8,128)S(1)}, f32[2,50,32,128]{3,2,1,0:T(8,128)S(1)}) custom-call(f32[2,50,32,128]{3,2,1,0:T(8,128)} %p_hbm.1, f32[2,50,32,128]{3,2,1,0:T(8,128)} %u_hbm.1, f32[2,50,32,128]{3,2,1,0:T(8,128)} %v_hbm.3), custom_call_target="tpu_custom_call" | custom-call | tf_op jit(solution)/shard_map/pallas_call | solution.py:487
  2.5 3.1 %collective-permute-start.2 = (f32[2,2,50,128]{3,2,1,0:T(8,128)S(1)}, f32[2,2,50,128]{3,2,1,0:T(8,128)S(1)}, u32[]{:S(2)}, u32[]{:S(2)}) collective-permute-start(f32[2,2,50,128]{3,2,1,0:T(8,128)S(1)} %get-tuple-element.53), channel_id=1, source_target_pairs={{4,0},{0,4},{5,1},{1,5},{6,2},{2,6},{7,3},{3,7},{12,8},{8,12},{13,... | collective-permute-start | bytes 307208 | tf_op jit(solution)/shard_map/ppermute | solution.py:459
  5.6 3.6 %collective-permute-start = (f32[32,128]{1,0:T(8,128)S(1)}, f32[32,128]{1,0:T(8,128)S(1)}, u32[]{:S(2)}, u32[]{:S(2)}) collective-permute-start(f32[32,128]{1,0:T(8,128)S(1)} %get-tuple-element.51), channel_id=1, source_target_pairs={{3,0},{2,1},{1,2},{0,3},{7,4},{6,5},{5,6},{4,7},{11,8},{10,9},{9,1... | collective-permute-start | bytes 49160 | tf_op jit(solution)/shard_map/ppermute | solution.py:459
  9.2 0.0 collective-permute-start.1
  9.2 0.0 copy-done.1
  9.2 0.0 copy-done
  9.2 0.0 copy-done.2
  9.2 3.8 %shard_map.74 = (f32[32,128]{1,0:T(8,128)S(1)}, f32[3,50,128]{2,1,0:T(8,128)S(1)}, f32[8,128]{1,0:T(8,128)S(1)}, f32[12,8,128]{2,1,0:T(8,128)S(1)}, f32[50,32,12...) custom-call(f32[50,32,128]{2,1,0:T(8,128)S(1)} %copy-done, ...), custom_call_target="tpu_custom_call" | custom-call | tf_op jit(solution)/shard_map/pallas_call | solution.py:498
  13.0 0.0 collective-permute-done.far_ref
  13.0 0.0 collective-permute-done.1.near_ref
  13.0 0.0 collective-permute-done.2.from_rows
  13.0 1.9 %shard_map.75 = (f32[32,128]{1,0:T(8,128)S(1)}, f32[32,128]{1,0:T(8,128)S(1)}, f32[2,2,50,128]{3,2,1,0:T(8,128)S(1)}, f32[2,50,32,128]{3,2,1,0:T(8,128)S(1)}, f3...) custom-call(f32[50,32,128]{2,1,0:T(8,128)S(1)} %copy-done, ...), custom_call_target="tpu_custom_call" | custom-call | tf_op jit(solution)/shard_map/pallas_call | solution.py:513
  15.0 0.6 %collective-permute-start.5 = (f32[2,2,50,128]{3,2,1,0:T(8,128)S(1)}, f32[2,2,50,128]{3,2,1,0:T(8,128)S(1)}, u32[]{:S(2)}, u32[]{:S(2)}) collective-permute-start(f32[2,2,50,128]{3,2,1,0:T(8,128)S(1)} %get-tuple-element.67), channel_id=1, source_target_pairs={{4,0},{0,4},{5,1},{1,5},{6,2},{2,6},{7,3},{3,7},{12,8},{8,12},{13,... | collective-permute-start | bytes 307208 | tf_op jit(solution)/shard_map/ppermute | solution.py:459
  15.5 1.7 %collective-permute-start.3 = (f32[32,128]{1,0:T(8,128)S(1)}, f32[32,128]{1,0:T(8,128)S(1)}, u32[]{:S(2)}, u32[]{:S(2)}) collective-permute-start(f32[32,128]{1,0:T(8,128)S(1)} %get-tuple-element.65), channel_id=1, source_target_pairs={{3,0},{2,1},{1,2},{0,3},{7,4},{6,5},{5,6},{4,7},{11,8},{10,9},{9,1... | collective-permute-start | bytes 49160 | tf_op jit(solution)/shard_map/ppermute | solution.py:459
  17.2 0.3 collective-permute-start.4
  17.6 2.4 %shard_map.76.sums_ref = f32[2,3,32,128]{3,2,1,0:T(8,128)S(1)} custom-call(f32[2,50,32,128]{3,2,1,0:T(8,128)S(1)} %get-tuple-element.54.p1_ref, f32[2,50,32,128]{3,2,1,0:T(8,128)S(1)} %get-tuple-element.55.zu_ref, f32[2,50,32,128]{3,2,1,0:T(8,128)S(1)} %get-tuple-element.56.zv_ref, f32[2,50,32,128]{3,2,1,0:T(8,128)S(1)} %get-tuple-element.57.w1_ref, ...), custom_call_target="tpu_custom_call" | custom-call | tf_op jit(solution)/shard_map/pallas_call | solution.py:517
  20.0 1.1 %collective-permute-done.3.far_ref = f32[32,128]{1,0:T(8,128)S(1)} collective-permute-done((f32[32,128]{1,0:T(8,128)S(1)}, f32[32,128]{1,0:T(8,128)S(1)}, u32[]{:S(2)}, u32[]{:S(2)}) %collective-permute-start.3) | collective-permute-done | bytes 16416 | tf_op jit(solution)/shard_map/ppermute | solution.py:459
  21.1 0.0 collective-permute-done.4.near_ref
  21.1 0.0 collective-permute-done.5.from_rows
  21.1 0.2 shard_map.77
  21.3 0.1 collective-permute-start.6
  21.4 1.6 %collective-permute-start.7 = (f32[2,3,8,128]{3,2,1,0:T(8,128)S(1)}, f32[2,3,8,128]{3,2,1,0:T(8,128)S(1)}, u32[]{:S(2)}, u32[]{:S(2)}) collective-permute-start(f32[2,3,8,128]{3,2,1,0:T(8,128)S(1)} %get-tuple-element.73), channel_id=1, source_target_pairs={{16,0},{24,8},{0,16},{8,24},{17,1},{25,9},{1,17},{9,25},{18,2},{26... | collective-permute-start | bytes 73736 | tf_op jit(solution)/shard_map/ppermute | solution.py:459
  23.0 0.3 collective-permute-start.8
  23.3 0.0 collective-permute-done.6.refs_1_
  23.3 2.0 %collective-permute-done.7.refs_2_ = f32[2,3,8,128]{3,2,1,0:T(8,128)S(1)} collective-permute-done((f32[2,3,8,128]{3,2,1,0:T(8,128)S(1)}, f32[2,3,8,128]{3,2,1,0:T(8,128)S(1)}, u32[]{:S(2)}, u32[]{:S(2)}) %collective-permute-start.7) | collective-permute-done | bytes 24608 | tf_op jit(solution)/shard_map/ppermute | solution.py:459
  25.3 0.9 %collective-permute-done.8.refs_3_ = f32[2,3,8,128]{3,2,1,0:T(8,128)S(1)} collective-permute-done((f32[2,3,8,128]{3,2,1,0:T(8,128)S(1)}, f32[2,3,8,128]{3,2,1,0:T(8,128)S(1)}, u32[]{:S(2)}, u32[]{:S(2)}) %collective-permute-start.8) | collective-permute-done | bytes 24608 | tf_op jit(solution)/shard_map/ppermute | solution.py:459
  26.3 1.6 %collective-permute-start.9 = (f32[6,8,128]{2,1,0:T(8,128)S(1)}, f32[6,8,128]{2,1,0:T(8,128)S(1)}, u32[]{:S(2)}, u32[]{:S(2)}) collective-permute-start(f32[6,8,128]{2,1,0:T(8,128)S(1)} %shard_map.78.refs_0_), channel_id=1, source_target_pairs={{4,0},{0,4},{5,1},{1,5},{6,2},{2,6},{7,3},{3,7},{12,8},{8,12},{13,... | collective-permute-start | bytes 73736 | tf_op jit(solution)/shard_map/ppermute | solution.py:459
  27.8 2.3 %collective-permute-done.9.refs_1_ = f32[6,8,128]{2,1,0:T(8,128)S(1)} collective-permute-done((f32[6,8,128]{2,1,0:T(8,128)S(1)}, f32[6,8,128]{2,1,0:T(8,128)S(1)}, u32[]{:S(2)}, u32[]{:S(2)}) %collective-permute-start.9) | collective-permute-done | bytes 24608 | tf_op jit(solution)/shard_map/ppermute | solution.py:459
  30.2 0.8 %collective-permute-start.10 = (f32[6,8,128]{2,1,0:T(8,128)S(1)}, f32[6,8,128]{2,1,0:T(8,128)S(1)}, u32[]{:S(2)}, u32[]{:S(2)}) collective-permute-start(f32[6,8,128]{2,1,0:T(8,128)S(1)} %get-tuple-element.76), channel_id=1, source_target_pairs={{1,0},{0,1},{3,2},{2,3},{5,4},{4,5},{7,6},{6,7},{9,8},{8,9},{11,10... | collective-permute-start | bytes 73736 | tf_op jit(solution)/shard_map/ppermute | solution.py:459
  30.9 1.8 %collective-permute-start.11 = (f32[6,8,128]{2,1,0:T(8,128)S(1)}, f32[6,8,128]{2,1,0:T(8,128)S(1)}, u32[]{:S(2)}, u32[]{:S(2)}) collective-permute-start(f32[6,8,128]{2,1,0:T(8,128)S(1)} %get-tuple-element.77), channel_id=1, source_target_pairs={{2,0},{3,1},{0,2},{1,3},{6,4},{7,5},{4,6},{5,7},{10,8},{11,9},{8,1... | collective-permute-start | bytes 73736 | tf_op jit(solution)/shard_map/ppermute | solution.py:459
  32.8 1.9 %collective-permute-start.12 = (f32[6,8,128]{2,1,0:T(8,128)S(1)}, f32[6,8,128]{2,1,0:T(8,128)S(1)}, u32[]{:S(2)}, u32[]{:S(2)}) collective-permute-start(f32[6,8,128]{2,1,0:T(8,128)S(1)} %get-tuple-element.78), channel_id=1, source_target_pairs={{3,0},{2,1},{1,2},{0,3},{7,4},{6,5},{5,6},{4,7},{11,8},{10,9},{9,1... | collective-permute-start | bytes 73736 | tf_op jit(solution)/shard_map/ppermute | solution.py:459
  34.6 0.0 collective-permute-done.10.refs_1_
  34.6 1.0 %collective-permute-done.11.refs_2_ = f32[6,8,128]{2,1,0:T(8,128)S(1)} collective-permute-done((f32[6,8,128]{2,1,0:T(8,128)S(1)}, f32[6,8,128]{2,1,0:T(8,128)S(1)}, u32[]{:S(2)}, u32[]{:S(2)}) %collective-permute-start.11) | collective-permute-done | bytes 24608 | tf_op jit(solution)/shard_map/ppermute | solution.py:459
  35.7 2.7 %collective-permute-done.12.refs_3_ = f32[6,8,128]{2,1,0:T(8,128)S(1)} collective-permute-done((f32[6,8,128]{2,1,0:T(8,128)S(1)}, f32[6,8,128]{2,1,0:T(8,128)S(1)}, u32[]{:S(2)}, u32[]{:S(2)}) %collective-permute-start.12) | collective-permute-done | bytes 24608 | tf_op jit(solution)/shard_map/ppermute | solution.py:459
  38.4 0.6 %shard_map.80 = f32[1,1,6,8,128]{4,3,2,1,0:T(8,128)} custom-call(f32[12,8,128]{2,1,0:T(8,128)S(1)} %get-tuple-element.44.masks_ref, f32[6,8,128]{2,1,0:T(8,128)S(1)} %get-tuple-element.75.refs_0_, f32[6,8,128]{2,1,0:T(8,128)S(1)} %collective-permute-done.10.refs_1_, f32[6,8,128]{2,1,0:T(8,128)S(1)} %collective-permute-done.11.refs_2_, ...), custom_call_target="tpu_custom_call" | custom-call | tf_op jit(solution)/shard_map/pallas_call | solution.py:541
  (2 shorter events, 0.0 us)
Async XLA Ops:
  0.0 9.2 %copy-start.1 = (f32[50]{0:T(128)S(1)}, f32[50]{0:T(128)}, u32[]{:S(2)}) copy-start(f32[50]{0:T(128)} %th_ref.3) | copy-start | bytes 604
  0.0 9.2 %copy-start = (f32[50,32,128]{2,1,0:T(8,128)S(1)}, f32[50,32,128]{2,1,0:T(8,128)}, u32[]{:S(2)}) copy-start(f32[50,32,128]{2,1,0:T(8,128)} %c_ref.3) | copy-start | bytes 2457604
  0.0 9.2 %copy-start.2 = (s32[8]{0:T(128)S(1)}, s32[8]{0:T(128)}, u32[]{:S(2)}) copy-start(s32[8]{0:T(128)} %owner_ref.1) | copy-start | bytes 100
  2.5 10.5 %collective-permute-start.2 = (f32[2,2,50,128]{3,2,1,0:T(8,128)S(1)}, f32[2,2,50,128]{3,2,1,0:T(8,128)S(1)}, u32[]{:S(2)}, u32[]{:S(2)}) collective-permute-start(f32[2,2,50,128]{3,2,1,0:T(8,128)S(1)} %get-tuple-element.53), channel_id=1, source_target_pairs={{4,0},{0,4},{5,1},{1,5},{6,2},{2,6},{7,3},{3,7},{12,8},{8,12},{13,... | collective-permute-start | bytes 307208 | tf_op jit(solution)/shard_map/ppermute | solution.py:459
  5.6 7.4 %collective-permute-start = (f32[32,128]{1,0:T(8,128)S(1)}, f32[32,128]{1,0:T(8,128)S(1)}, u32[]{:S(2)}, u32[]{:S(2)}) collective-permute-start(f32[32,128]{1,0:T(8,128)S(1)} %get-tuple-element.51), channel_id=1, source_target_pairs={{3,0},{2,1},{1,2},{0,3},{7,4},{6,5},{5,6},{4,7},{11,8},{10,9},{9,1... | collective-permute-start | bytes 49160 | tf_op jit(solution)/shard_map/ppermute | solution.py:459
  9.2 3.8 %collective-permute-start.1 = (f32[32,128]{1,0:T(8,128)S(1)}, f32[32,128]{1,0:T(8,128)S(1)}, u32[]{:S(2)}, u32[]{:S(2)}) collective-permute-start(f32[32,128]{1,0:T(8,128)S(1)} %get-tuple-element.52), channel_id=1, source_target_pairs={{1,0},{0,1},{3,2},{2,3},{5,4},{4,5},{7,6},{6,7},{9,8},{8,9},{11,10... | collective-permute-start | bytes 49160 | tf_op jit(solution)/shard_map/ppermute | solution.py:459
  15.0 6.2 %collective-permute-start.5 = (f32[2,2,50,128]{3,2,1,0:T(8,128)S(1)}, f32[2,2,50,128]{3,2,1,0:T(8,128)S(1)}, u32[]{:S(2)}, u32[]{:S(2)}) collective-permute-start(f32[2,2,50,128]{3,2,1,0:T(8,128)S(1)} %get-tuple-element.67), channel_id=1, source_target_pairs={{4,0},{0,4},{5,1},{1,5},{6,2},{2,6},{7,3},{3,7},{12,8},{8,12},{13,... | collective-permute-start | bytes 307208 | tf_op jit(solution)/shard_map/ppermute | solution.py:459
  15.5 5.6 %collective-permute-start.3 = (f32[32,128]{1,0:T(8,128)S(1)}, f32[32,128]{1,0:T(8,128)S(1)}, u32[]{:S(2)}, u32[]{:S(2)}) collective-permute-start(f32[32,128]{1,0:T(8,128)S(1)} %get-tuple-element.65), channel_id=1, source_target_pairs={{3,0},{2,1},{1,2},{0,3},{7,4},{6,5},{5,6},{4,7},{11,8},{10,9},{9,1... | collective-permute-start | bytes 49160 | tf_op jit(solution)/shard_map/ppermute | solution.py:459
  17.2 3.9 %collective-permute-start.4 = (f32[32,128]{1,0:T(8,128)S(1)}, f32[32,128]{1,0:T(8,128)S(1)}, u32[]{:S(2)}, u32[]{:S(2)}) collective-permute-start(f32[32,128]{1,0:T(8,128)S(1)} %get-tuple-element.66), channel_id=1, source_target_pairs={{1,0},{0,1},{3,2},{2,3},{5,4},{4,5},{7,6},{6,7},{9,8},{8,9},{11,10... | collective-permute-start | bytes 49160 | tf_op jit(solution)/shard_map/ppermute | solution.py:459
  21.3 1.9 %collective-permute-start.6 = (f32[2,3,8,128]{3,2,1,0:T(8,128)S(1)}, f32[2,3,8,128]{3,2,1,0:T(8,128)S(1)}, u32[]{:S(2)}, u32[]{:S(2)}) collective-permute-start(f32[2,3,8,128]{3,2,1,0:T(8,128)S(1)} %get-tuple-element.72), channel_id=1, source_target_pairs={{8,0},{0,8},{24,16},{16,24},{9,1},{1,9},{25,17},{17,25},{10,2},{2,... | collective-permute-start | bytes 73736 | tf_op jit(solution)/shard_map/ppermute | solution.py:459
  21.4 3.9 %collective-permute-start.7 = (f32[2,3,8,128]{3,2,1,0:T(8,128)S(1)}, f32[2,3,8,128]{3,2,1,0:T(8,128)S(1)}, u32[]{:S(2)}, u32[]{:S(2)}) collective-permute-start(f32[2,3,8,128]{3,2,1,0:T(8,128)S(1)} %get-tuple-element.73), channel_id=1, source_target_pairs={{16,0},{24,8},{0,16},{8,24},{17,1},{25,9},{1,17},{9,25},{18,2},{26... | collective-permute-start | bytes 73736 | tf_op jit(solution)/shard_map/ppermute | solution.py:459
  23.0 3.3 %collective-permute-start.8 = (f32[2,3,8,128]{3,2,1,0:T(8,128)S(1)}, f32[2,3,8,128]{3,2,1,0:T(8,128)S(1)}, u32[]{:S(2)}, u32[]{:S(2)}) collective-permute-start(f32[2,3,8,128]{3,2,1,0:T(8,128)S(1)} %get-tuple-element.74), channel_id=1, source_target_pairs={{24,0},{16,8},{8,16},{0,24},{25,1},{17,9},{9,17},{1,25},{26,2},{18... | collective-permute-start | bytes 73736 | tf_op jit(solution)/shard_map/ppermute | solution.py:459
  26.3 3.9 %collective-permute-start.9 = (f32[6,8,128]{2,1,0:T(8,128)S(1)}, f32[6,8,128]{2,1,0:T(8,128)S(1)}, u32[]{:S(2)}, u32[]{:S(2)}) collective-permute-start(f32[6,8,128]{2,1,0:T(8,128)S(1)} %shard_map.78.refs_0_), channel_id=1, source_target_pairs={{4,0},{0,4},{5,1},{1,5},{6,2},{2,6},{7,3},{3,7},{12,8},{8,12},{13,... | collective-permute-start | bytes 73736 | tf_op jit(solution)/shard_map/ppermute | solution.py:459
  30.2 4.5 %collective-permute-start.10 = (f32[6,8,128]{2,1,0:T(8,128)S(1)}, f32[6,8,128]{2,1,0:T(8,128)S(1)}, u32[]{:S(2)}, u32[]{:S(2)}) collective-permute-start(f32[6,8,128]{2,1,0:T(8,128)S(1)} %get-tuple-element.76), channel_id=1, source_target_pairs={{1,0},{0,1},{3,2},{2,3},{5,4},{4,5},{7,6},{6,7},{9,8},{8,9},{11,10... | collective-permute-start | bytes 73736 | tf_op jit(solution)/shard_map/ppermute | solution.py:459
  30.9 4.7 %collective-permute-start.11 = (f32[6,8,128]{2,1,0:T(8,128)S(1)}, f32[6,8,128]{2,1,0:T(8,128)S(1)}, u32[]{:S(2)}, u32[]{:S(2)}) collective-permute-start(f32[6,8,128]{2,1,0:T(8,128)S(1)} %get-tuple-element.77), channel_id=1, source_target_pairs={{2,0},{3,1},{0,2},{1,3},{6,4},{7,5},{4,6},{5,7},{10,8},{11,9},{8,1... | collective-permute-start | bytes 73736 | tf_op jit(solution)/shard_map/ppermute | solution.py:459
  32.8 5.6 %collective-permute-start.12 = (f32[6,8,128]{2,1,0:T(8,128)S(1)}, f32[6,8,128]{2,1,0:T(8,128)S(1)}, u32[]{:S(2)}, u32[]{:S(2)}) collective-permute-start(f32[6,8,128]{2,1,0:T(8,128)S(1)} %get-tuple-element.78), channel_id=1, source_target_pairs={{3,0},{2,1},{1,2},{0,3},{7,4},{6,5},{5,6},{4,7},{11,8},{10,9},{9,1... | collective-permute-start | bytes 73736 | tf_op jit(solution)/shard_map/ppermute | solution.py:459

commit v6 on v5

--- a/solution.py
+++ b/solution.py
@@ -113,9 +113,7 @@
     inner = levels - 1
     shape = (rows, cols)
     lane = lanes_of(shape)
-    row = rows_of(shape)
     first_lane, last_lane = lane == 0, lane == cols - 1
-    first_row, last_row = row == 0, row == rows - 1
     zero = jnp.zeros(shape, jnp.float32)
     vsq = VERT * VERT
 
@@ -156,6 +154,20 @@
 
     lax.fori_loop(0, inner // step, factor, (zero, zero, c_ref[0]))
 
+    group = 8
+    slices = [slice(at, at + group) for at in range(0, rows, group)]
+    glane, grow = lanes_of((group, cols)), rows_of((group, cols))
+    west_edge, east_edge = glane == 0, glane == cols - 1
+
+    def southern(x):
+        x = [pltpu.roll(v, 1, 0) for v in x]
+        return [jnp.where(grow == 0, x[i - 1] if i else 0.0, v) for i, v in enumerate(x)]
+
+    def northern(x):
+        x = [pltpu.roll(v, group - 1, 0) for v in x]
+        after = x[1:] + [0.0]
+        return [jnp.where(grow == group - 1, after[i], v) for i, v in enumerate(x)]
+
     def weights(k, y_above, y_here):
         g = th_ref[k] + VERT * (y_above - y_here)
         h = g * (HORIZ * c_ref[k])
@@ -164,8 +176,11 @@
         h35 = HORIZ * h
         hw_s[k] = jnp.where(first_lane, 0.0, west_roll(h))
         he_s[k] = jnp.where(last_lane, 0.0, east_roll(h35))
-        hs_s[k] = jnp.where(first_row, 0.0, south_roll(h))
-        hn_s[k] = jnp.where(last_row, 0.0, north_roll(h35))
+        h_south = southern([h[rs] for rs in slices])
+        h_north = northern([h35[rs] for rs in slices])
+        for i, rs in enumerate(slices):
+            hs_s[k, rs] = h_south[i]
+            hn_s[k, rs] = h_north[i]
         hrows_ref[0, pl.ds(k, 1), :] = h35[0:1, :]
         hrows_ref[1, pl.ds(k, 1), :] = h[rows - 1 : rows, :]
         hrows_ref[2, pl.ds(k, 1), :] = jnp.full((1, cols), HORIZ * th_ref[k], jnp.float32)
@@ -195,20 +210,6 @@
     for copy in copies[:members]:
         copy.wait()
     step1 = divisor(levels, STEP_P)
-
-    group = 8
-    slices = [slice(at, at + group) for at in range(0, rows, group)]
-    glane, grow = lanes_of((group, cols)), rows_of((group, cols))
-    west_edge, east_edge = glane == 0, glane == cols - 1
-
-    def southern(x):
-        x = [pltpu.roll(v, 1, 0) for v in x]
-        return [jnp.where(grow == 0, x[i - 1] if i else 0.0, v) for i, v in enumerate(x)]
-
-    def northern(x):
-        x = [pltpu.roll(v, group - 1, 0) for v in x]
-        after = x[1:] + [0.0]
-        return [jnp.where(grow == group - 1, after[i], v) for i, v in enumerate(x)]
 
     def first_winds(chunk, carry):
         for sub in range(step1):

time: 39.2 us -> 39.1 us (level)
  no operation moved by 1% of the time
where the time goes in v6:
time: 39.1 us; the launch traced here: 39 us
  starting transfers between devices  17.2 us (44%)
  Pallas kernels  11.5 us (29%)
  waiting for transfers between devices  10.2 us (26%)
    ppermute x13, starting transfers between devices, permuted(): lax.ppermute(block, axis, [(source(i) % count, i) for i in range(count)])  17.2 us
    ppermute x13, waiting for transfers between devices, permuted(): lax.ppermute(block, axis, [(source(i) % count, i) for i in range(count)])  10.2 us
    pallas_call x1, Pallas kernels, steps(): call(prepare_kernel, [(rows, cols), (3, levels, cols), (8, cols), (height...  3.79 us
    pallas_call x1, Pallas kernels, steps(): call(pack_kernel, [plane, plane, lines, many, many], [HBM] * 3, [pltpu.VM...  2.47 us
    pallas_call x1, Pallas kernels, steps(): call(sum_kernel, [(members, 3, rows, cols)], [VMEM] * 4 + [SMEM] + [VMEM]...  2.44 us
    pallas_call x1, Pallas kernels, steps(): call(solve_kernel, [plane, plane, lines, *[many] * 4], [VMEM] * 10)  1.95 us
  transfers between devices with their start and end apart: 13, of which 6 were waited for; matrix products, arithmetic and copies ran while one was open for 0% of the time, Pallas kernels for 16%

profile of v6, /device:TPU:0, one launch (start us, length us, event | category | flops | bytes accessed | tf_op | source)
XLA Modules:
  0.0 39.0 jit_solution(4998904445057290526)
XLA Ops:
  0.0 0.0 copy-start.1
  0.0 0.0 copy-start
  0.0 0.0 copy-start.2
  0.0 2.5 %shard_map.73 = (f32[32,128]{1,0:T(8,128)S(1)}, f32[32,128]{1,0:T(8,128)S(1)}, f32[2,2,50,128]{3,2,1,0:T(8,128)S(1)}, f32[2,50,32,128]{3,2,1,0:T(8,128)S(1)}, f32[2,50,32,128]{3,2,1,0:T(8,128)S(1)}) custom-call(f32[2,50,32,128]{3,2,1,0:T(8,128)} %p_hbm.1, f32[2,50,32,128]{3,2,1,0:T(8,128)} %u_hbm.1, f32[2,50,32,128]{3,2,1,0:T(8,128)} %v_hbm.3), custom_call_target="tpu_custom_call" | custom-call | tf_op jit(solution)/shard_map/pallas_call | solution.py:488
  2.5 3.1 %collective-permute-start.2 = (f32[2,2,50,128]{3,2,1,0:T(8,128)S(1)}, f32[2,2,50,128]{3,2,1,0:T(8,128)S(1)}, u32[]{:S(2)}, u32[]{:S(2)}) collective-permute-start(f32[2,2,50,128]{3,2,1,0:T(8,128)S(1)} %get-tuple-element.53), channel_id=1, source_target_pairs={{4,0},{0,4},{5,1},{1,5},{6,2},{2,6},{7,3},{3,7},{12,8},{8,12},{13,... | collective-permute-start | bytes 307208 | tf_op jit(solution)/shard_map/ppermute | solution.py:460
  5.6 3.6 %collective-permute-start = (f32[32,128]{1,0:T(8,128)S(1)}, f32[32,128]{1,0:T(8,128)S(1)}, u32[]{:S(2)}, u32[]{:S(2)}) collective-permute-start(f32[32,128]{1,0:T(8,128)S(1)} %get-tuple-element.51), channel_id=1, source_target_pairs={{3,0},{2,1},{1,2},{0,3},{7,4},{6,5},{5,6},{4,7},{11,8},{10,9},{9,1... | collective-permute-start | bytes 49160 | tf_op jit(solution)/shard_map/ppermute | solution.py:460
  9.2 0.0 collective-permute-start.1
  9.2 0.0 copy-done.1
  9.2 0.0 copy-done
  9.2 0.0 copy-done.2
  9.2 3.8 %shard_map.74 = (f32[32,128]{1,0:T(8,128)S(1)}, f32[3,50,128]{2,1,0:T(8,128)S(1)}, f32[8,128]{1,0:T(8,128)S(1)}, f32[12,8,128]{2,1,0:T(8,128)S(1)}, f32[50,32,12...) custom-call(f32[50,32,128]{2,1,0:T(8,128)S(1)} %copy-done, ...), custom_call_target="tpu_custom_call" | custom-call | tf_op jit(solution)/shard_map/pallas_call | solution.py:499
  13.0 0.0 collective-permute-done.far_ref
  13.0 0.0 collective-permute-done.1.near_ref
  13.0 0.0 collective-permute-done.2.from_rows
  13.0 1.9 %shard_map.75 = (f32[32,128]{1,0:T(8,128)S(1)}, f32[32,128]{1,0:T(8,128)S(1)}, f32[2,2,50,128]{3,2,1,0:T(8,128)S(1)}, f32[2,50,32,128]{3,2,1,0:T(8,128)S(1)}, f3...) custom-call(f32[50,32,128]{2,1,0:T(8,128)S(1)} %copy-done, ...), custom_call_target="tpu_custom_call" | custom-call | tf_op jit(solution)/shard_map/pallas_call | solution.py:514
  15.0 0.6 %collective-permute-start.5 = (f32[2,2,50,128]{3,2,1,0:T(8,128)S(1)}, f32[2,2,50,128]{3,2,1,0:T(8,128)S(1)}, u32[]{:S(2)}, u32[]{:S(2)}) collective-permute-start(f32[2,2,50,128]{3,2,1,0:T(8,128)S(1)} %get-tuple-element.67), channel_id=1, source_target_pairs={{4,0},{0,4},{5,1},{1,5},{6,2},{2,6},{7,3},{3,7},{12,8},{8,12},{13,... | collective-permute-start | bytes 307208 | tf_op jit(solution)/shard_map/ppermute | solution.py:460
  15.5 1.7 %collective-permute-start.3 = (f32[32,128]{1,0:T(8,128)S(1)}, f32[32,128]{1,0:T(8,128)S(1)}, u32[]{:S(2)}, u32[]{:S(2)}) collective-permute-start(f32[32,128]{1,0:T(8,128)S(1)} %get-tuple-element.65), channel_id=1, source_target_pairs={{3,0},{2,1},{1,2},{0,3},{7,4},{6,5},{5,6},{4,7},{11,8},{10,9},{9,1... | collective-permute-start | bytes 49160 | tf_op jit(solution)/shard_map/ppermute | solution.py:460
  17.2 0.3 collective-permute-start.4
  17.5 2.4 %shard_map.76.sums_ref = f32[2,3,32,128]{3,2,1,0:T(8,128)S(1)} custom-call(f32[2,50,32,128]{3,2,1,0:T(8,128)S(1)} %get-tuple-element.54.p1_ref, f32[2,50,32,128]{3,2,1,0:T(8,128)S(1)} %get-tuple-element.55.zu_ref, f32[2,50,32,128]{3,2,1,0:T(8,128)S(1)} %get-tuple-element.56.zv_ref, f32[2,50,32,128]{3,2,1,0:T(8,128)S(1)} %get-tuple-element.57.w1_ref, ...), custom_call_target="tpu_custom_call" | custom-call | tf_op jit(solution)/shard_map/pallas_call | solution.py:518
  20.0 1.1 %collective-permute-done.3.far_ref = f32[32,128]{1,0:T(8,128)S(1)} collective-permute-done((f32[32,128]{1,0:T(8,128)S(1)}, f32[32,128]{1,0:T(8,128)S(1)}, u32[]{:S(2)}, u32[]{:S(2)}) %collective-permute-start.3) | collective-permute-done | bytes 16416 | tf_op jit(solution)/shard_map/ppermute | solution.py:460
  21.1 0.0 collective-permute-done.4.near_ref
  21.1 0.0 collective-permute-done.5.from_rows
  21.1 0.2 shard_map.77
  21.3 0.1 collective-permute-start.6
  21.4 1.6 %collective-permute-start.7 = (f32[2,3,8,128]{3,2,1,0:T(8,128)S(1)}, f32[2,3,8,128]{3,2,1,0:T(8,128)S(1)}, u32[]{:S(2)}, u32[]{:S(2)}) collective-permute-start(f32[2,3,8,128]{3,2,1,0:T(8,128)S(1)} %get-tuple-element.73), channel_id=1, source_target_pairs={{16,0},{24,8},{0,16},{8,24},{17,1},{25,9},{1,17},{9,25},{18,2},{26... | collective-permute-start | bytes 73736 | tf_op jit(solution)/shard_map/ppermute | solution.py:460
  23.0 0.3 collective-permute-start.8
  23.3 0.0 collective-permute-done.6.refs_1_
  23.3 2.0 %collective-permute-done.7.refs_2_ = f32[2,3,8,128]{3,2,1,0:T(8,128)S(1)} collective-permute-done((f32[2,3,8,128]{3,2,1,0:T(8,128)S(1)}, f32[2,3,8,128]{3,2,1,0:T(8,128)S(1)}, u32[]{:S(2)}, u32[]{:S(2)}) %collective-permute-start.7) | collective-permute-done | bytes 24608 | tf_op jit(solution)/shard_map/ppermute | solution.py:460
  25.3 0.9 %collective-permute-done.8.refs_3_ = f32[2,3,8,128]{3,2,1,0:T(8,128)S(1)} collective-permute-done((f32[2,3,8,128]{3,2,1,0:T(8,128)S(1)}, f32[2,3,8,128]{3,2,1,0:T(8,128)S(1)}, u32[]{:S(2)}, u32[]{:S(2)}) %collective-permute-start.8) | collective-permute-done | bytes 24608 | tf_op jit(solution)/shard_map/ppermute | solution.py:460
  26.3 1.6 %collective-permute-start.9 = (f32[6,8,128]{2,1,0:T(8,128)S(1)}, f32[6,8,128]{2,1,0:T(8,128)S(1)}, u32[]{:S(2)}, u32[]{:S(2)}) collective-permute-start(f32[6,8,128]{2,1,0:T(8,128)S(1)} %shard_map.78.refs_0_), channel_id=1, source_target_pairs={{4,0},{0,4},{5,1},{1,5},{6,2},{2,6},{7,3},{3,7},{12,8},{8,12},{13,... | collective-permute-start | bytes 73736 | tf_op jit(solution)/shard_map/ppermute | solution.py:460
  27.8 2.3 %collective-permute-done.9.refs_1_ = f32[6,8,128]{2,1,0:T(8,128)S(1)} collective-permute-done((f32[6,8,128]{2,1,0:T(8,128)S(1)}, f32[6,8,128]{2,1,0:T(8,128)S(1)}, u32[]{:S(2)}, u32[]{:S(2)}) %collective-permute-start.9) | collective-permute-done | bytes 24608 | tf_op jit(solution)/shard_map/ppermute | solution.py:460
  30.2 0.8 %collective-permute-start.10 = (f32[6,8,128]{2,1,0:T(8,128)S(1)}, f32[6,8,128]{2,1,0:T(8,128)S(1)}, u32[]{:S(2)}, u32[]{:S(2)}) collective-permute-start(f32[6,8,128]{2,1,0:T(8,128)S(1)} %get-tuple-element.76), channel_id=1, source_target_pairs={{1,0},{0,1},{3,2},{2,3},{5,4},{4,5},{7,6},{6,7},{9,8},{8,9},{11,10... | collective-permute-start | bytes 73736 | tf_op jit(solution)/shard_map/ppermute | solution.py:460
  30.9 1.8 %collective-permute-start.11 = (f32[6,8,128]{2,1,0:T(8,128)S(1)}, f32[6,8,128]{2,1,0:T(8,128)S(1)}, u32[]{:S(2)}, u32[]{:S(2)}) collective-permute-start(f32[6,8,128]{2,1,0:T(8,128)S(1)} %get-tuple-element.77), channel_id=1, source_target_pairs={{2,0},{3,1},{0,2},{1,3},{6,4},{7,5},{4,6},{5,7},{10,8},{11,9},{8,1... | collective-permute-start | bytes 73736 | tf_op jit(solution)/shard_map/ppermute | solution.py:460
  32.8 1.9 %collective-permute-start.12 = (f32[6,8,128]{2,1,0:T(8,128)S(1)}, f32[6,8,128]{2,1,0:T(8,128)S(1)}, u32[]{:S(2)}, u32[]{:S(2)}) collective-permute-start(f32[6,8,128]{2,1,0:T(8,128)S(1)} %get-tuple-element.78), channel_id=1, source_target_pairs={{3,0},{2,1},{1,2},{0,3},{7,4},{6,5},{5,6},{4,7},{11,8},{10,9},{9,1... | collective-permute-start | bytes 73736 | tf_op jit(solution)/shard_map/ppermute | solution.py:460
  34.6 0.0 collective-permute-done.10.refs_1_
  34.6 1.0 %collective-permute-done.11.refs_2_ = f32[6,8,128]{2,1,0:T(8,128)S(1)} collective-permute-done((f32[6,8,128]{2,1,0:T(8,128)S(1)}, f32[6,8,128]{2,1,0:T(8,128)S(1)}, u32[]{:S(2)}, u32[]{:S(2)}) %collective-permute-start.11) | collective-permute-done | bytes 24608 | tf_op jit(solution)/shard_map/ppermute | solution.py:460
  35.7 2.7 %collective-permute-done.12.refs_3_ = f32[6,8,128]{2,1,0:T(8,128)S(1)} collective-permute-done((f32[6,8,128]{2,1,0:T(8,128)S(1)}, f32[6,8,128]{2,1,0:T(8,128)S(1)}, u32[]{:S(2)}, u32[]{:S(2)}) %collective-permute-start.12) | collective-permute-done | bytes 24608 | tf_op jit(solution)/shard_map/ppermute | solution.py:460
  38.4 0.6 %shard_map.80 = f32[1,1,6,8,128]{4,3,2,1,0:T(8,128)} custom-call(f32[12,8,128]{2,1,0:T(8,128)S(1)} %get-tuple-element.44.masks_ref, f32[6,8,128]{2,1,0:T(8,128)S(1)} %get-tuple-element.75.refs_0_, f32[6,8,128]{2,1,0:T(8,128)S(1)} %collective-permute-done.10.refs_1_, f32[6,8,128]{2,1,0:T(8,128)S(1)} %collective-permute-done.11.refs_2_, ...), custom_call_target="tpu_custom_call" | custom-call | tf_op jit(solution)/shard_map/pallas_call | solution.py:542
  (2 shorter events, 0.0 us)
Async XLA Ops:
  0.0 9.2 %copy-start.1 = (f32[50]{0:T(128)S(1)}, f32[50]{0:T(128)}, u32[]{:S(2)}) copy-start(f32[50]{0:T(128)} %th_ref.3) | copy-start | bytes 604
  0.0 9.2 %copy-start = (f32[50,32,128]{2,1,0:T(8,128)S(1)}, f32[50,32,128]{2,1,0:T(8,128)}, u32[]{:S(2)}) copy-start(f32[50,32,128]{2,1,0:T(8,128)} %c_ref.3) | copy-start | bytes 2457604
  0.0 9.2 %copy-start.2 = (s32[8]{0:T(128)S(1)}, s32[8]{0:T(128)}, u32[]{:S(2)}) copy-start(s32[8]{0:T(128)} %owner_ref.1) | copy-start | bytes 100
  2.5 10.5 %collective-permute-start.2 = (f32[2,2,50,128]{3,2,1,0:T(8,128)S(1)}, f32[2,2,50,128]{3,2,1,0:T(8,128)S(1)}, u32[]{:S(2)}, u32[]{:S(2)}) collective-permute-start(f32[2,2,50,128]{3,2,1,0:T(8,128)S(1)} %get-tuple-element.53), channel_id=1, source_target_pairs={{4,0},{0,4},{5,1},{1,5},{6,2},{2,6},{7,3},{3,7},{12,8},{8,12},{13,... | collective-permute-start | bytes 307208 | tf_op jit(solution)/shard_map/ppermute | solution.py:460
  5.6 7.4 %collective-permute-start = (f32[32,128]{1,0:T(8,128)S(1)}, f32[32,128]{1,0:T(8,128)S(1)}, u32[]{:S(2)}, u32[]{:S(2)}) collective-permute-start(f32[32,128]{1,0:T(8,128)S(1)} %get-tuple-element.51), channel_id=1, source_target_pairs={{3,0},{2,1},{1,2},{0,3},{7,4},{6,5},{5,6},{4,7},{11,8},{10,9},{9,1... | collective-permute-start | bytes 49160 | tf_op jit(solution)/shard_map/ppermute | solution.py:460
  9.2 3.8 %collective-permute-start.1 = (f32[32,128]{1,0:T(8,128)S(1)}, f32[32,128]{1,0:T(8,128)S(1)}, u32[]{:S(2)}, u32[]{:S(2)}) collective-permute-start(f32[32,128]{1,0:T(8,128)S(1)} %get-tuple-element.52), channel_id=1, source_target_pairs={{1,0},{0,1},{3,2},{2,3},{5,4},{4,5},{7,6},{6,7},{9,8},{8,9},{11,10... | collective-permute-start | bytes 49160 | tf_op jit(solution)/shard_map/ppermute | solution.py:460
  15.0 6.2 %collective-permute-start.5 = (f32[2,2,50,128]{3,2,1,0:T(8,128)S(1)}, f32[2,2,50,128]{3,2,1,0:T(8,128)S(1)}, u32[]{:S(2)}, u32[]{:S(2)}) collective-permute-start(f32[2,2,50,128]{3,2,1,0:T(8,128)S(1)} %get-tuple-element.67), channel_id=1, source_target_pairs={{4,0},{0,4},{5,1},{1,5},{6,2},{2,6},{7,3},{3,7},{12,8},{8,12},{13,... | collective-permute-start | bytes 307208 | tf_op jit(solution)/shard_map/ppermute | solution.py:460
  15.5 5.6 %collective-permute-start.3 = (f32[32,128]{1,0:T(8,128)S(1)}, f32[32,128]{1,0:T(8,128)S(1)}, u32[]{:S(2)}, u32[]{:S(2)}) collective-permute-start(f32[32,128]{1,0:T(8,128)S(1)} %get-tuple-element.65), channel_id=1, source_target_pairs={{3,0},{2,1},{1,2},{0,3},{7,4},{6,5},{5,6},{4,7},{11,8},{10,9},{9,1... | collective-permute-start | bytes 49160 | tf_op jit(solution)/shard_map/ppermute | solution.py:460
  17.2 3.9 %collective-permute-start.4 = (f32[32,128]{1,0:T(8,128)S(1)}, f32[32,128]{1,0:T(8,128)S(1)}, u32[]{:S(2)}, u32[]{:S(2)}) collective-permute-start(f32[32,128]{1,0:T(8,128)S(1)} %get-tuple-element.66), channel_id=1, source_target_pairs={{1,0},{0,1},{3,2},{2,3},{5,4},{4,5},{7,6},{6,7},{9,8},{8,9},{11,10... | collective-permute-start | bytes 49160 | tf_op jit(solution)/shard_map/ppermute | solution.py:460
  21.3 1.9 %collective-permute-start.6 = (f32[2,3,8,128]{3,2,1,0:T(8,128)S(1)}, f32[2,3,8,128]{3,2,1,0:T(8,128)S(1)}, u32[]{:S(2)}, u32[]{:S(2)}) collective-permute-start(f32[2,3,8,128]{3,2,1,0:T(8,128)S(1)} %get-tuple-element.72), channel_id=1, source_target_pairs={{8,0},{0,8},{24,16},{16,24},{9,1},{1,9},{25,17},{17,25},{10,2},{2,... | collective-permute-start | bytes 73736 | tf_op jit(solution)/shard_map/ppermute | solution.py:460
  21.4 3.9 %collective-permute-start.7 = (f32[2,3,8,128]{3,2,1,0:T(8,128)S(1)}, f32[2,3,8,128]{3,2,1,0:T(8,128)S(1)}, u32[]{:S(2)}, u32[]{:S(2)}) collective-permute-start(f32[2,3,8,128]{3,2,1,0:T(8,128)S(1)} %get-tuple-element.73), channel_id=1, source_target_pairs={{16,0},{24,8},{0,16},{8,24},{17,1},{25,9},{1,17},{9,25},{18,2},{26... | collective-permute-start | bytes 73736 | tf_op jit(solution)/shard_map/ppermute | solution.py:460
  23.0 3.3 %collective-permute-start.8 = (f32[2,3,8,128]{3,2,1,0:T(8,128)S(1)}, f32[2,3,8,128]{3,2,1,0:T(8,128)S(1)}, u32[]{:S(2)}, u32[]{:S(2)}) collective-permute-start(f32[2,3,8,128]{3,2,1,0:T(8,128)S(1)} %get-tuple-element.74), channel_id=1, source_target_pairs={{24,0},{16,8},{8,16},{0,24},{25,1},{17,9},{9,17},{1,25},{26,2},{18... | collective-permute-start | bytes 73736 | tf_op jit(solution)/shard_map/ppermute | solution.py:460
  26.3 3.9 %collective-permute-start.9 = (f32[6,8,128]{2,1,0:T(8,128)S(1)}, f32[6,8,128]{2,1,0:T(8,128)S(1)}, u32[]{:S(2)}, u32[]{:S(2)}) collective-permute-start(f32[6,8,128]{2,1,0:T(8,128)S(1)} %shard_map.78.refs_0_), channel_id=1, source_target_pairs={{4,0},{0,4},{5,1},{1,5},{6,2},{2,6},{7,3},{3,7},{12,8},{8,12},{13,... | collective-permute-start | bytes 73736 | tf_op jit(solution)/shard_map/ppermute | solution.py:460
  30.2 4.5 %collective-permute-start.10 = (f32[6,8,128]{2,1,0:T(8,128)S(1)}, f32[6,8,128]{2,1,0:T(8,128)S(1)}, u32[]{:S(2)}, u32[]{:S(2)}) collective-permute-start(f32[6,8,128]{2,1,0:T(8,128)S(1)} %get-tuple-element.76), channel_id=1, source_target_pairs={{1,0},{0,1},{3,2},{2,3},{5,4},{4,5},{7,6},{6,7},{9,8},{8,9},{11,10... | collective-permute-start | bytes 73736 | tf_op jit(solution)/shard_map/ppermute | solution.py:460
  30.9 4.7 %collective-permute-start.11 = (f32[6,8,128]{2,1,0:T(8,128)S(1)}, f32[6,8,128]{2,1,0:T(8,128)S(1)}, u32[]{:S(2)}, u32[]{:S(2)}) collective-permute-start(f32[6,8,128]{2,1,0:T(8,128)S(1)} %get-tuple-element.77), channel_id=1, source_target_pairs={{2,0},{3,1},{0,2},{1,3},{6,4},{7,5},{4,6},{5,7},{10,8},{11,9},{8,1... | collective-permute-start | bytes 73736 | tf_op jit(solution)/shard_map/ppermute | solution.py:460
  32.8 5.6 %collective-permute-start.12 = (f32[6,8,128]{2,1,0:T(8,128)S(1)}, f32[6,8,128]{2,1,0:T(8,128)S(1)}, u32[]{:S(2)}, u32[]{:S(2)}) collective-permute-start(f32[6,8,128]{2,1,0:T(8,128)S(1)} %get-tuple-element.78), channel_id=1, source_target_pairs={{3,0},{2,1},{1,2},{0,3},{7,4},{6,5},{5,6},{4,7},{11,8},{10,9},{9,1... | collective-permute-start | bytes 73736 | tf_op jit(solution)/shard_map/ppermute | solution.py:460
